TPU v7x, 32 devices: a whole 2x2x4 slice. The times are simulated.
32 devices in a mesh: row: 4 (over y, x), col: 8 (over z, core).
Axes of the slice: x: 2, y: 2, z: 4, core: 2. Of those that a mesh axis runs over, the one named last changes fastest.
Arguments:
- values: bfloat16 [4096, 4096], P('row', 'col'), may hold values from 0.0001296997 to 0.12988281
- tile_mask: int32 [32, 32], P('row', 'col'), may hold values 0 or 1
- keep_mask: int32 [32, 32], P('row', 'col'), may hold values 0 or 1
- thr_index: int32 [4096], P('col'), may hold values from 0 to 9
Outputs:
- expanded: bfloat16 [4096, 4096], P('row', 'col')
All inputs are finite; a program needn't handle non-finite values. No bound on the sum of `tile_mask` or of `keep_mask` on one device may be relied on, other than what follows from the above.
Results may differ from a plain program's by a relative error of at most 0.0004.
Values may be sent and summed in bfloat16 or wider, within the bound.
No kernel may reach another device: no remote copies, remote signals or barrier semaphores. Data moves between devices by JAX's collectives and lax.ppermute only.
A program may use at most 64 MiB of HBM per device.

v0:
```python
import jax
import jax.numpy as jnp
from jax import lax
from jax.sharding import PartitionSpec as P

TB = 128


def on_device(values, tile_mask, keep_mask, thr_index):
    row_count, col_count = values.shape
    row_tiles = row_count // TB
    col_tiles = col_count // TB
    matrix = (
        values.reshape(row_tiles, TB, col_tiles, TB)
        * tile_mask[:, None, :, None].astype(jnp.bfloat16)
    ).reshape(row_count, col_count)
    kept_cells = jnp.broadcast_to(
        keep_mask[:, None, :, None].astype(jnp.float32), (row_tiles, TB, col_tiles, TB)
    ).reshape(row_count, col_count)
    order_all = row_count * lax.axis_size("row")
    thresholds = 0.125 * thr_index.astype(jnp.float32)
    col_panel = lax.all_gather(matrix, "row", axis=0, tiled=True)
    product = jnp.dot(
        lax.all_gather(matrix, "col", axis=1, tiled=True),
        col_panel,
        preferred_element_type=jnp.float32,
    )
    outputs = []
    for phase_idx in range(col_tiles):
        lo_col = phase_idx * TB
        part_prod = product[:, lo_col : lo_col + TB]
        col_means = lax.psum(jnp.sum(part_prod, axis=0), "row") / order_all
        pruned = (
            jnp.maximum(part_prod - thresholds[lo_col : lo_col + TB] * col_means, 0.0)
            * kept_cells[:, lo_col : lo_col + TB]
        )
        col_totals = lax.psum(jnp.sum(pruned, axis=0), "row") / order_all
        outputs.append(pruned / jnp.maximum(col_totals, 0.1))
    result = jnp.concatenate(outputs, axis=1)
    return result.astype(jnp.bfloat16)


def solution(mesh):
    return jax.shard_map(
        on_device,
        mesh=mesh,
        in_specs=(P("row", "col"), P("row", "col"), P("row", "col"), P("col")),
        out_specs=P("row", "col"),
        check_vma=False,
    )
```

profile of v0, /device:TPU:0, one launch (start us, length us, event | category | flops | bytes accessed | tf_op | source)
XLA Modules:
  0.0 188.3 jit_solution(8773886451617511830)
XLA Ops:
  6.5 0.0 all-gather.5.cloned.1.call-start
  6.5 0.7 convert_element_type.12
  7.2 0.1 copy.5
  7.3 0.3 mul.41
  7.7 0.0 copy-start.1
  7.7 2.3 %bitcast_multiply_fusion = bf16[1024,512]{1,0:T(8,128)(2,1)} fusion(bf16[1024,512]{1,0:T(8,128)(2,1)} %param.4, bf16[128,8,4,128]{3,2,1,0:T(4,128)(2,1)S(1)} %bitcast.14), kind=kLoop, calls=%fused_computation.1 | loop fusion | flops 524288 | bytes 3145728 | tf_op jit(solution)/shard_map/mul | solution.py:14
  10.0 0.0 all-gather.5.cloned.1.call-update
  10.0 0.0 all-gather.3.cloned.1.call-start
  10.1 0.7 all-gather.3.cloned.1.call-update
  10.8 0.1 copy.6
  10.9 0.3 broadcast_in_dim.2
  11.2 0.0 copy-start.2
  11.3 0.2 copy.11
  11.4 0.5 copy-done.2
  11.9 53.6 %all-gather.5.cloned.1.call-done = bf16[4096,512]{1,0:T(8,128)(2,1)} async-done(((bf16[1024,512]{1,0:T(8,128)(2,1)}), bf16[4096,512]{1,0:T(8,128)(2,1)}) %all-gather.5.cloned.1.call-update) | async-done | bytes 4194320 | tf_op jit(solution)/shard_map/all_gather | solution.py:22
  65.5 83.7 %all-gather.3.cloned.1.call-done = bf16[1024,4096]{1,0:T(8,128)(2,1)} async-done(((bf16[1024,512]{1,0:T(8,128)(2,1)}), bf16[1024,4096]{1,0:T(8,128)(2,1)}) %all-gather.3.cloned.1.call-update) | async-done | bytes 8388624 | tf_op jit(solution)/shard_map/all_gather | solution.py:24
  149.2 8.1 %fusion.4 = f32[1024,512]{1,0:T(8,128)S(1)} fusion(bf16[1024,4096]{1,0:T(8,128)(2,1)} %all-gather.3.cloned.1.call-done, bf16[4096,512]{1,0:T(8,128)(2,1)} %all-gather.5.cloned.1.call-done), kind=kOutput, calls=%fused_computation.28 | convolution fusion | flops 4294967296 | bytes 14680064 | tf_op jit(solution)/shard_map/dot_general | solution.py:23
  157.3 1.3 copy-done
  158.7 0.2 slice_reduce_fusion.3
  158.8 9.8 %all-reduce.1 = (f32[128]{0:T(128)S(1)}, f32[128]{0:T(128)S(1)}, f32[128]{0:T(128)S(1)}, f32[128]{0:T(128)S(1)}) all-reduce(f32[128]{0:T(128)S(1)} %get-tuple-element.9, f32[128]{0:T(128)S(1)} %get-tuple-element.10, f32[128]{0:T(128)S(1)} %get-tuple-element.11, f32[128]{0:T(128)S(1)} %get-tuple-element.12), channel_id=1, replica_groups=mesh['row'=4,'col'=8] {'row'}, use_global_device_ids=true, to_apply=%region_1.0 | all-reduce | flops 512 | bytes 4096 | tf_op jit(solution)/shard_map/psum | solution.py:32
  168.7 1.8 fusion
  170.5 8.0 %all-reduce = (f32[128]{0:T(128)S(1)}, f32[128]{0:T(128)S(1)}, f32[128]{0:T(128)S(1)}, f32[128]{0:T(128)S(1)}) all-reduce(f32[128]{0:T(128)S(1)} %get-tuple-element.6, f32[128]{0:T(128)S(1)} %get-tuple-element.7, f32[128]{0:T(128)S(1)} %get-tuple-element.8, f32[128]{0:T(128)S(1)} %get-tuple-element.5), channel_id=1, replica_groups=mesh['row'=4,'col'=8] {'row'}, use_global_device_ids=true, to_apply=%region_15.0 | all-reduce | flops 512 | bytes 4096 | tf_op jit(solution)/shard_map/psum | solution.py:37
  178.5 1.9 %divide_convert_fusion.3 = (bf16[1024,128]{1,0:T(8,128)(2,1)S(1)}, bf16[1024,128]{1,0:T(8,128)(2,1)S(1)}, bf16[1024,128]{1,0:T(8,128)(2,1)S(1)}, bf16[1024,128]{1,0:T(8,128)(2,1)S(1)}) fusion(f32[128]{0:T(128)S(1)} %get-tuple-element.32, f32[1024,512]{1,0:T(8,128)S(1)} %bitcast.12, f32[128]{0:T(128)S(1)} %get-tuple-element.28, f32[1024,512]{1,0:T(8,128)} %copy-done, ...), kind=kLoop, calls=%fused_computation.10 | loop fusion | flops 2621440 | bytes 5246976 | tf_op jit(solution)/shard_map/convert
  180.4 1.1 pad_maximum_fusion
  (7 shorter events, 0.0 us)
Async XLA Ops:
  6.5 59.0 %all-gather.5.cloned.1.call-start = ((), (), s32[]{:S(2)}) async-start(), calls=%async_computation.1 | async-start | bytes 5242880 | tf_op jit(solution)/shard_map/all_gather | solution.py:22
  7.7 3.1 %copy-start.1 = (s32[8,4]{0,1:T(4,128)S(1)}, s32[8,4]{0,1:T(4,128)}, u32[]{:S(2)}) copy-start(s32[8,4]{0,1:T(4,128)} %param.6) | copy-start | bytes 388
  10.0 139.1 %all-gather.3.cloned.1.call-start = ((), (), s32[]{:S(2)}) async-start(), calls=%async_computation | async-start | bytes 9437184 | tf_op jit(solution)/shard_map/all_gather | solution.py:24
  11.2 0.7 copy-start.2
  157.3 1.4 copy-start
Sparse Core Ops, SparseCore 0:
  10.2 55.2 all-gather.4
  67.1 82.0 all-gather.2
where the time goes:
time: 189 us; the launch traced here: 188 us
  waiting for transfers between devices  138 us (73%)
  blocking collectives  17.8 us (9%)
  between operations  13.5 us (7%)
  matrix products  8.14 us (4%)
  other arithmetic  8.02 us (4%)
  local copies, waits for them, and re-layouts  2.87 us (2%)
    all_gather x1, waiting for transfers between devices, on_device(): lax.all_gather(matrix, 'col', axis=1, tiled=True)  83.7 us
    all_gather x1, waiting for transfers between devices, on_device(): col_panel = lax.all_gather(matrix, 'row', axis=0, tiled=True)  53.6 us
    psum x1, blocking collectives, on_device(): col_means = lax.psum(jnp.sum(part_prod, axis=0), 'row') / order_all  9.85 us
    dot_general x1, matrix products, on_device(): jnp.dot(lax.all_gather(matrix, 'col', axis=1, tiled=True), col_panel, pre...  8.14 us
    psum x1, blocking collectives, on_device(): col_totals = lax.psum(jnp.sum(pruned, axis=0), 'row') / order_all  7.98 us
  transfers between devices with their start and end apart: 2, of which 2 were waited for; matrix products, arithmetic and copies ran while one was open for 0% of the time, Pallas kernels for 0%

commit v1 on v0

v1 whole, which is shorter than its diff:
```python
import functools

import jax
import jax.numpy as jnp
from jax import lax
from jax.experimental import pallas as pl
from jax.experimental.pallas import tpu as pltpu
from jax.sharding import PartitionSpec as P

TB = 128
PAD = 16
AXES = ("row", "col")
F32, BF16, I32 = jnp.float32, jnp.bfloat16, jnp.int32
ANY = pl.BlockSpec(memory_space=pl.ANY)
VMEM = pl.BlockSpec(memory_space=pltpu.VMEM)
SMEM = pl.BlockSpec(memory_space=pltpu.SMEM)


def params(limit=56):
    return pltpu.CompilerParams(vmem_limit_bytes=limit * 1024 * 1024)


def cost(flops, moved):
    return pl.CostEstimate(flops=int(flops), bytes_accessed=int(moved), transcendentals=0)


def tiles_of(shape):
    return shape[0] // TB, shape[1] // TB


def pack_kernel(slots, mask_ref, block_ref, out_ref):
    ti, tj = tiles_of(block_ref.shape)
    lane = lax.broadcasted_iota(I32, (PAD, TB), 1)
    table = jnp.full((PAD, TB), -1, I32)
    used = jnp.int32(0)
    for i in range(ti):
        for j in range(tj):
            stored = mask_ref[j, i]
            fits = jnp.logical_and(stored > 0, used < slots)

            @pl.when(fits)
            def _(i=i, j=j, used=used):
                at = pl.multiple_of(used * TB, TB)
                out_ref[pl.ds(at, TB), :] = block_ref[i * TB : (i + 1) * TB, j * TB : (j + 1) * TB]

            table = jnp.where(lane == i * tj + j, jnp.where(fits, used, -1), table)
            used = used + stored
    table = jnp.where(lane == ti * tj, used, table)
    out_ref[slots * TB :, :] = table.astype(F32).astype(BF16)


def pack(block, mask_t, slots):
    return pl.pallas_call(
        functools.partial(pack_kernel, slots),
        out_shape=jax.ShapeDtypeStruct((slots * TB + PAD, TB), BF16),
        in_specs=[SMEM, VMEM],
        out_specs=VMEM,
        compiler_params=params(),
        cost_estimate=cost(1e6, 2 * block.size * 2),
        name="pack",
    )(mask_t, block)


def read_table(slots, buf, at, itab, stab, sem):
    itab[...] = buf[slots * TB : slots * TB + 8, :].astype(F32).astype(I32)
    copy = pltpu.make_async_copy(itab, stab.at[at], sem)
    copy.start()
    copy.wait()


def tile_from(buf, slot):
    at = pl.multiple_of(jnp.maximum(slot, 0) * TB, TB)
    return jnp.where(slot >= 0, buf[pl.ds(at, TB), :], jnp.zeros((TB, TB), BF16))


def panel_kernel(slots, n, rows, me_ref, *refs):
    bufs, (panel_ref, sums_ref), (itab, stab, sem) = refs[:n], refs[n : n + 2], refs[n + 2 :]
    cols = panel_ref.shape[1]
    ti, tj = rows // TB, cols // TB
    worst = jnp.int32(0)
    sums_ref[...] = jnp.zeros_like(sums_ref)
    for q in range(n):
        read_table(slots, bufs[q], q, itab, stab, sem)
        worst = jnp.maximum(worst, stab[q, 0, ti * tj])
        base = (me_ref[0] ^ q) * rows

        @pl.loop(0, ti)
        def _(i, q=q, base=base):
            for j in range(tj):
                tile = tile_from(bufs[q], stab[q, 0, i * tj + j])
                panel_ref[pl.ds(pl.multiple_of(base + i * TB, TB), TB), j * TB : (j + 1) * TB] = tile
                part = jnp.sum(tile.astype(F32), axis=0, keepdims=True)
                sums_ref[j : j + 1, :] += part

    flag = jnp.where(worst > slots, 1.0, 0.0)
    sums_ref[tj : tj + 1, :] = jnp.full((1, TB), 1.0, F32) * flag


def panel(me, payloads, slots, rows, cols):
    n = len(payloads)
    s_rows = -(-(cols // TB + 1) // 8) * 8
    return pl.pallas_call(
        functools.partial(panel_kernel, slots, n, rows),
        out_shape=(
            jax.ShapeDtypeStruct((n * rows, cols), BF16),
            jax.ShapeDtypeStruct((s_rows, TB), F32),
        ),
        in_specs=[SMEM] + [VMEM] * n,
        out_specs=(VMEM, VMEM),
        scratch_shapes=[
            pltpu.VMEM((8, TB), I32),
            pltpu.SMEM((n, 8, TB), I32),
            pltpu.SemaphoreType.DMA,
        ],
        compiler_params=params(),
        cost_estimate=cost(1e7, 2 * n * rows * cols * 2),
        name="panel",
    )(me, *payloads)


def unpack_row(slots, buf, at, rows, cols, itab, stab, sem, lhs, lane0):
    ti, tj = rows // TB, cols // TB
    read_table(slots, buf, at, itab, stab, sem)

    @pl.loop(0, ti)
    def _(i):
        for j in range(tj):
            tile = tile_from(buf, stab[at, 0, i * tj + j])
            lhs[pl.ds(pl.multiple_of(i * TB, TB), TB), pl.ds(pl.multiple_of(lane0 + j * TB, TB), TB)] = tile


def row_step(rows):
    return min(rows, 256)


def dot_kernel(slots, pairs, rows, cols, me_ref, *refs):
    n = 2 * pairs
    bufs, panel_ref, acc_ref = refs[:n], refs[n], refs[n + 1]
    itab, stab, sem, lhs = refs[n + 2 :]
    core, z = me_ref[1], me_ref[2]
    step = row_step(rows)
    for q in range(pairs):
        unpack_row(slots, bufs[2 * q], 2 * q, rows, cols, itab, stab, sem, lhs, core * cols)
        unpack_row(slots, bufs[2 * q + 1], 2 * q + 1, rows, cols, itab, stab, sem, lhs, (1 - core) * cols)
        at = pl.multiple_of((z ^ q) * 2 * cols, TB)

        @pl.loop(0, rows // step)
        def _(m, q=q, at=at):
            here = pl.ds(pl.multiple_of(m * step, step), step)
            got = jnp.dot(lhs[here, :], panel_ref[pl.ds(at, 2 * cols), :], preferred_element_type=F32)
            acc_ref[here, :] = got if q == 0 else acc_ref[here, :] + got


def dots(me, payloads, dense, slots, rows, cols):
    pairs = len(payloads) // 2
    return pl.pallas_call(
        functools.partial(dot_kernel, slots, pairs, rows, cols),
        out_shape=jax.ShapeDtypeStruct((rows, cols), F32),
        in_specs=[SMEM] + [VMEM] * (2 * pairs + 1),
        out_specs=VMEM,
        scratch_shapes=[
            pltpu.VMEM((8, TB), I32),
            pltpu.SMEM((2 * pairs, 8, TB), I32),
            pltpu.SemaphoreType.DMA,
            pltpu.VMEM((rows, 2 * cols), BF16),
        ],
        compiler_params=params(),
        cost_estimate=cost(2 * rows * 2 * cols * pairs * cols, 12 * rows * cols * pairs),
        name="dots",
    )(me, *payloads, dense)


def means_kernel(n_pairs, s_rows, order, me_ref, *refs):
    msgs, thr_ref, panel_ref, out_ref = refs[:n_pairs], *refs[n_pairs:]
    core, z = me_ref[1], me_ref[2]
    cols = panel_ref.shape[1]
    tj = cols // TB
    total = jnp.zeros((8, cols), F32)
    row = lax.broadcasted_iota(I32, (8, TB), 0)
    for q in range(n_pairs):
        for b in range(2):
            for t in range(tj):
                s = jnp.broadcast_to(msgs[q][b * s_rows + t : b * s_rows + t + 1, :], (8, TB))
                high = s.astype(BF16).astype(F32)
                mid = (s - high).astype(BF16).astype(F32)
                low = s - high - mid
                lhs = jnp.where(row == 0, high, jnp.where(row == 1, mid, jnp.where(row == 2, low, 0.0)))
                at = (z ^ q) * 2 * cols + (core ^ b) * cols + t * TB
                total += jnp.dot(
                    lhs.astype(BF16),
                    panel_ref[pl.ds(pl.multiple_of(at, TB), TB), :],
                    preferred_element_type=F32,
                )
    mean = jnp.sum(total, axis=0, keepdims=True) / order
    out_ref[...] = jnp.broadcast_to(0.125 * thr_ref[...].astype(F32) * mean, out_ref.shape)


def cuts_of(me, messages, thr, dense, s_rows, order):
    n = len(messages)
    cols = dense.shape[1]
    return pl.pallas_call(
        functools.partial(means_kernel, n, s_rows, order),
        out_shape=jax.ShapeDtypeStruct((8, cols), F32),
        in_specs=[SMEM] + [VMEM] * (n + 2),
        out_specs=VMEM,
        compiler_params=params(),
        cost_estimate=cost(1e7, dense.size * 2),
        name="cuts",
    )(me, *messages, thr, dense)


def last_kernel(slots, n_parts, pair, rows, cols, me_ref, keep_ref, *refs):
    parts = refs[: 2 * n_parts]
    panel_ref, prior_ref, cut_ref, acc_ref, tot_ref = refs[2 * n_parts : 2 * n_parts + 5]
    mine, other, itab, stab, sem, lhs, rhs, sems = refs[2 * n_parts + 5 :]
    core, z, part = me_ref[1], me_ref[2], me_ref[3]
    step = row_step(rows)
    at = pl.multiple_of((z ^ pair) * 2 * cols, TB)
    get = pltpu.make_async_copy(panel_ref.at[pl.ds(at, 2 * cols), :], rhs, sems.at[2])
    get.start()
    for p in range(n_parts):

        @pl.when(part == p)
        def _(p=p):
            pltpu.make_async_copy(parts[2 * p], mine, sems.at[0]).start()
            pltpu.make_async_copy(parts[2 * p + 1], other, sems.at[1]).start()

    pltpu.make_async_copy(parts[0], mine, sems.at[0]).wait()
    unpack_row(slots, mine, 0, rows, cols, itab, stab, sem, lhs, core * cols)
    pltpu.make_async_copy(parts[1], other, sems.at[1]).wait()
    unpack_row(slots, other, 1, rows, cols, itab, stab, sem, lhs, (1 - core) * cols)
    get.wait()
    tot_ref[...] = jnp.zeros_like(tot_ref)
    cut = cut_ref[0:1, :]
    per = step // TB

    @pl.loop(0, rows // step)
    def _(m):
        here = pl.ds(pl.multiple_of(m * step, step), step)
        got = prior_ref[here, :] + jnp.dot(lhs[here, :], rhs[...], preferred_element_type=F32)
        got = jnp.maximum(got - cut, 0.0)
        for a in range(per):
            for j in range(cols // TB):
                kept = keep_ref[j, m * per + a].astype(F32)
                cell = got[a * TB : (a + 1) * TB, j * TB : (j + 1) * TB] * kept
                acc_ref[pl.ds(pl.multiple_of(m * step + a * TB, TB), TB), j * TB : (j + 1) * TB] = cell
                tot_ref[:, j * TB : (j + 1) * TB] += jnp.sum(cell.reshape(TB // 8, 8, TB), axis=0)


def finish(me, keep_t, parts, dense, prior, cut, slots, pair, rows, cols):
    n_parts = len(parts) // 2
    return pl.pallas_call(
        functools.partial(last_kernel, slots, n_parts, pair, rows, cols),
        out_shape=(jax.ShapeDtypeStruct((rows, cols), F32), jax.ShapeDtypeStruct((8, cols), F32)),
        in_specs=[SMEM, SMEM] + [ANY] * (2 * n_parts + 1) + [VMEM, VMEM],
        out_specs=(VMEM, VMEM),
        scratch_shapes=[
            pltpu.VMEM(parts[0].shape, BF16),
            pltpu.VMEM(parts[0].shape, BF16),
            pltpu.VMEM((8, TB), I32),
            pltpu.SMEM((2, 8, TB), I32),
            pltpu.SemaphoreType.DMA,
            pltpu.VMEM((rows, 2 * cols), BF16),
            pltpu.VMEM((2 * cols, cols), BF16),
            pltpu.SemaphoreType.DMA((3,)),
        ],
        compiler_params=params(),
        cost_estimate=cost(2 * rows * 2 * cols * cols, 12 * rows * cols),
        name="finish",
    )(me, keep_t, *parts, dense, prior, cut)


def scale_kernel(n, order, x_ref, *refs):
    tots, out_ref = refs[:n], refs[n]
    total = tots[0][...]
    for t in tots[1:]:
        total = total + t[...]
    total = jnp.sum(total, axis=0, keepdims=True) / order
    out_ref[...] = (x_ref[...] / jnp.maximum(total, 0.1)).astype(BF16)


def scale(x, totals, order):
    rows, cols = x.shape
    step = row_step(rows)
    n = len(totals)
    return pl.pallas_call(
        functools.partial(scale_kernel, n, order),
        out_shape=jax.ShapeDtypeStruct(x.shape, BF16),
        grid=(rows // step,),
        in_specs=[pl.BlockSpec((step, cols), lambda i: (i, 0))]
        + [pl.BlockSpec((8, cols), lambda i: (0, 0))] * n,
        out_specs=pl.BlockSpec((step, cols), lambda i: (i, 0)),
        compiler_params=params(),
        cost_estimate=cost(2 * x.size, 6 * x.size),
        name="scale",
    )(x, *totals)


def dense_path(values, tile_mask, keep_mask, thr_index, n_row, n_col):
    rows, cols = values.shape
    ti, tj = tiles_of(values.shape)
    matrix = (
        values.reshape(ti, TB, tj, TB) * tile_mask[:, None, :, None].astype(BF16)
    ).reshape(rows, cols)
    kept = jnp.broadcast_to(keep_mask[:, None, :, None].astype(F32), (ti, TB, tj, TB)).reshape(rows, cols)
    r, c = lax.axis_index("row"), lax.axis_index("col")
    order = rows * n_row

    def col_ring(i, carry):
        block, panel_ = carry
        panel_ = lax.dynamic_update_slice(panel_, block, (((r - i) % n_row) * rows, 0))
        return lax.ppermute(block, "row", [(k, (k + 1) % n_row) for k in range(n_row)]), panel_

    _, panel_ = lax.fori_loop(0, n_row, col_ring, (matrix, jnp.zeros((order, cols), BF16)))

    def row_ring(i, carry):
        block, acc = carry
        part = lax.dynamic_slice(panel_, (((c - i) % n_col) * cols, 0), (cols, cols))
        acc = acc + jnp.dot(block, part, preferred_element_type=F32)
        return lax.ppermute(block, "col", [(k, (k + 1) % n_col) for k in range(n_col)]), acc

    _, product = lax.fori_loop(0, n_col, row_ring, (matrix, jnp.zeros((rows, cols), F32)))
    means = lax.psum(jnp.sum(product, axis=0), "row") / order
    pruned = jnp.maximum(product - 0.125 * thr_index.astype(F32) * means, 0.0) * kept
    totals = lax.psum(jnp.sum(pruned, axis=0), "row") / order
    return (pruned / jnp.maximum(totals, 0.1)).astype(BF16)


def line_plan(n_z):
    plan = {}
    for dist in range(1, n_z):
        for j in range(1, n_z):
            groups = {}
            for z in range(n_z):
                b = z ^ j
                if abs(z - b) != dist:
                    continue
                if dist <= 2:
                    groups.setdefault(("own", None), []).append((b, z))
                else:
                    near = z + (1 if b > z else -1)
                    jn = near ^ b
                    part = next(p for p, g in enumerate(plan[jn]) if near in [t for _, t in g[1]])
                    groups.setdefault((jn, part), []).append((near, z))
            for key, pairs in groups.items():
                plan.setdefault(j, []).append((key, pairs))
    merged = {}
    for j, items in plan.items():
        merged[j] = items
    return merged


def on_device(values, tile_mask, keep_mask, thr_index, n_row, n_col):
    return body(values, tile_mask, keep_mask, thr_index, n_row, n_col)


def body(values, tile_mask, keep_mask, thr_index, n_row, n_col):
    rows, cols = values.shape
    ti, tj = tiles_of(values.shape)
    slots = ti * tj * 3 // 4
    n_z = n_col // 2
    order = rows * n_row
    r, c = lax.axis_index("row"), lax.axis_index("col")

    def at(rr, zz, cc):
        return rr * n_col + zz * 2 + cc

    def along_z(pairs):
        return [(at(rr, a, cc), at(rr, b, cc)) for rr in range(n_row) for a, b in pairs for cc in range(2)]

    def along_row(q):
        return [(at(rr, zz, cc), at(rr ^ q, zz, cc)) for rr in range(n_row) for zz in range(n_z) for cc in range(2)]

    def swap_cores(zs):
        return [(at(rr, zz, cc), at(rr, zz, 1 - cc)) for rr in range(n_row) for zz in zs for cc in range(2)]

    def send(x, pairs):
        return lax.ppermute(x, AXES, pairs)

    own = pack(values, tile_mask.T, slots)

    plan = line_plan(n_z)
    got = {}
    done = set()
    for dist in range(1, n_z):
        for j, items in plan.items():
            for p, (key, pairs) in enumerate(items):
                if abs(pairs[0][0] - (pairs[0][1] ^ j)) == 0 and key[0] == "own" and dist == 1:
                    got[(j, p)] = (send(own, along_z(pairs)), [b for _, b in pairs])
                    done.add((j, p))
    while len(done) < sum(len(v) for v in plan.values()):
        for j, items in plan.items():
            for p, (key, pairs) in enumerate(items):
                if (j, p) not in done and key in done:
                    got[(j, p)] = (send(got[key][0], along_z(pairs)), [b for _, b in pairs])
                    done.add((j, p))

    column = [own] + [send(own, along_row(q)) for q in range(1, n_row)]
    swapped = send(own, swap_cores(range(n_z)))
    pairs = [[own, swapped]]
    for j in range(1, n_z):
        entry = []
        for p in range(len(plan[j])):
            x, zs = got[(j, p)]
            entry += [x, send(x, swap_cores(zs))]
        pairs.append(entry)

    z = c // 2
    core = c % 2
    last = n_z - 1
    part_table = [0] * n_z
    for p, (_, prs) in enumerate(plan[last]):
        for _, b in prs:
            part_table[b] = p
    part = jnp.array(part_table, I32)[z]
    me = jnp.stack([r, core, z, part]).astype(I32)

    dense, sums = panel(me, column, slots, rows, cols)
    s_rows = sums.shape[0]
    early = []
    for j in range(last):
        e = pairs[j]
        if len(e) == 2:
            early += e
        else:
            where = [0] * n_z
            for p, (_, prs) in enumerate(plan[j]):
                for _, b in prs:
                    where[b] = p
            pick = jnp.array(where, I32)[z]
            for side in range(2):
                x = e[side]
                for p in range(1, len(e) // 2):
                    x = jnp.where(pick == p, e[2 * p + side], x)
                early.append(x)
    prior = dots(me, early, dense, slots, rows, cols)
    both = jnp.concatenate([sums, send(sums, swap_cores(range(n_z)))], axis=0)
    messages = [both] + [send(both, along_z([(a, a ^ j) for a in range(n_z)])) for j in range(1, n_z)]
    cut = cuts_of(me, messages, thr_index.reshape(1, cols), dense, s_rows, order)
    over = functools.reduce(jnp.maximum, [m[b * s_rows + tj, 0] for m in messages for b in range(2)]) > 0.0

    def fast():
        pruned, tot = finish(
            me, keep_mask.T, pairs[last], dense, prior, cut, slots, last, rows, cols
        )
        totals = [tot] + [send(tot, along_row(q)) for q in range(1, n_row)]
        return scale(pruned, totals, order)

    def full():
        return dense_path(values, tile_mask, keep_mask, thr_index, n_row, n_col)

    return lax.cond(over, full, fast)


def solution(mesh):
    n_row, n_col = mesh.shape["row"], mesh.shape["col"]
    return jax.shard_map(
        functools.partial(on_device, n_row=n_row, n_col=n_col),
        mesh=mesh,
        in_specs=(P("row", "col"), P("row", "col"), P("row", "col"), P("col")),
        out_specs=P("row", "col"),
        check_vma=False,
    )
```

time: 189 us -> 119 us (0.63)
  waiting for transfers between devices: 138 us -> 44.1 us
  Pallas kernels: 0 us -> 34.4 us
  starting transfers between devices: 0.04 us -> 25.8 us
  blocking collectives: 17.8 us -> 0 us
  between operations: 13.5 us -> 4.93 us
  matrix products: 8.14 us -> 0 us
  other arithmetic: 8.02 us -> 0.7 us
  local copies, waits for them, and re-layouts: 2.87 us -> 8.68 us
    all_gather x2 -> x0, waiting for transfers between devices: 137 us -> none  [the longest x1 83.7 us: on_device(): lax.all_gather(matrix, 'col', axis=1, tiled=True)]
    ppermute x0 -> x19, waiting for transfers between devices: none -> 44.1 us  [send(): return lax.ppermute(x, AXES, pairs)]
    pallas_call x0 -> x6, Pallas kernels: none -> 34.4 us  [the longest x1 13.4 us: dots(): pl.pallas_call(functools.partial(dot_kernel, slots, pairs, rows, cols), o...]
    ppermute x0 -> x19, starting transfers between devices: none -> 25.8 us  [send(): return lax.ppermute(x, AXES, pairs)]
    psum x2 -> x0, blocking collectives: 17.8 us -> none  [the longest x1 9.85 us: on_device(): col_means = lax.psum(jnp.sum(part_prod, axis=0), 'row') / order_all]
    dot_general x1 -> x0, matrix products: 8.14 us -> none  [on_device(): jnp.dot(lax.all_gather(matrix, 'col', axis=1, tiled=True), col_panel, pre...]
    slice x0 -> x5, local copies, waits for them, and re-layouts: none -> 3.48 us  [body(): m[b * s_rows + tj, 0]]
    mul x3 -> x0, other arithmetic: 2.36 us -> none  [the longest x1 2.34 us: on_device(): values.reshape(row_tiles, TB, col_tiles, TB)]
  transfers between devices with their start and end apart: 2 -> 19, of which waited for: 2 -> 9; matrix products, arithmetic and copies ran while one was open for 0% -> 5% of each run, Pallas kernels for 0% -> 18%
where the time goes in v1:
time: 119 us
  waiting for transfers between devices  44.1 us (37%)
  Pallas kernels  34.4 us (29%)
  starting transfers between devices  25.8 us (22%)
  local copies, waits for them, and re-layouts  8.68 us (7%)
  between operations  4.93 us (4%)
    ppermute x19, waiting for transfers between devices, send(): return lax.ppermute(x, AXES, pairs)  44.1 us
    ppermute x19, starting transfers between devices, send(): return lax.ppermute(x, AXES, pairs)  25.8 us
    pallas_call x1, Pallas kernels, dots(): pl.pallas_call(functools.partial(dot_kernel, slots, pairs, rows, cols), o...  13.4 us
    pallas_call x1, Pallas kernels, finish(): pl.pallas_call(functools.partial(last_kernel, slots, n_parts, pair, rows,...  6.98 us
    pallas_call x1, Pallas kernels, panel(): pl.pallas_call(functools.partial(panel_kernel, slots, n, rows), out_shape...  6.57 us
    pallas_call x1, Pallas kernels, scale(): pl.pallas_call(functools.partial(scale_kernel, n, order), out_shape=jax.S...  3.63 us
    slice x5, local copies, waits for them, and re-layouts, body(): m[b * s_rows + tj, 0]  3.48 us
    unnamed x27, local copies, waits for them, and re-layouts  3.34 us
  transfers between devices with their start and end apart: 19, of which 9 were waited for; matrix products, arithmetic and copies ran while one was open for 5% of the time, Pallas kernels for 18%

profile of v1, /device:TPU:0, one launch (start us, length us, event | category | flops | bytes accessed | tf_op | source)
XLA Modules:
  0.0 118.7 jit_solution(3852902072655801744)
XLA Ops:
  0.0 2.5 %pack.1.refs_0_ = bf16[3088,128]{1,0:T(8,128)(2,1)} custom-call(s32[4,8]{1,0:T(4,128)} %bitcast.32, bf16[1024,512]{1,0:T(8,128)(2,1)} %block_ref.1), custom_call_target="tpu_custom_call" | custom-call | flops 1000000 | bytes 2097152 | tf_op jit(solution)/shard_map/pack/pallas_call | solution.py:53
  2.5 3.0 %collective-permute-start.5 = (bf16[3088,128]{1,0:T(8,128)(2,1)}, bf16[3088,128]{1,0:T(8,128)(2,1)S(1)}, u32[]{:S(2)}, u32[]{:S(2)}) collective-permute-start(bf16[3088,128]{1,0:T(8,128)(2,1)} %pack.1.refs_0_), channel_id=1, source_target_pairs={{0,8},{1,9},{2,10},{3,11},{4,12},{5,13},{6,14},{7,15},{8,0},{9,1},... | collective-permute-start | bytes 2371592 | tf_op jit(solution)/shard_map/ppermute | solution.py:378
  5.4 2.6 %collective-permute-start.14 = (bf16[3088,128]{1,0:T(8,128)(2,1)}, bf16[3088,128]{1,0:T(8,128)(2,1)}, u32[]{:S(2)}, u32[]{:S(2)}) collective-permute-start(bf16[3088,128]{1,0:T(8,128)(2,1)} %pack.1.refs_0_), channel_id=1, source_target_pairs={{4,0},{5,1},{6,2},{7,3},{0,4},{1,5},{2,6},{3,7},{12,8},{13,9},{14,... | collective-permute-start | bytes 2371592 | tf_op jit(solution)/shard_map/ppermute | solution.py:378
  8.0 1.5 %collective-permute-start.6 = (bf16[3088,128]{1,0:T(8,128)(2,1)}, bf16[3088,128]{1,0:T(8,128)(2,1)S(1)}, u32[]{:S(2)}, u32[]{:S(2)}) collective-permute-start(bf16[3088,128]{1,0:T(8,128)(2,1)} %pack.1.refs_0_), channel_id=1, source_target_pairs={{0,16},{1,17},{2,18},{3,19},{4,20},{5,21},{6,22},{7,23},{8,24},{9,... | collective-permute-start | bytes 2371592 | tf_op jit(solution)/shard_map/ppermute | solution.py:378
  10.0 1.6 %collective-permute-start.18 = (bf16[3088,128]{1,0:T(8,128)(2,1)}, bf16[3088,128]{1,0:T(8,128)(2,1)}, u32[]{:S(2)}, u32[]{:S(2)}) collective-permute-start(bf16[3088,128]{1,0:T(8,128)(2,1)} %pack.1.refs_0_), channel_id=1, source_target_pairs={{2,0},{3,1},{0,2},{1,3},{6,4},{7,5},{4,6},{5,7},{10,8},{11,9},{8,1... | collective-permute-start | bytes 2371592 | tf_op jit(solution)/shard_map/ppermute | solution.py:378
  11.6 12.6 %collective-permute-done.5.refs_1_ = bf16[3088,128]{1,0:T(8,128)(2,1)S(1)} collective-permute-done((bf16[3088,128]{1,0:T(8,128)(2,1)}, bf16[3088,128]{1,0:T(8,128)(2,1)S(1)}, u32[]{:S(2)}, u32[]{:S(2)}) %collective-permute-start.5) | collective-permute-done | bytes 790560 | tf_op jit(solution)/shard_map/ppermute | solution.py:378
  24.2 1.6 %collective-permute-start.12 = (bf16[3088,128]{1,0:T(8,128)(2,1)}, bf16[3088,128]{1,0:T(8,128)(2,1)}, u32[]{:S(2)}, u32[]{:S(2)}) collective-permute-start(bf16[3088,128]{1,0:T(8,128)(2,1)} %pack.1.refs_0_), channel_id=1, source_target_pairs={{4,2},{5,3},{2,4},{3,5},{12,10},{13,11},{10,12},{11,13},{20,18},{2... | collective-permute-start | bytes 2371592 | tf_op jit(solution)/shard_map/ppermute | solution.py:378
  25.8 18.1 %collective-permute-done.14.refs_4_ = bf16[3088,128]{1,0:T(8,128)(2,1)} collective-permute-done((bf16[3088,128]{1,0:T(8,128)(2,1)}, bf16[3088,128]{1,0:T(8,128)(2,1)}, u32[]{:S(2)}, u32[]{:S(2)}) %collective-permute-start.14) | collective-permute-done | bytes 790560 | tf_op jit(solution)/shard_map/ppermute | solution.py:378
  48.9 6.6 %panel.1 = (bf16[4096,512]{1,0:T(8,128)(2,1)S(1)}, f32[8,128]{1,0:T(8,128)}) custom-call(s32[4]{0:T(128)S(1)} %pad_add_fusion.me_ref, bf16[3088,128]{1,0:T(8,128)(2,1)} %pack.1.refs_0_, bf16[3088,128]{1,0:T(8,128)(2,1)} %copy-done.3, bf16[3088,128]{1,0:T(8,128)(2,1)} %copy-done.4, bf16[3088,128]{1,0:T(8,128)(2,1)} %copy-done.5), custom_call_target="tpu_custom_call" | custom-call | flops 10000000 | bytes 8388608 | tf_op jit(solution)/shard_map/panel/pallas_call | solution.py:102
  57.8 4.6 %collective-permute-start.10 = (f32[16,128]{1,0:T(8,128)S(1)}, f32[16,128]{1,0:T(8,128)S(1)}, u32[]{:S(2)}, u32[]{:S(2)}) collective-permute-start(f32[16,128]{1,0:T(8,128)S(1)} %constant_dynamic-update-slice_fusion.1.refs_0_), channel_id=1, source_target_pairs={{0,4},{1,5},{2,6},{3,7},{4,0},{5,1},{6,2},{7,3},{8,12},{9,13},{10,... | collective-permute-start | bytes 24584 | tf_op jit(solution)/shard_map/ppermute | solution.py:378
  62.3 1.6 %collective-permute-done.10.refs_2_ = f32[16,128]{1,0:T(8,128)S(1)} collective-permute-done((f32[16,128]{1,0:T(8,128)S(1)}, f32[16,128]{1,0:T(8,128)S(1)}, u32[]{:S(2)}, u32[]{:S(2)}) %collective-permute-start.10) | collective-permute-done | bytes 8224 | tf_op jit(solution)/shard_map/ppermute | solution.py:378
  64.0 1.4 %collective-permute-start.11 = (f32[16,128]{1,0:T(8,128)S(1)}, f32[16,128]{1,0:T(8,128)S(1)}, u32[]{:S(2)}, u32[]{:S(2)}) collective-permute-start(f32[16,128]{1,0:T(8,128)S(1)} %constant_dynamic-update-slice_fusion.1.refs_0_), channel_id=1, source_target_pairs={{0,6},{1,7},{2,4},{3,5},{4,2},{5,3},{6,0},{7,1},{8,14},{9,15},{10,... | collective-permute-start | bytes 24584 | tf_op jit(solution)/shard_map/ppermute | solution.py:378
  65.3 4.1 %collective-permute-done.11.refs_3_ = f32[16,128]{1,0:T(8,128)S(1)} collective-permute-done((f32[16,128]{1,0:T(8,128)S(1)}, f32[16,128]{1,0:T(8,128)S(1)}, u32[]{:S(2)}, u32[]{:S(2)}) %collective-permute-start.11) | collective-permute-done | bytes 8224 | tf_op jit(solution)/shard_map/ppermute | solution.py:378
  69.6 3.5 %collective-permute-done.9.refs_1_ = f32[16,128]{1,0:T(8,128)S(1)} collective-permute-done((f32[16,128]{1,0:T(8,128)S(1)}, f32[16,128]{1,0:T(8,128)S(1)}, u32[]{:S(2)}, u32[]{:S(2)}) %collective-permute-start.9) | collective-permute-done | bytes 8224 | tf_op jit(solution)/shard_map/ppermute | solution.py:378
  73.1 1.5 %collective-permute-start.13 = (bf16[3088,128]{1,0:T(8,128)(2,1)}, bf16[3088,128]{1,0:T(8,128)(2,1)}, u32[]{:S(2)}, u32[]{:S(2)}) collective-permute-start(bf16[3088,128]{1,0:T(8,128)(2,1)} %collective-permute-done.12), channel_id=1, source_target_pairs={{2,3},{3,2},{4,5},{5,4},{10,11},{11,10},{12,13},{13,12},{18,19},{1... | collective-permute-start | bytes 2371592 | tf_op jit(solution)/shard_map/ppermute | solution.py:378
  74.6 1.9 %collective-permute-start.16 = (bf16[3088,128]{1,0:T(8,128)(2,1)}, bf16[3088,128]{1,0:T(8,128)(2,1)}, u32[]{:S(2)}, u32[]{:S(2)}) collective-permute-start(bf16[3088,128]{1,0:T(8,128)(2,1)} %collective-permute-done.15), channel_id=1, source_target_pairs={{0,1},{1,0},{6,7},{7,6},{8,9},{9,8},{14,15},{15,14},{16,17},{17,16... | collective-permute-start | bytes 2371592 | tf_op jit(solution)/shard_map/ppermute | solution.py:378
  84.8 1.4 %cuts.1 = f32[8,512]{1,0:T(8,128)S(1)} custom-call(s32[4]{0:T(128)S(1)} %pad_add_fusion.me_ref, f32[16,128]{1,0:T(8,128)} %copy-done.6, f32[16,128]{1,0:T(8,128)} %copy-done.12, f32[16,128]{1,0:T(8,128)} %copy-done.10, f32[16,128]{1,0:T(8,128)} %copy-done.11, s32[1,512]{1,0:T(1,128)S(1)} %bitcast.31, bf16[4096,512]{1,0:T(8,128)(2,1)S(1)} %get-tuple-element.296.refs_6_.refs_5_), custom_call_target="tpu_custom_call" | custom-call | flops 10000000 | bytes 4194304 | tf_op jit(solution)/shard_map/cuts/pallas_call | solution.py:201
  87.1 13.4 %dots.1 = f32[1024,512]{1,0:T(8,128)S(1)} custom-call(s32[4]{0:T(128)S(1)} %pad_add_fusion.me_ref, bf16[3088,128]{1,0:T(8,128)(2,1)} %pack.1.refs_0_, bf16[3088,128]{1,0:T(8,128)(2,1)} %copy-done.16, bf16[3088,128]{1,0:T(8,128)(2,1)} %collective-permute-done.18.refs_2_, bf16[3088,128]{1,0:T(8,128)(2,1)} %collective-permute-done.19.refs_3_, ...), custom_call_target="tpu_custom_call" | custom-call | flops 3221225472 | bytes 18874368 | tf_op jit(solution)/shard_map/dots/pallas_call | solution.py:156
  100.6 18.2 %conditional.1 = (bf16[1024,512]{1,0:T(8,128)(2,1)}) conditional(s32[]{:T(128)} %bitcast.5, (s32[8,4]{0,1:T(4,128)S(1)}, s32[4]{0:T(128)S(1)}, bf16[3088,128]{1,0:T(8,128)(2,1)}, bf16[3088,128]{1,0:T(8,128)(2,1)}, bf16[3088,128]{1,0:T(8,128)(2,1)}, /*index=5*/bf16[3088,128]{1,0:T(8,128)(2,1)}, bf16[4096,512]{1,0:T(8,128)(2,1)S(1)}, ...), branch_computations={%region_0.1_spmd, %region_1.10_spmd} | conditional | flops 1074790400 | bytes 55080728 | solution.py:452
  100.6 7.0 %finish.1 = (f32[1024,512]{1,0:T(8,128)}, f32[8,512]{1,0:T(8,128)}) custom-call(s32[4]{0:T(128)S(1)} %get-tuple-element.265.me_ref, s32[4,8]{1,0:T(4,128)S(1)} %bitcast.33, bf16[3088,128]{1,0:T(8,128)(2,1)} %get-tuple-element.267.refs_0_, bf16[3088,128]{1,0:T(8,128)(2,1)} %get-tuple-element.268.refs_1_, bf16[3088,128]{1,0:T(8,128)(2,1)} %get-tuple-element.269.refs_2_, ...), custom_call_target="tpu_custom_call" | custom-call | flops 1073741824 | bytes 6291456 | tf_op jit(solution)/shard_map/cond/branch_0_fun/finish/pallas_call | solution.py:252
  108.2 1.5 %collective-permute-start.1 = (f32[8,512]{1,0:T(8,128)}, f32[8,512]{1,0:T(8,128)S(1)}, u32[]{:S(2)}, u32[]{:S(2)}) collective-permute-start(f32[8,512]{1,0:T(8,128)} %get-tuple-element.275.refs_0_), channel_id=1, source_target_pairs={{0,16},{1,17},{2,18},{3,19},{4,20},{5,21},{6,22},{7,23},{8,24},{9,... | collective-permute-start | bytes 49160 | tf_op jit(solution)/shard_map/cond/branch_0_fun/ppermute | solution.py:378
  109.7 1.5 %collective-permute-start.2 = (f32[8,512]{1,0:T(8,128)}, f32[8,512]{1,0:T(8,128)S(1)}, u32[]{:S(2)}, u32[]{:S(2)}) collective-permute-start(f32[8,512]{1,0:T(8,128)} %get-tuple-element.275.refs_0_), channel_id=1, source_target_pairs={{0,24},{1,25},{2,26},{3,27},{4,28},{5,29},{6,30},{7,31},{8,16},{9,... | collective-permute-start | bytes 49160 | tf_op jit(solution)/shard_map/cond/branch_0_fun/ppermute | solution.py:378
  112.1 2.4 %collective-permute-done.2.refs_3_ = f32[8,512]{1,0:T(8,128)S(1)} collective-permute-done((f32[8,512]{1,0:T(8,128)}, f32[8,512]{1,0:T(8,128)S(1)}, u32[]{:S(2)}, u32[]{:S(2)}) %collective-permute-start.2) | collective-permute-done | bytes 16416 | tf_op jit(solution)/shard_map/cond/branch_0_fun/ppermute | solution.py:378
  115.1 3.6 %scale.1 = bf16[1024,512]{1,0:T(8,128)(2,1)} custom-call(f32[1024,512]{1,0:T(8,128)} %get-tuple-element.274.x_ref, f32[8,512]{1,0:T(8,128)} %get-tuple-element.275.refs_0_, f32[8,512]{1,0:T(8,128)} %copy-done.7, f32[8,512]{1,0:T(8,128)} %copy-done.8, f32[8,512]{1,0:T(8,128)} %copy-done.9), custom_call_target="tpu_custom_call" | custom-call | flops 1048576 | bytes 3145728 | tf_op jit(solution)/shard_map/cond/branch_0_fun/scale/pallas_call | solution.py:286
  (62 shorter events, 14.5 us)
Async XLA Ops:
  2.5 53.1 %copy-start.2 = (bf16[3088,128]{1,0:T(8,128)(2,1)S(1)}, bf16[3088,128]{1,0:T(8,128)(2,1)}, u32[]{:S(2)}) copy-start(bf16[3088,128]{1,0:T(8,128)(2,1)} %pack.1.refs_0_) | copy-start | bytes 2371588
  2.5 82.3 %copy-start.13 = (s32[512]{0:T(512)S(1)}, s32[512]{0:T(512)}, u32[]{:S(2)}) copy-start(s32[512]{0:T(512)} %param.14) | copy-start | bytes 6148
  2.5 21.7 %collective-permute-start.5 = (bf16[3088,128]{1,0:T(8,128)(2,1)}, bf16[3088,128]{1,0:T(8,128)(2,1)S(1)}, u32[]{:S(2)}, u32[]{:S(2)}) collective-permute-start(bf16[3088,128]{1,0:T(8,128)(2,1)} %pack.1.refs_0_), channel_id=1, source_target_pairs={{0,8},{1,9},{2,10},{3,11},{4,12},{5,13},{6,14},{7,15},{8,0},{9,1},... | collective-permute-start | bytes 2371592 | tf_op jit(solution)/shard_map/ppermute | solution.py:378
  5.4 38.4 %collective-permute-start.14 = (bf16[3088,128]{1,0:T(8,128)(2,1)}, bf16[3088,128]{1,0:T(8,128)(2,1)}, u32[]{:S(2)}, u32[]{:S(2)}) collective-permute-start(bf16[3088,128]{1,0:T(8,128)(2,1)} %pack.1.refs_0_), channel_id=1, source_target_pairs={{4,0},{5,1},{6,2},{7,3},{0,4},{1,5},{2,6},{3,7},{12,8},{13,9},{14,... | collective-permute-start | bytes 2371592 | tf_op jit(solution)/shard_map/ppermute | solution.py:378
  8.0 39.1 %collective-permute-start.6 = (bf16[3088,128]{1,0:T(8,128)(2,1)}, bf16[3088,128]{1,0:T(8,128)(2,1)S(1)}, u32[]{:S(2)}, u32[]{:S(2)}) collective-permute-start(bf16[3088,128]{1,0:T(8,128)(2,1)} %pack.1.refs_0_), channel_id=1, source_target_pairs={{0,16},{1,17},{2,18},{3,19},{4,20},{5,21},{6,22},{7,23},{8,24},{9,... | collective-permute-start | bytes 2371592 | tf_op jit(solution)/shard_map/ppermute | solution.py:378
  9.5 37.6 %collective-permute-start.7 = (bf16[3088,128]{1,0:T(8,128)(2,1)}, bf16[3088,128]{1,0:T(8,128)(2,1)S(1)}, u32[]{:S(2)}, u32[]{:S(2)}) collective-permute-start(bf16[3088,128]{1,0:T(8,128)(2,1)} %pack.1.refs_0_), channel_id=1, source_target_pairs={{0,24},{1,25},{2,26},{3,27},{4,28},{5,29},{6,30},{7,31},{8,16},{9,... | collective-permute-start | bytes 2371592 | tf_op jit(solution)/shard_map/ppermute | solution.py:378
  10.0 46.0 %collective-permute-start.18 = (bf16[3088,128]{1,0:T(8,128)(2,1)}, bf16[3088,128]{1,0:T(8,128)(2,1)}, u32[]{:S(2)}, u32[]{:S(2)}) collective-permute-start(bf16[3088,128]{1,0:T(8,128)(2,1)} %pack.1.refs_0_), channel_id=1, source_target_pairs={{2,0},{3,1},{0,2},{1,3},{6,4},{7,5},{4,6},{5,7},{10,8},{11,9},{8,1... | collective-permute-start | bytes 2371592 | tf_op jit(solution)/shard_map/ppermute | solution.py:378
  24.2 22.9 %copy-start.3 = (bf16[3088,128]{1,0:T(8,128)(2,1)}, bf16[3088,128]{1,0:T(8,128)(2,1)S(1)}, u32[]{:S(2)}) copy-start(bf16[3088,128]{1,0:T(8,128)(2,1)S(1)} %collective-permute-done.5.refs_1_) | copy-start | bytes 2371588
  24.2 33.6 %collective-permute-start.12 = (bf16[3088,128]{1,0:T(8,128)(2,1)}, bf16[3088,128]{1,0:T(8,128)(2,1)}, u32[]{:S(2)}, u32[]{:S(2)}) collective-permute-start(bf16[3088,128]{1,0:T(8,128)(2,1)} %pack.1.refs_0_), channel_id=1, source_target_pairs={{4,2},{5,3},{2,4},{3,5},{12,10},{13,11},{10,12},{11,13},{20,18},{2... | collective-permute-start | bytes 2371592 | tf_op jit(solution)/shard_map/ppermute | solution.py:378
  43.9 30.8 %collective-permute-start.15 = (bf16[3088,128]{1,0:T(8,128)(2,1)}, bf16[3088,128]{1,0:T(8,128)(2,1)}, u32[]{:S(2)}, u32[]{:S(2)}) collective-permute-start(bf16[3088,128]{1,0:T(8,128)(2,1)} %collective-permute-done.14.refs_4_), channel_id=1, source_target_pairs={{2,0},{3,1},{4,6},{5,7},{10,8},{11,9},{12,14},{13,15},{18,16},{19,... | collective-permute-start | bytes 2371592 | tf_op jit(solution)/shard_map/ppermute | solution.py:378
  55.5 1.4 %collective-permute-start.8 = (f32[8,128]{1,0:T(8,128)}, f32[8,128]{1,0:T(8,128)S(1)}, u32[]{:S(2)}, u32[]{:S(2)}) collective-permute-start(f32[8,128]{1,0:T(8,128)} %get-tuple-element.295), channel_id=1, source_target_pairs={{0,1},{1,0},{2,3},{3,2},{4,5},{5,4},{6,7},{7,6},{8,9},{9,8},{10,11... | collective-permute-start | bytes 12296 | tf_op jit(solution)/shard_map/ppermute | solution.py:378
  55.6 30.7 %collective-permute-start.17 = (bf16[3088,128]{1,0:T(8,128)(2,1)S(1)}, bf16[3088,128]{1,0:T(8,128)(2,1)S(1)}, u32[]{:S(2)}, u32[]{:S(2)}) collective-permute-start(bf16[3088,128]{1,0:T(8,128)(2,1)S(1)} %copy-done.2), channel_id=1, source_target_pairs={{0,1},{1,0},{2,3},{3,2},{4,5},{5,4},{6,7},{7,6},{8,9},{9,8},{10,11... | collective-permute-start | bytes 2371592 | tf_op jit(solution)/shard_map/ppermute | solution.py:378
  56.1 30.2 %collective-permute-start.20 = (bf16[3088,128]{1,0:T(8,128)(2,1)}, bf16[3088,128]{1,0:T(8,128)(2,1)}, u32[]{:S(2)}, u32[]{:S(2)}) collective-permute-start(bf16[3088,128]{1,0:T(8,128)(2,1)} %collective-permute-done.14.refs_4_), channel_id=1, source_target_pairs={{0,1},{1,0},{2,3},{3,2},{4,5},{5,4},{6,7},{7,6},{8,9},{9,8},{10,11... | collective-permute-start | bytes 2371592 | tf_op jit(solution)/shard_map/ppermute | solution.py:378
  56.9 30.2 %collective-permute-start.19 = (bf16[3088,128]{1,0:T(8,128)(2,1)}, bf16[3088,128]{1,0:T(8,128)(2,1)}, u32[]{:S(2)}, u32[]{:S(2)}) collective-permute-start(bf16[3088,128]{1,0:T(8,128)(2,1)} %collective-permute-done.18.refs_2_), channel_id=1, source_target_pairs={{0,1},{1,0},{2,3},{3,2},{4,5},{5,4},{6,7},{7,6},{8,9},{9,8},{10,11... | collective-permute-start | bytes 2371592 | tf_op jit(solution)/shard_map/ppermute | solution.py:378
  57.8 27.0 %copy-start.6 = (f32[16,128]{1,0:T(8,128)}, f32[16,128]{1,0:T(8,128)S(1)}, u32[]{:S(2)}) copy-start(f32[16,128]{1,0:T(8,128)S(1)} %constant_dynamic-update-slice_fusion.1.refs_0_) | copy-start | bytes 24580
  57.8 6.2 %collective-permute-start.10 = (f32[16,128]{1,0:T(8,128)S(1)}, f32[16,128]{1,0:T(8,128)S(1)}, u32[]{:S(2)}, u32[]{:S(2)}) collective-permute-start(f32[16,128]{1,0:T(8,128)S(1)} %constant_dynamic-update-slice_fusion.1.refs_0_), channel_id=1, source_target_pairs={{0,4},{1,5},{2,6},{3,7},{4,0},{5,1},{6,2},{7,3},{8,12},{9,13},{10,... | collective-permute-start | bytes 24584 | tf_op jit(solution)/shard_map/ppermute | solution.py:378
  64.0 20.8 %copy-start.10 = (f32[16,128]{1,0:T(8,128)}, f32[16,128]{1,0:T(8,128)S(1)}, u32[]{:S(2)}) copy-start(f32[16,128]{1,0:T(8,128)S(1)} %collective-permute-done.10.refs_2_) | copy-start | bytes 24580
  64.0 5.4 %collective-permute-start.11 = (f32[16,128]{1,0:T(8,128)S(1)}, f32[16,128]{1,0:T(8,128)S(1)}, u32[]{:S(2)}, u32[]{:S(2)}) collective-permute-start(f32[16,128]{1,0:T(8,128)S(1)} %constant_dynamic-update-slice_fusion.1.refs_0_), channel_id=1, source_target_pairs={{0,6},{1,7},{2,4},{3,5},{4,2},{5,3},{6,0},{7,1},{8,14},{9,15},{10,... | collective-permute-start | bytes 24584 | tf_op jit(solution)/shard_map/ppermute | solution.py:378
  69.4 3.7 %collective-permute-start.9 = (f32[16,128]{1,0:T(8,128)S(1)}, f32[16,128]{1,0:T(8,128)S(1)}, u32[]{:S(2)}, u32[]{:S(2)}) collective-permute-start(f32[16,128]{1,0:T(8,128)S(1)} %constant_dynamic-update-slice_fusion.1.refs_0_), channel_id=1, source_target_pairs={{0,2},{1,3},{2,0},{3,1},{4,6},{5,7},{6,4},{7,5},{8,10},{9,11},{10,... | collective-permute-start | bytes 24584 | tf_op jit(solution)/shard_map/ppermute | solution.py:378
  73.1 27.4 %collective-permute-start.13 = (bf16[3088,128]{1,0:T(8,128)(2,1)}, bf16[3088,128]{1,0:T(8,128)(2,1)}, u32[]{:S(2)}, u32[]{:S(2)}) collective-permute-start(bf16[3088,128]{1,0:T(8,128)(2,1)} %collective-permute-done.12), channel_id=1, source_target_pairs={{2,3},{3,2},{4,5},{5,4},{10,11},{11,10},{12,13},{13,12},{18,19},{1... | collective-permute-start | bytes 2371592 | tf_op jit(solution)/shard_map/ppermute | solution.py:378
  74.6 25.9 %collective-permute-start.16 = (bf16[3088,128]{1,0:T(8,128)(2,1)}, bf16[3088,128]{1,0:T(8,128)(2,1)}, u32[]{:S(2)}, u32[]{:S(2)}) collective-permute-start(bf16[3088,128]{1,0:T(8,128)(2,1)} %collective-permute-done.15), channel_id=1, source_target_pairs={{0,1},{1,0},{6,7},{7,6},{8,9},{9,8},{14,15},{15,14},{16,17},{17,16... | collective-permute-start | bytes 2371592 | tf_op jit(solution)/shard_map/ppermute | solution.py:378
  107.6 4.0 %collective-permute-start = (f32[8,512]{1,0:T(8,128)}, f32[8,512]{1,0:T(8,128)S(1)}, u32[]{:S(2)}, u32[]{:S(2)}) collective-permute-start(f32[8,512]{1,0:T(8,128)} %get-tuple-element.275.refs_0_), channel_id=1, source_target_pairs={{0,8},{1,9},{2,10},{3,11},{4,12},{5,13},{6,14},{7,15},{8,0},{9,1},... | collective-permute-start | bytes 49160 | tf_op jit(solution)/shard_map/cond/branch_0_fun/ppermute | solution.py:378
  108.2 3.9 %collective-permute-start.1 = (f32[8,512]{1,0:T(8,128)}, f32[8,512]{1,0:T(8,128)S(1)}, u32[]{:S(2)}, u32[]{:S(2)}) collective-permute-start(f32[8,512]{1,0:T(8,128)} %get-tuple-element.275.refs_0_), channel_id=1, source_target_pairs={{0,16},{1,17},{2,18},{3,19},{4,20},{5,21},{6,22},{7,23},{8,24},{9,... | collective-permute-start | bytes 49160 | tf_op jit(solution)/shard_map/cond/branch_0_fun/ppermute | solution.py:378
  109.7 4.8 %collective-permute-start.2 = (f32[8,512]{1,0:T(8,128)}, f32[8,512]{1,0:T(8,128)S(1)}, u32[]{:S(2)}, u32[]{:S(2)}) collective-permute-start(f32[8,512]{1,0:T(8,128)} %get-tuple-element.275.refs_0_), channel_id=1, source_target_pairs={{0,24},{1,25},{2,26},{3,27},{4,28},{5,29},{6,30},{7,31},{8,16},{9,... | collective-permute-start | bytes 49160 | tf_op jit(solution)/shard_map/cond/branch_0_fun/ppermute | solution.py:378
  (11 other events, 78.6 us)

commit v2 on v0

v2 whole, which is shorter than its diff:
```python
import functools

import jax
import jax.numpy as jnp
from jax import lax
from jax.experimental import pallas as pl
from jax.experimental.pallas import tpu as pltpu
from jax.sharding import PartitionSpec as P

TB = 128
PAD = 16
AXES = ("row", "col")
F32, BF16, I32 = jnp.float32, jnp.bfloat16, jnp.int32
VMEM = pl.BlockSpec(memory_space=pltpu.VMEM)
SMEM = pl.BlockSpec(memory_space=pltpu.SMEM)


def params(mib):
    return pltpu.CompilerParams(vmem_limit_bytes=mib * 1024 * 1024)


def cost(flops, moved):
    return pl.CostEstimate(flops=int(flops), bytes_accessed=int(moved), transcendentals=0)


def tiles_of(shape):
    return shape[0] // TB, shape[1] // TB


def place():
    col = lax.axis_index("col")
    return lax.axis_index("row"), col // 2, col % 2


def pack_kernel(slots, mask_ref, block_ref, out_ref):
    ti, tj = tiles_of(block_ref.shape)
    lane = lax.broadcasted_iota(I32, (PAD, TB), 1)
    table = jnp.full((PAD, TB), -1, I32)
    used = jnp.int32(0)
    for i in range(ti):
        for j in range(tj):
            stored = mask_ref[j, i]
            fits = jnp.logical_and(stored > 0, used < slots)

            @pl.when(fits)
            def _(i=i, j=j, used=used):
                at = pl.multiple_of(used * TB, TB)
                out_ref[pl.ds(at, TB), :] = block_ref[i * TB : (i + 1) * TB, j * TB : (j + 1) * TB]

            table = jnp.where(lane == i * tj + j, jnp.where(fits, used, -1), table)
            used = used + stored
    table = jnp.where(lane == ti * tj, used, table)
    out_ref[slots * TB :, :] = table.astype(F32).astype(BF16)


def pack(block, mask_t, slots):
    return pl.pallas_call(
        functools.partial(pack_kernel, slots),
        out_shape=jax.ShapeDtypeStruct((slots * TB + PAD, TB), BF16),
        in_specs=[SMEM, VMEM],
        out_specs=VMEM,
        compiler_params=params(8),
        cost_estimate=cost(1e6, 2 * block.size * 2),
        name="pack",
    )(mask_t, block)


def read_tables(blocks, itab, stab, sem):
    for q, parts in enumerate(blocks):
        end = parts[-1].shape[0]
        table = parts[-1][end - PAD : end, :].astype(F32).astype(I32)
        itab[q : q + 1, :] = table[0:1, :]
    copy = pltpu.make_async_copy(itab, stab, sem)
    copy.start()
    copy.wait()


def tile_from(parts, slot):
    def load(ref, at):
        return ref[pl.ds(pl.multiple_of(at * TB, TB), TB), :]

    tile = load(parts[0], jnp.maximum(slot, 0))
    if len(parts) == 2:
        first = parts[0].shape[0] // TB
        tile = load(parts[0], jnp.clip(slot, 0, first - 1))
        tile = jnp.where(slot >= first, load(parts[1], jnp.maximum(slot - first, 0)), tile)
    return jnp.where(slot >= 0, tile, jnp.zeros((TB, TB), BF16))


def table_scratch(n):
    n8 = -(-n // 8) * 8
    return [pltpu.VMEM((n8, TB), I32), pltpu.SMEM((n8, TB), I32), pltpu.SemaphoreType.DMA]


def regroup(refs, sizes):
    out = []
    for s in sizes:
        out.append(refs[:s])
        refs = refs[s:]
    return out


def panel_kernel(slots, sizes, rows, *refs):
    n = len(sizes)
    blocks = regroup(refs, sizes)
    panel_ref, sums_ref, itab, stab, sem = refs[sum(sizes) :]
    cols = panel_ref.shape[1]
    ti, tj = rows // TB, cols // TB
    me = place()[0]
    read_tables(blocks, itab, stab, sem)
    worst = jnp.int32(0)
    sums = tuple(jnp.zeros((8, TB), F32) for _ in range(tj))
    for q in range(n):
        worst = jnp.maximum(worst, stab[q, ti * tj])
        base = (me ^ q) * rows

        def strip(i, sums, q=q, base=base):
            out = []
            for j in range(tj):
                tile = tile_from(blocks[q], stab[q, i * tj + j])
                panel_ref[pl.ds(pl.multiple_of(base + i * TB, TB), TB), j * TB : (j + 1) * TB] = tile
                out.append(sums[j] + jnp.sum(tile.astype(F32).reshape(TB // 8, 8, TB), axis=0))
            return tuple(out)

        sums = lax.fori_loop(0, ti, strip, sums, unroll=2)
    sums_ref[...] = jnp.zeros_like(sums_ref)
    for j in range(tj):
        sums_ref[j : j + 1, :] = jnp.sum(sums[j], axis=0, keepdims=True)
    sums_ref[tj : tj + 1, :] = jnp.full((1, TB), 1.0, F32) * jnp.where(worst > slots, 1.0, 0.0)


def panel(payloads, slots, rows, cols):
    n = len(payloads)
    s_rows = -(-(cols // TB + 1) // 8) * 8
    sizes = [len(p) for p in payloads]
    return pl.pallas_call(
        functools.partial(panel_kernel, slots, sizes, rows),
        out_shape=(
            jax.ShapeDtypeStruct((n * rows, cols), BF16),
            jax.ShapeDtypeStruct((s_rows, TB), F32),
        ),
        in_specs=[VMEM] * sum(sizes),
        out_specs=(VMEM, VMEM),
        scratch_shapes=table_scratch(n),
        compiler_params=params(20),
        cost_estimate=cost(1e7, 2 * n * rows * cols * 2),
        name="panel",
    )(*[x for p in payloads for x in p])


def strip_rows(rows):
    return min(rows, 256)


def unpack_strip(blocks, stab, rows, cols, m, lhs):
    step = strip_rows(rows)
    tj = cols // TB
    for b, parts in enumerate(blocks):
        for a in range(step // TB):
            for j in range(tj):
                tile = tile_from(parts, stab[b, (m * (step // TB) + a) * tj + j])
                lhs[a * TB : (a + 1) * TB, b * cols + j * TB : b * cols + (j + 1) * TB] = tile


def products(blocks, sides, pair, panel_ref, stab, lhs, rows, use):
    cols = panel_ref.shape[1]
    step = strip_rows(rows)
    _, z, core = place()
    n = rows // step
    unpack_strip(blocks, stab, rows, cols, 0, lhs.at[0])
    for m in range(n):
        if m + 1 < n:
            unpack_strip(blocks, stab, rows, cols, m + 1, lhs.at[(m + 1) % 2])
        total = None
        for b, side in enumerate(sides):
            at = pl.multiple_of((z ^ pair) * 2 * cols + (core ^ side) * cols, TB)
            got = jnp.dot(
                lhs[m % 2, :, b * cols : (b + 1) * cols],
                panel_ref[pl.ds(at, cols), :],
                preferred_element_type=F32,
            )
            total = got if total is None else total + got
        use(m, total)


def dot_kernel(n_blocks, sides, pair, rows, has_prior, *refs):
    blocks = regroup(refs, [1] * n_blocks)
    refs = refs[n_blocks:]
    panel_ref = refs[0]
    prior_ref = refs[1] if has_prior else None
    acc_ref, itab, stab, sem, lhs = refs[1 + has_prior :]
    step = strip_rows(rows)
    read_tables(blocks, itab, stab, sem)

    def use(m, got):
        here = slice(m * step, (m + 1) * step)
        acc_ref[here, :] = prior_ref[here, :] + got if has_prior else got

    products(blocks, sides, pair, panel_ref, stab, lhs, rows, use)


def dot_scratch(n, rows, cols):
    return table_scratch(n) + [pltpu.VMEM((2, strip_rows(rows), n * cols), BF16)]


def dots(payloads, sides, pair, dense, prior, rows):
    cols = dense.shape[1]
    n = len(payloads)
    extra = [] if prior is None else [prior]
    return pl.pallas_call(
        functools.partial(dot_kernel, n, sides, pair, rows, len(extra)),
        out_shape=jax.ShapeDtypeStruct((rows, cols), F32),
        in_specs=[VMEM] * (n + 1 + len(extra)),
        out_specs=VMEM,
        scratch_shapes=dot_scratch(n, rows, cols),
        input_output_aliases={n + 1: 0} if extra else {},
        compiler_params=params(20),
        cost_estimate=cost(2 * rows * cols * n * cols, 12 * rows * cols),
        name="dots",
    )(*payloads, dense, *extra)


def means_kernel(n_pairs, s_rows, order, *refs):
    msgs, (thr_ref, panel_ref, out_ref, flag_ref) = refs[:n_pairs], refs[n_pairs:]
    _, z, core = place()
    cols = panel_ref.shape[1]
    tj = cols // TB
    total = jnp.zeros((8, cols), F32)
    row = lax.broadcasted_iota(I32, (8, TB), 0)
    over = jnp.zeros((1, TB), F32)
    for q in range(n_pairs):
        for b in range(2):
            over = jnp.maximum(over, msgs[q][b * s_rows + tj : b * s_rows + tj + 1, :])
            for t in range(tj):
                s = jnp.broadcast_to(msgs[q][b * s_rows + t : b * s_rows + t + 1, :], (8, TB))
                high = s.astype(BF16).astype(F32)
                mid = (s - high).astype(BF16).astype(F32)
                low = s - high - mid
                lhs = jnp.where(row == 0, high, jnp.where(row == 1, mid, jnp.where(row == 2, low, 0.0)))
                at = (z ^ q) * 2 * cols + (core ^ b) * cols + t * TB
                total += jnp.dot(
                    lhs.astype(BF16),
                    panel_ref[pl.ds(pl.multiple_of(at, TB), TB), :],
                    preferred_element_type=F32,
                )
    mean = jnp.sum(total, axis=0, keepdims=True) / order
    out_ref[...] = jnp.broadcast_to(0.125 * thr_ref[...].astype(F32) * mean, out_ref.shape)
    flag_ref[0] = jnp.where(jnp.max(over) > 0.0, 1, 0).astype(I32)


def cuts_of(messages, thr, dense, s_rows, order):
    n = len(messages)
    cols = dense.shape[1]
    return pl.pallas_call(
        functools.partial(means_kernel, n, s_rows, order),
        out_shape=(jax.ShapeDtypeStruct((8, cols), F32), jax.ShapeDtypeStruct((1,), I32)),
        in_specs=[VMEM] * (n + 2),
        out_specs=(VMEM, SMEM),
        compiler_params=params(12),
        cost_estimate=cost(1e7, dense.size * 2),
        name="cuts",
    )(*messages, thr, dense)


def last_kernel(n_blocks, sides, pair, rows, keep_ref, *refs):
    blocks = regroup(refs, [1] * n_blocks)
    panel_ref, prior_ref, cut_ref, acc_ref, tot_ref, itab, stab, sem, lhs = refs[n_blocks:]
    step = strip_rows(rows)
    cols = panel_ref.shape[1]
    read_tables(blocks, itab, stab, sem)
    tot_ref[...] = jnp.zeros_like(tot_ref)
    per = step // TB

    def use(m, got):
        got = prior_ref[m * step : (m + 1) * step, :] + got
        got = jnp.maximum(got - cut_ref[0:1, :], 0.0)
        for a in range(per):
            at = (m * per + a) * TB
            for j in range(cols // TB):
                kept = keep_ref[j, m * per + a].astype(F32)
                cell = got[a * TB : (a + 1) * TB, j * TB : (j + 1) * TB] * kept
                acc_ref[at : at + TB, j * TB : (j + 1) * TB] = cell
                tot_ref[:, j * TB : (j + 1) * TB] += jnp.sum(cell.reshape(TB // 8, 8, TB), axis=0)

    products(blocks, sides, pair, panel_ref, stab, lhs, rows, use)


def finish(keep_t, payloads, sides, pair, dense, prior, cut, rows):
    cols = dense.shape[1]
    n = len(payloads)
    return pl.pallas_call(
        functools.partial(last_kernel, n, sides, pair, rows),
        out_shape=(jax.ShapeDtypeStruct((rows, cols), F32), jax.ShapeDtypeStruct((8, cols), F32)),
        in_specs=[SMEM] + [VMEM] * (n + 3),
        out_specs=(VMEM, VMEM),
        scratch_shapes=dot_scratch(n, rows, cols),
        compiler_params=params(20),
        cost_estimate=cost(2 * rows * cols * n * cols, 12 * rows * cols),
        name="finish",
    )(keep_t, *payloads, dense, prior, cut)


def scale_kernel(n, order, x_ref, *refs):
    tots, out_ref = refs[:n], refs[n]
    total = tots[0][...]
    for t in tots[1:]:
        total = total + t[...]
    total = jnp.sum(total, axis=0, keepdims=True) / order
    factor = 1.0 / jnp.maximum(total, 0.1)
    out_ref[...] = (x_ref[...] * factor).astype(BF16)


def scale(x, totals, order):
    n = len(totals)
    return pl.pallas_call(
        functools.partial(scale_kernel, n, order),
        out_shape=jax.ShapeDtypeStruct(x.shape, BF16),
        in_specs=[VMEM] * (n + 1),
        out_specs=VMEM,
        compiler_params=params(12),
        cost_estimate=cost(2 * x.size, 6 * x.size),
        name="scale",
    )(x, *totals)


def dense_path(values, tile_mask, keep_mask, thr_index, n_row, n_col):
    rows, cols = values.shape
    ti, tj = tiles_of(values.shape)
    matrix = (
        values.reshape(ti, TB, tj, TB) * tile_mask[:, None, :, None].astype(BF16)
    ).reshape(rows, cols)
    kept = jnp.broadcast_to(keep_mask[:, None, :, None].astype(F32), (ti, TB, tj, TB)).reshape(rows, cols)
    r, c = lax.axis_index("row"), lax.axis_index("col")
    order = rows * n_row

    def col_ring(i, carry):
        block, panel_ = carry
        panel_ = lax.dynamic_update_slice(panel_, block, (((r - i) % n_row) * rows, 0))
        return lax.ppermute(block, "row", [(k, (k + 1) % n_row) for k in range(n_row)]), panel_

    _, panel_ = lax.fori_loop(0, n_row, col_ring, (matrix, jnp.zeros((order, cols), BF16)))

    def row_ring(i, carry):
        block, acc = carry
        part = lax.dynamic_slice(panel_, (((c - i) % n_col) * cols, 0), (cols, cols))
        acc = acc + jnp.dot(block, part, preferred_element_type=F32)
        return lax.ppermute(block, "col", [(k, (k + 1) % n_col) for k in range(n_col)]), acc

    _, product = lax.fori_loop(0, n_col, row_ring, (matrix, jnp.zeros((rows, cols), F32)))
    means = lax.psum(jnp.sum(product, axis=0), "row") / order
    pruned = jnp.maximum(product - 0.125 * thr_index.astype(F32) * means, 0.0) * kept
    totals = lax.psum(jnp.sum(pruned, axis=0), "row") / order
    return (pruned / jnp.maximum(totals, 0.1)).astype(BF16)


def on_device(values, tile_mask, keep_mask, thr_index, n_row, n_col):
    return body(values, tile_mask, keep_mask, thr_index, n_row, n_col)


def body(values, tile_mask, keep_mask, thr_index, n_row, n_col):
    rows, cols = values.shape
    ti, tj = tiles_of(values.shape)
    slots = ti * tj * 3 // 4
    half = slots // 2 * TB
    n_z = n_col // 2
    last = n_z - 1
    order = rows * n_row

    def send(x, dr=0, dz=0, dc=0):
        pairs = [
            (r * n_col + z * 2 + c, (r ^ dr) * n_col + (z ^ dz) * 2 + (c ^ dc))
            for r in range(n_row)
            for z in range(n_z)
            for c in range(2)
        ]
        return lax.ppermute(x, AXES, pairs)

    own = pack(values, tile_mask.T, slots)

    line = {0: own}
    for j in range(1, n_z):
        low = j & -j
        line[j] = send(line[j ^ low], dz=low)
    swapped = {j: send(line[j], dc=1) for j in range(n_z)}

    column = {0: [own]}
    for q in range(1, n_row):
        low = q & -q
        rest = q ^ low
        if rest and rest & -rest == rest:
            column[q] = [send(column[low][0][:half], dr=rest), send(column[rest][0][half:], dr=low)]
        else:
            column[q] = [send(own, dr=q)]

    dense, sums = panel([column[q] for q in range(n_row)], slots, rows, cols)
    acc = None
    for j in range(last):
        acc = dots([line[j], swapped[j]], (0, 1), j, dense, acc, rows)
    acc = dots([line[last]], (0,), last, dense, acc, rows)

    both = jnp.concatenate([sums, send(sums, dc=1)], axis=0)
    messages = [both] + [send(both, dz=j) for j in range(1, n_z)]
    cut, over = cuts_of(messages, thr_index.reshape(1, cols), dense, sums.shape[0], order)

    def fast():
        pruned, tot = finish(keep_mask.T, [swapped[last]], (1,), last, dense, acc, cut, rows)
        totals = [tot] + [send(tot, dr=q) for q in range(1, n_row)]
        return scale(pruned, totals, order)

    def full():
        return dense_path(values, tile_mask, keep_mask, thr_index, n_row, n_col)

    return lax.cond(over[0] > 0, full, fast)


def solution(mesh):
    n_row, n_col = mesh.shape["row"], mesh.shape["col"]
    return jax.shard_map(
        functools.partial(on_device, n_row=n_row, n_col=n_col),
        mesh=mesh,
        in_specs=(P("row", "col"), P("row", "col"), P("row", "col"), P("col")),
        out_specs=P("row", "col"),
        check_vma=False,
    )
```

time: 189 us -> 92.4 us (0.49)
  waiting for transfers between devices: 138 us -> 49.6 us
  starting transfers between devices: 0.04 us -> 25 us
  blocking collectives: 17.8 us -> 0 us
  Pallas kernels: 0 us -> 16.7 us
  between operations: 13.5 us -> 0.81 us
  matrix products: 8.14 us -> 0 us
  other arithmetic: 8.02 us -> 0 us
  local copies, waits for them, and re-layouts: 2.87 us -> 0.08 us
    all_gather x2 -> x0, waiting for transfers between devices: 137 us -> none  [the longest x1 83.7 us: on_device(): lax.all_gather(matrix, 'col', axis=1, tiled=True)]
    ppermute x0 -> x18, waiting for transfers between devices: none -> 49.6 us  [send(): return lax.ppermute(x, AXES, pairs)]
    ppermute x0 -> x18, starting transfers between devices: none -> 25 us  [send(): return lax.ppermute(x, AXES, pairs)]
    psum x2 -> x0, blocking collectives: 17.8 us -> none  [the longest x1 9.85 us: on_device(): col_means = lax.psum(jnp.sum(part_prod, axis=0), 'row') / order_all]
    pallas_call x0 -> x9, Pallas kernels: none -> 16.7 us  [the longest x4 8.52 us: dots(): pl.pallas_call(functools.partial(dot_kernel, n, sides, pair, rows, len(ex...]
    dot_general x1 -> x0, matrix products: 8.14 us -> none  [on_device(): jnp.dot(lax.all_gather(matrix, 'col', axis=1, tiled=True), col_panel, pre...]
    mul x3 -> x0, other arithmetic: 2.36 us -> none  [the longest x1 2.34 us: on_device(): values.reshape(row_tiles, TB, col_tiles, TB)]
    unnamed x7 -> x9, local copies, waits for them, and re-layouts: 2.02 us -> 0.02 us
  transfers between devices with their start and end apart: 2 -> 18, of which waited for: 2 -> 8; matrix products, arithmetic and copies ran while one was open for 0% -> 0% of each run, Pallas kernels for 0% -> 13%
where the time goes in v2:
time: 92.4 us; the launch traced here: 92.2 us
  waiting for transfers between devices  49.6 us (54%)
  starting transfers between devices  25 us (27%)
  Pallas kernels  16.7 us (18%)
    ppermute x18, waiting for transfers between devices, send(): return lax.ppermute(x, AXES, pairs)  49.6 us
    ppermute x18, starting transfers between devices, send(): return lax.ppermute(x, AXES, pairs)  25 us
    pallas_call x4, Pallas kernels, dots(): pl.pallas_call(functools.partial(dot_kernel, n, sides, pair, rows, len(ex...  8.52 us
    pallas_call x1, Pallas kernels, panel(): pl.pallas_call(functools.partial(panel_kernel, slots, sizes, rows), out_s...  2.22 us
    pallas_call x1, Pallas kernels, finish(): pl.pallas_call(functools.partial(last_kernel, n, sides, pair, rows), out_...  2.15 us
  transfers between devices with their start and end apart: 18, of which 8 were waited for; matrix products, arithmetic and copies ran while one was open for 0% of the time, Pallas kernels for 13%

profile of v2, /device:TPU:0, one launch (start us, length us, event | category | flops | bytes accessed | tf_op | source)
XLA Modules:
  0.0 92.2 jit_solution(3124205205773058936)
XLA Ops:
  0.0 1.6 %pack.1.refs_0_ = bf16[3088,128]{1,0:T(8,128)(2,1)S(1)} custom-call(s32[4,8]{1,0:T(4,128)} %bitcast.30, bf16[1024,512]{1,0:T(8,128)(2,1)} %block_ref.1), custom_call_target="tpu_custom_call" | custom-call | flops 1000000 | bytes 2097152 | tf_op jit(solution)/shard_map/pack/pallas_call | solution.py:57
  1.6 4.1 %collective-permute-start.13 = (bf16[3088,128]{1,0:T(8,128)(2,1)S(1)}, bf16[3088,128]{1,0:T(8,128)(2,1)S(1)}, u32[]{:S(2)}, u32[]{:S(2)}) collective-permute-start(bf16[3088,128]{1,0:T(8,128)(2,1)S(1)} %pack.1.refs_0_), channel_id=1, source_target_pairs={{0,4},{1,5},{2,6},{3,7},{4,0},{5,1},{6,2},{7,3},{8,12},{9,13},{10,... | collective-permute-start | bytes 2371592 | tf_op jit(solution)/shard_map/ppermute | solution.py:376
  5.7 1.5 %collective-permute-start.5 = (bf16[3088,128]{1,0:T(8,128)(2,1)S(1)}, bf16[3088,128]{1,0:T(8,128)(2,1)S(1)}, u32[]{:S(2)}, u32[]{:S(2)}) collective-permute-start(bf16[3088,128]{1,0:T(8,128)(2,1)S(1)} %pack.1.refs_0_), channel_id=1, source_target_pairs={{0,8},{1,9},{2,10},{3,11},{4,12},{5,13},{6,14},{7,15},{8,0},{9,1},... | collective-permute-start | bytes 2371592 | tf_op jit(solution)/shard_map/ppermute | solution.py:376
  7.2 1.6 %collective-permute-start.17 = (bf16[3088,128]{1,0:T(8,128)(2,1)S(1)}, bf16[3088,128]{1,0:T(8,128)(2,1)S(1)}, u32[]{:S(2)}, u32[]{:S(2)}) collective-permute-start(bf16[3088,128]{1,0:T(8,128)(2,1)S(1)} %pack.1.refs_0_), channel_id=1, source_target_pairs={{0,2},{1,3},{2,0},{3,1},{4,6},{5,7},{6,4},{7,5},{8,10},{9,11},{10,... | collective-permute-start | bytes 2371592 | tf_op jit(solution)/shard_map/ppermute | solution.py:376
  8.8 1.5 %collective-permute-start.6 = (bf16[3088,128]{1,0:T(8,128)(2,1)S(1)}, bf16[3088,128]{1,0:T(8,128)(2,1)S(1)}, u32[]{:S(2)}, u32[]{:S(2)}) collective-permute-start(bf16[3088,128]{1,0:T(8,128)(2,1)S(1)} %pack.1.refs_0_), channel_id=1, source_target_pairs={{0,16},{1,17},{2,18},{3,19},{4,20},{5,21},{6,22},{7,23},{8,24},{9,... | collective-permute-start | bytes 2371592 | tf_op jit(solution)/shard_map/ppermute | solution.py:376
  10.3 30.1 %collective-permute-done.13.refs_0_ = bf16[3088,128]{1,0:T(8,128)(2,1)S(1)} collective-permute-done((bf16[3088,128]{1,0:T(8,128)(2,1)S(1)}, bf16[3088,128]{1,0:T(8,128)(2,1)S(1)}, u32[]{:S(2)}, u32[]{:S(2)}) %collective-permute-start.13) | collective-permute-done | bytes 790560 | tf_op jit(solution)/shard_map/ppermute | solution.py:376
  41.1 1.6 %collective-permute-start.7 = (bf16[1536,128]{1,0:T(8,128)(2,1)S(1)}, bf16[1536,128]{1,0:T(8,128)(2,1)S(1)}, u32[]{:S(2)}, u32[]{:S(2)}) collective-permute-start(bf16[1536,128]{1,0:T(8,128)(2,1)S(1)} %slice.8), channel_id=1, source_target_pairs={{0,16},{1,17},{2,18},{3,19},{4,20},{5,21},{6,22},{7,23},{8,24},{9,... | collective-permute-start | bytes 1179656 | tf_op jit(solution)/shard_map/ppermute | solution.py:376
  43.2 1.5 %collective-permute-start.8 = (bf16[1552,128]{1,0:T(8,128)(2,1)S(1)}, bf16[1552,128]{1,0:T(8,128)(2,1)S(1)}, u32[]{:S(2)}, u32[]{:S(2)}) collective-permute-start(bf16[1552,128]{1,0:T(8,128)(2,1)S(1)} %slice.9), channel_id=1, source_target_pairs={{0,8},{1,9},{2,10},{3,11},{4,12},{5,13},{6,14},{7,15},{8,0},{9,1},... | collective-permute-start | bytes 1191944 | tf_op jit(solution)/shard_map/ppermute | solution.py:376
  44.7 7.2 %collective-permute-done.7.refs_3_ = bf16[1536,128]{1,0:T(8,128)(2,1)S(1)} collective-permute-done((bf16[1536,128]{1,0:T(8,128)(2,1)S(1)}, bf16[1536,128]{1,0:T(8,128)(2,1)S(1)}, u32[]{:S(2)}, u32[]{:S(2)}) %collective-permute-start.7) | collective-permute-done | bytes 393248 | tf_op jit(solution)/shard_map/ppermute | solution.py:376
  51.9 7.2 %collective-permute-done.14.refs_0_ = bf16[3088,128]{1,0:T(8,128)(2,1)S(1)} collective-permute-done((bf16[3088,128]{1,0:T(8,128)(2,1)S(1)}, bf16[3088,128]{1,0:T(8,128)(2,1)S(1)}, u32[]{:S(2)}, u32[]{:S(2)}) %collective-permute-start.14) | collective-permute-done | bytes 790560 | tf_op jit(solution)/shard_map/ppermute | solution.py:376
  59.1 2.2 %panel.1 = (bf16[4096,512]{1,0:T(8,128)(2,1)S(1)}, f32[8,128]{1,0:T(8,128)S(1)}) custom-call(bf16[3088,128]{1,0:T(8,128)(2,1)S(1)} %pack.1.refs_0_, bf16[3088,128]{1,0:T(8,128)(2,1)S(1)} %collective-permute-done.5.refs_1_, bf16[3088,128]{1,0:T(8,128)(2,1)S(1)} %collective-permute-done.6.refs_2_, bf16[1536,128]{1,0:T(8,128)(2,1)S(1)} %collective-permute-done.7.refs_3_, ...), custom_call_target="tpu_custom_call" | custom-call | flops 10000000 | bytes 8388608 | tf_op jit(solution)/shard_map/panel/pallas_call | solution.py:136
  62.8 1.5 %collective-permute-start.10 = (f32[16,128]{1,0:T(8,128)S(1)}, f32[16,128]{1,0:T(8,128)S(1)}, u32[]{:S(2)}, u32[]{:S(2)}) collective-permute-start(f32[16,128]{1,0:T(8,128)S(1)} %constant_dynamic-update-slice_fusion.1.refs_0_), channel_id=1, source_target_pairs={{0,2},{1,3},{2,0},{3,1},{4,6},{5,7},{6,4},{7,5},{8,10},{9,11},{10,... | collective-permute-start | bytes 24584 | tf_op jit(solution)/shard_map/ppermute | solution.py:376
  64.2 3.4 %collective-permute-start.11 = (f32[16,128]{1,0:T(8,128)S(1)}, f32[16,128]{1,0:T(8,128)S(1)}, u32[]{:S(2)}, u32[]{:S(2)}) collective-permute-start(f32[16,128]{1,0:T(8,128)S(1)} %constant_dynamic-update-slice_fusion.1.refs_0_), channel_id=1, source_target_pairs={{0,4},{1,5},{2,6},{3,7},{4,0},{5,1},{6,2},{7,3},{8,12},{9,13},{10,... | collective-permute-start | bytes 24584 | tf_op jit(solution)/shard_map/ppermute | solution.py:376
  67.6 3.1 %collective-permute-start.12 = (f32[16,128]{1,0:T(8,128)S(1)}, f32[16,128]{1,0:T(8,128)S(1)}, u32[]{:S(2)}, u32[]{:S(2)}) collective-permute-start(f32[16,128]{1,0:T(8,128)S(1)} %constant_dynamic-update-slice_fusion.1.refs_0_), channel_id=1, source_target_pairs={{0,6},{1,7},{2,4},{3,5},{4,2},{5,3},{6,0},{7,1},{8,14},{9,15},{10,... | collective-permute-start | bytes 24584 | tf_op jit(solution)/shard_map/ppermute | solution.py:376
  70.7 2.2 %dots.4.refs_3_ = f32[1024,512]{1,0:T(8,128)S(1)} custom-call(bf16[3088,128]{1,0:T(8,128)(2,1)S(1)} %pack.1.refs_0_, bf16[3088,128]{1,0:T(8,128)(2,1)S(1)} %collective-permute-done.19.refs_1_, bf16[4096,512]{1,0:T(8,128)(2,1)S(1)} %get-tuple-element.286.refs_5_.refs_2_.refs_1_), custom_call_target="tpu_custom_call" | custom-call | flops 1073741824 | bytes 6291456 | tf_op jit(solution)/shard_map/dots/pallas_call | solution.py:210
  74.9 2.3 %dots.5.refs_3_ = f32[1024,512]{1,0:T(8,128)S(1)} custom-call(bf16[3088,128]{1,0:T(8,128)(2,1)S(1)} %collective-permute-done.17.refs_0_, bf16[3088,128]{1,0:T(8,128)(2,1)S(1)} %collective-permute-done.18.refs_1_, bf16[4096,512]{1,0:T(8,128)(2,1)S(1)} %get-tuple-element.286.refs_5_.refs_2_.refs_1_, ...), custom_call_target="tpu_custom_call", output_to_operand_aliasing={{}: (3, {})} | custom-call | flops 1073741824 | bytes 6291456 | tf_op jit(solution)/shard_map/dots/pallas_call | solution.py:210
  77.2 2.3 %dots.6.refs_2_ = f32[1024,512]{1,0:T(8,128)S(1)} custom-call(bf16[3088,128]{1,0:T(8,128)(2,1)S(1)} %collective-permute-done.13.refs_0_, bf16[3088,128]{1,0:T(8,128)(2,1)S(1)} %collective-permute-done.16.refs_1_, bf16[4096,512]{1,0:T(8,128)(2,1)S(1)} %get-tuple-element.286.refs_5_.refs_2_.refs_1_, ...), custom_call_target="tpu_custom_call", output_to_operand_aliasing={{}: (3, {})} | custom-call | flops 1073741824 | bytes 6291456 | tf_op jit(solution)/shard_map/dots/pallas_call | solution.py:210
  79.6 1.7 %dots.7 = f32[1024,512]{1,0:T(8,128)S(1)} custom-call(bf16[3088,128]{1,0:T(8,128)(2,1)S(1)} %collective-permute-done.14.refs_0_, bf16[4096,512]{1,0:T(8,128)(2,1)S(1)} %get-tuple-element.286.refs_5_.refs_2_.refs_1_, f32[1024,512]{1,0:T(8,128)S(1)} %dots.6.refs_2_), custom_call_target="tpu_custom_call", output_to_operand_aliasing={{}: (2, {})} | custom-call | flops 536870912 | bytes 6291456 | tf_op jit(solution)/shard_map/dots/pallas_call | solution.py:210
  81.3 10.9 %conditional.1 = (bf16[1024,512]{1,0:T(8,128)(2,1)}) conditional(s32[]{:T(128)} %bitcast.3, (s32[8,4]{0,1:T(4,128)S(1)}, bf16[3088,128]{1,0:T(8,128)(2,1)S(1)}, bf16[4096,512]{1,0:T(8,128)(2,1)S(1)}, f32[1024,512]{1,0:T(8,128)S(1)}, f32[8,512]{1,0:T(8,128)S(1)}) %tuple.93, (s32[8,4]{0,1:T(4,128)S(1)}, bf16[1024,512]{1,0:T(8,128)(2,1)S(1)}, ...), branch_computations={%region_0.0_spmd, %region_1.10_spmd} | conditional | flops 543689792 | bytes 55080728 | solution.py:413
  81.3 2.2 %finish.1 = (f32[1024,512]{1,0:T(8,128)S(1)}, f32[8,512]{1,0:T(8,128)S(1)}) custom-call(s32[4,8]{1,0:T(4,128)S(1)} %bitcast.29, bf16[3088,128]{1,0:T(8,128)(2,1)S(1)} %get-tuple-element.258.refs_0_, bf16[4096,512]{1,0:T(8,128)(2,1)S(1)} %get-tuple-element.259.refs_1_, f32[1024,512]{1,0:T(8,128)S(1)} %get-tuple-element.260.refs_2_, ...), custom_call_target="tpu_custom_call" | custom-call | flops 536870912 | bytes 6291456 | tf_op jit(solution)/shard_map/cond/branch_0_fun/finish/pallas_call | solution.py:291
  83.5 1.5 %collective-permute-start = (f32[8,512]{1,0:T(8,128)S(1)}, f32[8,512]{1,0:T(8,128)S(1)}, u32[]{:S(2)}, u32[]{:S(2)}) collective-permute-start(f32[8,512]{1,0:T(8,128)S(1)} %get-tuple-element.263.refs_0_), channel_id=1, source_target_pairs={{0,8},{1,9},{2,10},{3,11},{4,12},{5,13},{6,14},{7,15},{8,0},{9,1},... | collective-permute-start | bytes 49160 | tf_op jit(solution)/shard_map/cond/branch_0_fun/ppermute | solution.py:376
  85.0 1.5 %collective-permute-start.1 = (f32[8,512]{1,0:T(8,128)S(1)}, f32[8,512]{1,0:T(8,128)S(1)}, u32[]{:S(2)}, u32[]{:S(2)}) collective-permute-start(f32[8,512]{1,0:T(8,128)S(1)} %get-tuple-element.263.refs_0_), channel_id=1, source_target_pairs={{0,16},{1,17},{2,18},{3,19},{4,20},{5,21},{6,22},{7,23},{8,24},{9,... | collective-permute-start | bytes 49160 | tf_op jit(solution)/shard_map/cond/branch_0_fun/ppermute | solution.py:376
  87.3 1.4 %collective-permute-done.1.refs_2_ = f32[8,512]{1,0:T(8,128)S(1)} collective-permute-done((f32[8,512]{1,0:T(8,128)S(1)}, f32[8,512]{1,0:T(8,128)S(1)}, u32[]{:S(2)}, u32[]{:S(2)}) %collective-permute-start.1) | collective-permute-done | bytes 16416 | tf_op jit(solution)/shard_map/cond/branch_0_fun/ppermute | solution.py:376
  88.7 2.4 %collective-permute-done.2.refs_3_ = f32[8,512]{1,0:T(8,128)S(1)} collective-permute-done((f32[8,512]{1,0:T(8,128)S(1)}, f32[8,512]{1,0:T(8,128)S(1)}, u32[]{:S(2)}, u32[]{:S(2)}) %collective-permute-start.2) | collective-permute-done | bytes 16416 | tf_op jit(solution)/shard_map/cond/branch_0_fun/ppermute | solution.py:376
  (34 shorter events, 5.9 us)
Async XLA Ops:
  1.6 38.8 %collective-permute-start.13 = (bf16[3088,128]{1,0:T(8,128)(2,1)S(1)}, bf16[3088,128]{1,0:T(8,128)(2,1)S(1)}, u32[]{:S(2)}, u32[]{:S(2)}) collective-permute-start(bf16[3088,128]{1,0:T(8,128)(2,1)S(1)} %pack.1.refs_0_), channel_id=1, source_target_pairs={{0,4},{1,5},{2,6},{3,7},{4,0},{5,1},{6,2},{7,3},{8,12},{9,13},{10,... | collective-permute-start | bytes 2371592 | tf_op jit(solution)/shard_map/ppermute | solution.py:376
  5.7 35.4 %collective-permute-start.5 = (bf16[3088,128]{1,0:T(8,128)(2,1)S(1)}, bf16[3088,128]{1,0:T(8,128)(2,1)S(1)}, u32[]{:S(2)}, u32[]{:S(2)}) collective-permute-start(bf16[3088,128]{1,0:T(8,128)(2,1)S(1)} %pack.1.refs_0_), channel_id=1, source_target_pairs={{0,8},{1,9},{2,10},{3,11},{4,12},{5,13},{6,14},{7,15},{8,0},{9,1},... | collective-permute-start | bytes 2371592 | tf_op jit(solution)/shard_map/ppermute | solution.py:376
  7.2 35.5 %collective-permute-start.17 = (bf16[3088,128]{1,0:T(8,128)(2,1)S(1)}, bf16[3088,128]{1,0:T(8,128)(2,1)S(1)}, u32[]{:S(2)}, u32[]{:S(2)}) collective-permute-start(bf16[3088,128]{1,0:T(8,128)(2,1)S(1)} %pack.1.refs_0_), channel_id=1, source_target_pairs={{0,2},{1,3},{2,0},{3,1},{4,6},{5,7},{6,4},{7,5},{8,10},{9,11},{10,... | collective-permute-start | bytes 2371592 | tf_op jit(solution)/shard_map/ppermute | solution.py:376
  8.8 34.4 %collective-permute-start.6 = (bf16[3088,128]{1,0:T(8,128)(2,1)S(1)}, bf16[3088,128]{1,0:T(8,128)(2,1)S(1)}, u32[]{:S(2)}, u32[]{:S(2)}) collective-permute-start(bf16[3088,128]{1,0:T(8,128)(2,1)S(1)} %pack.1.refs_0_), channel_id=1, source_target_pairs={{0,16},{1,17},{2,18},{3,19},{4,20},{5,21},{6,22},{7,23},{8,24},{9,... | collective-permute-start | bytes 2371592 | tf_op jit(solution)/shard_map/ppermute | solution.py:376
  40.4 18.7 %collective-permute-start.14 = (bf16[3088,128]{1,0:T(8,128)(2,1)S(1)}, bf16[3088,128]{1,0:T(8,128)(2,1)S(1)}, u32[]{:S(2)}, u32[]{:S(2)}) collective-permute-start(bf16[3088,128]{1,0:T(8,128)(2,1)S(1)} %collective-permute-done.13.refs_0_), channel_id=1, source_target_pairs={{0,2},{1,3},{2,0},{3,1},{4,6},{5,7},{6,4},{7,5},{8,10},{9,11},{10,... | collective-permute-start | bytes 2371592 | tf_op jit(solution)/shard_map/ppermute | solution.py:376
  41.1 10.8 %collective-permute-start.7 = (bf16[1536,128]{1,0:T(8,128)(2,1)S(1)}, bf16[1536,128]{1,0:T(8,128)(2,1)S(1)}, u32[]{:S(2)}, u32[]{:S(2)}) collective-permute-start(bf16[1536,128]{1,0:T(8,128)(2,1)S(1)} %slice.8), channel_id=1, source_target_pairs={{0,16},{1,17},{2,18},{3,19},{4,20},{5,21},{6,22},{7,23},{8,24},{9,... | collective-permute-start | bytes 1179656 | tf_op jit(solution)/shard_map/ppermute | solution.py:376
  42.7 21.6 %collective-permute-start.19 = (bf16[3088,128]{1,0:T(8,128)(2,1)S(1)}, bf16[3088,128]{1,0:T(8,128)(2,1)S(1)}, u32[]{:S(2)}, u32[]{:S(2)}) collective-permute-start(bf16[3088,128]{1,0:T(8,128)(2,1)S(1)} %pack.1.refs_0_), channel_id=1, source_target_pairs={{0,1},{1,0},{2,3},{3,2},{4,5},{5,4},{6,7},{7,6},{8,9},{9,8},{10,11... | collective-permute-start | bytes 2371592 | tf_op jit(solution)/shard_map/ppermute | solution.py:376
  42.7 32.2 %collective-permute-start.18 = (bf16[3088,128]{1,0:T(8,128)(2,1)S(1)}, bf16[3088,128]{1,0:T(8,128)(2,1)S(1)}, u32[]{:S(2)}, u32[]{:S(2)}) collective-permute-start(bf16[3088,128]{1,0:T(8,128)(2,1)S(1)} %collective-permute-done.17.refs_0_), channel_id=1, source_target_pairs={{0,1},{1,0},{2,3},{3,2},{4,5},{5,4},{6,7},{7,6},{8,9},{9,8},{10,11... | collective-permute-start | bytes 2371592 | tf_op jit(solution)/shard_map/ppermute | solution.py:376
  43.2 15.9 %collective-permute-start.8 = (bf16[1552,128]{1,0:T(8,128)(2,1)S(1)}, bf16[1552,128]{1,0:T(8,128)(2,1)S(1)}, u32[]{:S(2)}, u32[]{:S(2)}) collective-permute-start(bf16[1552,128]{1,0:T(8,128)(2,1)S(1)} %slice.9), channel_id=1, source_target_pairs={{0,8},{1,9},{2,10},{3,11},{4,12},{5,13},{6,14},{7,15},{8,0},{9,1},... | collective-permute-start | bytes 1191944 | tf_op jit(solution)/shard_map/ppermute | solution.py:376
  51.9 25.3 %collective-permute-start.16 = (bf16[3088,128]{1,0:T(8,128)(2,1)S(1)}, bf16[3088,128]{1,0:T(8,128)(2,1)S(1)}, u32[]{:S(2)}, u32[]{:S(2)}) collective-permute-start(bf16[3088,128]{1,0:T(8,128)(2,1)S(1)} %collective-permute-done.13.refs_0_), channel_id=1, source_target_pairs={{0,1},{1,0},{2,3},{3,2},{4,5},{5,4},{6,7},{7,6},{8,9},{9,8},{10,11... | collective-permute-start | bytes 2371592 | tf_op jit(solution)/shard_map/ppermute | solution.py:376
  59.1 22.1 %collective-permute-start.15 = (bf16[3088,128]{1,0:T(8,128)(2,1)S(1)}, bf16[3088,128]{1,0:T(8,128)(2,1)S(1)}, u32[]{:S(2)}, u32[]{:S(2)}) collective-permute-start(bf16[3088,128]{1,0:T(8,128)(2,1)S(1)} %collective-permute-done.14.refs_0_), channel_id=1, source_target_pairs={{0,1},{1,0},{2,3},{3,2},{4,5},{5,4},{6,7},{7,6},{8,9},{9,8},{10,11... | collective-permute-start | bytes 2371592 | tf_op jit(solution)/shard_map/ppermute | solution.py:376
  61.4 1.4 %collective-permute-start.9 = (f32[8,128]{1,0:T(8,128)S(1)}, f32[8,128]{1,0:T(8,128)S(1)}, u32[]{:S(2)}, u32[]{:S(2)}) collective-permute-start(f32[8,128]{1,0:T(8,128)S(1)} %get-tuple-element.285), channel_id=1, source_target_pairs={{0,1},{1,0},{2,3},{3,2},{4,5},{5,4},{6,7},{7,6},{8,9},{9,8},{10,11... | collective-permute-start | bytes 12296 | tf_op jit(solution)/shard_map/ppermute | solution.py:376
  62.8 4.9 %collective-permute-start.10 = (f32[16,128]{1,0:T(8,128)S(1)}, f32[16,128]{1,0:T(8,128)S(1)}, u32[]{:S(2)}, u32[]{:S(2)}) collective-permute-start(f32[16,128]{1,0:T(8,128)S(1)} %constant_dynamic-update-slice_fusion.1.refs_0_), channel_id=1, source_target_pairs={{0,2},{1,3},{2,0},{3,1},{4,6},{5,7},{6,4},{7,5},{8,10},{9,11},{10,... | collective-permute-start | bytes 24584 | tf_op jit(solution)/shard_map/ppermute | solution.py:376
  64.2 8.7 %collective-permute-start.11 = (f32[16,128]{1,0:T(8,128)S(1)}, f32[16,128]{1,0:T(8,128)S(1)}, u32[]{:S(2)}, u32[]{:S(2)}) collective-permute-start(f32[16,128]{1,0:T(8,128)S(1)} %constant_dynamic-update-slice_fusion.1.refs_0_), channel_id=1, source_target_pairs={{0,4},{1,5},{2,6},{3,7},{4,0},{5,1},{6,2},{7,3},{8,12},{9,13},{10,... | collective-permute-start | bytes 24584 | tf_op jit(solution)/shard_map/ppermute | solution.py:376
  67.6 5.4 %collective-permute-start.12 = (f32[16,128]{1,0:T(8,128)S(1)}, f32[16,128]{1,0:T(8,128)S(1)}, u32[]{:S(2)}, u32[]{:S(2)}) collective-permute-start(f32[16,128]{1,0:T(8,128)S(1)} %constant_dynamic-update-slice_fusion.1.refs_0_), channel_id=1, source_target_pairs={{0,6},{1,7},{2,4},{3,5},{4,2},{5,3},{6,0},{7,1},{8,14},{9,15},{10,... | collective-permute-start | bytes 24584 | tf_op jit(solution)/shard_map/ppermute | solution.py:376
  70.7 2.4 %copy-start.2 = (s32[512]{0:T(512)S(1)}, s32[512]{0:T(512)}, u32[]{:S(2)}) copy-start(s32[512]{0:T(512)} %param.13) | copy-start | bytes 6148
  79.6 1.7 %copy-start.1 = (bf16[1024,512]{1,0:T(8,128)(2,1)S(1)}, bf16[1024,512]{1,0:T(8,128)(2,1)}, u32[]{:S(2)}) copy-start(bf16[1024,512]{1,0:T(8,128)(2,1)} %block_ref.1) | copy-start | bytes 3145732
  79.6 1.7 %copy-start.3 = (s32[8,4]{0,1:T(4,128)S(1)}, s32[8,4]{0,1:T(4,128)}, u32[]{:S(2)}) copy-start(s32[8,4]{0,1:T(4,128)} %param.12) | copy-start | bytes 388
  79.6 1.7 %copy-start.4 = (s32[8,4]{0,1:T(4,128)S(1)}, s32[8,4]{0,1:T(4,128)}, u32[]{:S(2)}) copy-start(s32[8,4]{0,1:T(4,128)} %param.11) | copy-start | bytes 388
  83.5 3.8 %collective-permute-start = (f32[8,512]{1,0:T(8,128)S(1)}, f32[8,512]{1,0:T(8,128)S(1)}, u32[]{:S(2)}, u32[]{:S(2)}) collective-permute-start(f32[8,512]{1,0:T(8,128)S(1)} %get-tuple-element.263.refs_0_), channel_id=1, source_target_pairs={{0,8},{1,9},{2,10},{3,11},{4,12},{5,13},{6,14},{7,15},{8,0},{9,1},... | collective-permute-start | bytes 49160 | tf_op jit(solution)/shard_map/cond/branch_0_fun/ppermute | solution.py:376
  85.0 3.7 %collective-permute-start.1 = (f32[8,512]{1,0:T(8,128)S(1)}, f32[8,512]{1,0:T(8,128)S(1)}, u32[]{:S(2)}, u32[]{:S(2)}) collective-permute-start(f32[8,512]{1,0:T(8,128)S(1)} %get-tuple-element.263.refs_0_), channel_id=1, source_target_pairs={{0,16},{1,17},{2,18},{3,19},{4,20},{5,21},{6,22},{7,23},{8,24},{9,... | collective-permute-start | bytes 49160 | tf_op jit(solution)/shard_map/cond/branch_0_fun/ppermute | solution.py:376
  86.5 4.6 %collective-permute-start.2 = (f32[8,512]{1,0:T(8,128)S(1)}, f32[8,512]{1,0:T(8,128)S(1)}, u32[]{:S(2)}, u32[]{:S(2)}) collective-permute-start(f32[8,512]{1,0:T(8,128)S(1)} %get-tuple-element.263.refs_0_), channel_id=1, source_target_pairs={{0,24},{1,25},{2,26},{3,27},{4,28},{5,29},{6,30},{7,31},{8,16},{9,... | collective-permute-start | bytes 49160 | tf_op jit(solution)/shard_map/cond/branch_0_fun/ppermute | solution.py:376

commit v3 on v2

v3 whole, which is shorter than its diff:
```python
import functools

import jax
import jax.numpy as jnp
from jax import lax
from jax.experimental import pallas as pl
from jax.experimental.pallas import tpu as pltpu
from jax.sharding import PartitionSpec as P

TB = 128
PAD = 16
AXES = ("row", "col")
F32, BF16, I32 = jnp.float32, jnp.bfloat16, jnp.int32
VMEM = pl.BlockSpec(memory_space=pltpu.VMEM)
SMEM = pl.BlockSpec(memory_space=pltpu.SMEM)


def params(mib):
    return pltpu.CompilerParams(vmem_limit_bytes=mib * 1024 * 1024)


def cost(flops, moved):
    return pl.CostEstimate(flops=int(flops), bytes_accessed=int(moved), transcendentals=0)


def tiles_of(shape):
    return shape[0] // TB, shape[1] // TB


def place():
    col = lax.axis_index("col")
    return lax.axis_index("row"), col // 2, col % 2


def table_of(ref):
    end = ref.shape[0]
    return ref[end - PAD : end, :].astype(F32).astype(I32)[0:1, :]


def pack_kernel(mask_ref, block_ref, out_ref, head_ref):
    ti, tj = tiles_of(block_ref.shape)
    slots, first = (out_ref.shape[0] - PAD) // TB, (head_ref.shape[0] - PAD) // TB
    lane = lax.broadcasted_iota(I32, (PAD, TB), 1)
    table = jnp.full((PAD, TB), -1, I32)
    used = jnp.int32(0)
    for i in range(ti):
        for j in range(tj):
            stored = mask_ref[j, i]

            @pl.when(jnp.logical_and(stored > 0, used < slots))
            def _(i=i, j=j, used=used):
                tile = block_ref[i * TB : (i + 1) * TB, j * TB : (j + 1) * TB]
                here = pl.ds(pl.multiple_of(used * TB, TB), TB)
                out_ref[here, :] = tile

                @pl.when(used < first)
                def _():
                    head_ref[here, :] = tile

            table = jnp.where(lane == i * tj + j, jnp.where(stored > 0, used, -1), table)
            used = used + stored
    table = jnp.where(lane == ti * tj, used, table).astype(F32).astype(BF16)
    out_ref[slots * TB :, :] = table
    head_ref[first * TB :, :] = table


def pack(block, mask_t, slots, first):
    return pl.pallas_call(
        pack_kernel,
        out_shape=tuple(jax.ShapeDtypeStruct((n * TB + PAD, TB), BF16) for n in (slots, first)),
        in_specs=[SMEM, VMEM],
        out_specs=(VMEM, VMEM),
        compiler_params=params(8),
        cost_estimate=cost(1e6, 2 * block.size * 2),
        name="pack",
    )(mask_t, block)


def load(ref, at, count):
    return ref[pl.ds(pl.multiple_of(jnp.clip(at, 0, count - 1) * TB, TB), TB), :]


def pool_kernel(first, mask_ref, block_ref, own_ref, other_ref, out_ref, msg_ref):
    ti, tj = tiles_of(block_ref.shape)
    slots, n = (own_ref.shape[0] - PAD) // TB, out_ref.shape[0] // TB
    core = place()[2]
    count = jnp.int32(0)
    sums = [jnp.zeros((8, TB), F32) for _ in range(tj)]
    for i in range(ti):
        for j in range(tj):
            stored = mask_ref[j, i]
            count = count + stored
            tile = block_ref[i * TB : (i + 1) * TB, j * TB : (j + 1) * TB].astype(F32)
            sums[j] += jnp.sum(tile.reshape(TB // 8, 8, TB), axis=0) * stored.astype(F32)
    lane = lax.broadcasted_iota(I32, (1, TB), 1)
    theirs = jnp.max(jnp.where(lane == ti * tj, table_of(other_ref), 0))
    left = jnp.maximum(count - first, 0)
    left_other = jnp.maximum(theirs - first, 0)
    left_0 = jnp.where(core == 0, left, left_other)
    for i in range(n):
        p = core * n + i
        in_0 = p < left_0
        at = first + jnp.where(in_0, p, p - left_0)
        mine = jnp.where(in_0, 0, 1) == core
        tile = jnp.where(mine, load(own_ref, at, slots), load(other_ref, at, slots))
        out_ref[i * TB : (i + 1) * TB, :] = tile
    over = jnp.logical_or(count > slots, left + left_other > 2 * n)
    msg_ref[...] = jnp.zeros_like(msg_ref)
    for j in range(tj):
        msg_ref[j : j + 1, :] = jnp.sum(sums[j], axis=0, keepdims=True)
    msg_ref[tj : tj + 1, :] = jnp.full((1, TB), 1.0, F32) * jnp.where(over, 1.0, 0.0)


def pool(block, mask_t, own, other, first, n):
    s_rows = -(-(block.shape[1] // TB + 1) // 8) * 8
    return pl.pallas_call(
        functools.partial(pool_kernel, first),
        out_shape=(
            jax.ShapeDtypeStruct((n * TB, TB), BF16),
            jax.ShapeDtypeStruct((s_rows, TB), F32),
        ),
        in_specs=[SMEM] + [VMEM] * 3,
        out_specs=(VMEM, VMEM),
        compiler_params=params(8),
        cost_estimate=cost(1e6, 2 * block.size * 2),
        name="pool",
    )(mask_t, block, own, other)


def read_tables(refs, itab, stab, sem):
    for q, ref in enumerate(refs):
        itab[q : q + 1, :] = table_of(ref)
    copy = pltpu.make_async_copy(itab, stab, sem)
    copy.start()
    copy.wait()


def zero_tile():
    return jnp.zeros((TB, TB), BF16)


def whole_tile(parts, slots, at):
    first = parts[0].shape[0] // TB if len(parts) == 2 else slots
    tile = load(parts[0], at, first)
    if len(parts) == 2:
        tile = jnp.where(at >= first, load(parts[1], at - first, slots - first), tile)
    return jnp.where(at >= 0, tile, zero_tile())


def table_scratch(n):
    n8 = -(-n // 8) * 8
    return [pltpu.VMEM((n8, TB), I32), pltpu.SMEM((n8, TB), I32), pltpu.SemaphoreType.DMA]


def regroup(refs, sizes):
    out = []
    for s in sizes:
        out.append(refs[:s])
        refs = refs[s:]
    return out


def panel_kernel(slots, sizes, rows, *refs):
    blocks = regroup(refs, sizes)
    panel_ref, itab, stab, sem = refs[sum(sizes) :]
    cols = panel_ref.shape[1]
    ti, tj = rows // TB, cols // TB
    me = place()[0]
    read_tables([b[-1] for b in blocks], itab, stab, sem)
    for q in range(len(sizes)):
        base = (me ^ q) * rows

        def strip(i, done, q=q, base=base):
            for j in range(tj):
                tile = whole_tile(blocks[q], slots, stab[q, i * tj + j])
                panel_ref[pl.ds(pl.multiple_of(base + i * TB, TB), TB), j * TB : (j + 1) * TB] = tile
            return done

        lax.fori_loop(0, ti, strip, 0, unroll=2)


def panel(payloads, slots, rows, cols):
    n = len(payloads)
    sizes = [len(p) for p in payloads]
    return pl.pallas_call(
        functools.partial(panel_kernel, slots, sizes, rows),
        out_shape=jax.ShapeDtypeStruct((n * rows, cols), BF16),
        in_specs=[VMEM] * sum(sizes),
        out_specs=VMEM,
        scratch_shapes=table_scratch(n),
        compiler_params=params(20),
        cost_estimate=cost(1e7, 2 * n * rows * cols * 2),
        name="panel",
    )(*[x for p in payloads for x in p])


def strip_rows(rows):
    return min(rows, 256)


def tile_getters(kind, refs, stab, tiles, core):
    if kind == "whole":
        slots = (refs[0].shape[0] - PAD) // TB
        return [lambda at, r=r: whole_tile([r], slots, at) for r in refs]
    first = (refs[0].shape[0] - PAD) // TB
    if kind == "heads":
        return [
            lambda at, r=r: jnp.where(
                jnp.logical_and(at >= 0, at < first), load(r, at, first), zero_tile()
            )
            for r in refs
        ]
    n = refs[2].shape[0] // TB
    left = [jnp.maximum(stab[b, tiles] - first, 0) for b in range(2)]
    left_0 = jnp.where(core == 0, left[0], left[1])

    def getter(side):
        base = jnp.where((core ^ side) == 1, left_0, 0) - first

        def get(at):
            p = at + base
            part = jnp.where(p >= n, 1, 0)
            local = p - part * n
            rest = jnp.where(part == core, load(refs[2], local, n), load(refs[3], local, n))
            if kind == "pools":
                return jnp.where(at >= first, rest, zero_tile())
            tile = jnp.where(at >= first, rest, load(refs[side], at, first))
            return jnp.where(at >= 0, tile, zero_tile())

        return get

    return [getter(0), getter(1)]


def products(kind, refs, pair, panel_ref, itab, stab, sem, lhs, rows, use):
    cols = panel_ref.shape[1]
    step = strip_rows(rows)
    tj = cols // TB
    _, z, core = place()
    read_tables(refs[:2], itab, stab, sem)
    getters = tile_getters(kind, refs, stab, rows // TB * tj, core)
    n = rows // step
    start = (refs[0].shape[0] - PAD) // TB // tj * TB // step if kind == "pools" else 0

    def unpack(m):
        for b, get in enumerate(getters):
            for a in range(step // TB):
                for j in range(tj):
                    tile = get(stab[b, (m * (step // TB) + a) * tj + j])
                    lhs[m % 2, a * TB : (a + 1) * TB, b * cols + j * TB : b * cols + (j + 1) * TB] = tile

    unpack(start)
    for m in range(start):
        use(m, None)
    for m in range(start, n):
        if m + 1 < n:
            unpack(m + 1)
        total = None
        for b in range(2):
            at = pl.multiple_of((z ^ pair) * 2 * cols + (core ^ b) * cols, TB)
            got = jnp.dot(
                lhs[m % 2, :, b * cols : (b + 1) * cols],
                panel_ref[pl.ds(at, cols), :],
                preferred_element_type=F32,
            )
            total = got if total is None else total + got
        use(m, total)


def dot_kernel(kind, n, pair, rows, has_prior, *refs):
    panel_ref = refs[n]
    prior_ref = refs[n + 1] if has_prior else None
    acc_ref, itab, stab, sem, lhs = refs[n + 1 + has_prior :]
    step = strip_rows(rows)

    def use(m, got):
        here = slice(m * step, (m + 1) * step)
        acc_ref[here, :] = prior_ref[here, :] + got if has_prior else got

    products(kind, refs[:n], pair, panel_ref, itab, stab, sem, lhs, rows, use)


def dot_scratch(rows, cols):
    return table_scratch(2) + [pltpu.VMEM((2, strip_rows(rows), 2 * cols), BF16)]


def dots(kind, payloads, pair, dense, prior, rows):
    cols = dense.shape[1]
    n = len(payloads)
    extra = [] if prior is None else [prior]
    return pl.pallas_call(
        functools.partial(dot_kernel, kind, n, pair, rows, len(extra)),
        out_shape=jax.ShapeDtypeStruct((rows, cols), F32),
        in_specs=[VMEM] * (n + 1 + len(extra)),
        out_specs=VMEM,
        scratch_shapes=dot_scratch(rows, cols),
        input_output_aliases={n + 1: 0} if extra else {},
        compiler_params=params(20),
        cost_estimate=cost(4 * rows * cols * cols, 12 * rows * cols),
        name="dots",
    )(*payloads, dense, *extra)


def means_kernel(n_pairs, s_rows, order, *refs):
    msgs, (thr_ref, panel_ref, out_ref, flag_ref) = refs[:n_pairs], refs[n_pairs:]
    _, z, core = place()
    cols = panel_ref.shape[1]
    tj = cols // TB
    total = jnp.zeros((8, cols), F32)
    row = lax.broadcasted_iota(I32, (8, TB), 0)
    over = jnp.zeros((1, TB), F32)
    for q in range(n_pairs):
        for b in range(2):
            over = jnp.maximum(over, msgs[q][b * s_rows + tj : b * s_rows + tj + 1, :])
            for t in range(tj):
                s = jnp.broadcast_to(msgs[q][b * s_rows + t : b * s_rows + t + 1, :], (8, TB))
                high = s.astype(BF16).astype(F32)
                mid = (s - high).astype(BF16).astype(F32)
                low = s - high - mid
                lhs = jnp.where(row == 0, high, jnp.where(row == 1, mid, jnp.where(row == 2, low, 0.0)))
                at = (z ^ q) * 2 * cols + (core ^ b) * cols + t * TB
                total += jnp.dot(
                    lhs.astype(BF16),
                    panel_ref[pl.ds(pl.multiple_of(at, TB), TB), :],
                    preferred_element_type=F32,
                )
    mean = jnp.sum(total, axis=0, keepdims=True) / order
    out_ref[...] = jnp.broadcast_to(0.125 * thr_ref[...].astype(F32) * mean, out_ref.shape)
    flag_ref[0] = jnp.where(jnp.max(over) > 0.0, 1, 0).astype(I32)


def cuts_of(messages, thr, dense, s_rows, order):
    n = len(messages)
    cols = dense.shape[1]
    return pl.pallas_call(
        functools.partial(means_kernel, n, s_rows, order),
        out_shape=(jax.ShapeDtypeStruct((8, cols), F32), jax.ShapeDtypeStruct((1,), I32)),
        in_specs=[VMEM] * (n + 2),
        out_specs=(VMEM, SMEM),
        compiler_params=params(12),
        cost_estimate=cost(1e7, dense.size * 2),
        name="cuts",
    )(*messages, thr, dense)


def last_kernel(kind, n, pair, rows, keep_ref, *refs):
    panel_ref, prior_ref, cut_ref, acc_ref, tot_ref, itab, stab, sem, lhs = refs[n:]
    step = strip_rows(rows)
    cols = panel_ref.shape[1]
    per = step // TB
    totals = [jnp.zeros((8, TB), F32) for _ in range(cols // TB)]

    def use(m, got):
        prior = prior_ref[m * step : (m + 1) * step, :]
        got = jnp.maximum((prior if got is None else prior + got) - cut_ref[0:1, :], 0.0)
        for a in range(per):
            at = (m * per + a) * TB
            for j in range(cols // TB):
                kept = keep_ref[j, m * per + a].astype(F32)
                cell = got[a * TB : (a + 1) * TB, j * TB : (j + 1) * TB] * kept
                acc_ref[at : at + TB, j * TB : (j + 1) * TB] = cell
                totals[j] += jnp.sum(cell.reshape(TB // 8, 8, TB), axis=0)

    products(kind, refs[:n], pair, panel_ref, itab, stab, sem, lhs, rows, use)
    for j, t in enumerate(totals):
        tot_ref[:, j * TB : (j + 1) * TB] = jnp.sum(t, axis=0, keepdims=True)


def finish(kind, keep_t, payloads, pair, dense, prior, cut, rows):
    cols = dense.shape[1]
    n = len(payloads)
    return pl.pallas_call(
        functools.partial(last_kernel, kind, n, pair, rows),
        out_shape=(jax.ShapeDtypeStruct((rows, cols), F32), jax.ShapeDtypeStruct((1, cols), F32)),
        in_specs=[SMEM] + [VMEM] * (n + 3),
        out_specs=(VMEM, VMEM),
        scratch_shapes=dot_scratch(rows, cols),
        compiler_params=params(20),
        cost_estimate=cost(4 * rows * cols * cols, 12 * rows * cols),
        name="finish",
    )(keep_t, *payloads, dense, prior, cut)


def scale_kernel(n, order, x_ref, *refs):
    tots, out_ref = refs[:n], refs[n]
    total = tots[0][...]
    for t in tots[1:]:
        total = total + t[...]
    total = total / order
    factor = 1.0 / jnp.maximum(total, 0.1)
    out_ref[...] = (x_ref[...] * factor).astype(BF16)


def scale(x, totals, order):
    n = len(totals)
    return pl.pallas_call(
        functools.partial(scale_kernel, n, order),
        out_shape=jax.ShapeDtypeStruct(x.shape, BF16),
        in_specs=[VMEM] * (n + 1),
        out_specs=VMEM,
        compiler_params=params(12),
        cost_estimate=cost(2 * x.size, 6 * x.size),
        name="scale",
    )(x, *totals)


def dense_path(values, tile_mask, keep_mask, thr_index, n_row, n_col):
    rows, cols = values.shape
    ti, tj = tiles_of(values.shape)
    matrix = (
        values.reshape(ti, TB, tj, TB) * tile_mask[:, None, :, None].astype(BF16)
    ).reshape(rows, cols)
    kept = jnp.broadcast_to(keep_mask[:, None, :, None].astype(F32), (ti, TB, tj, TB)).reshape(rows, cols)
    r, c = lax.axis_index("row"), lax.axis_index("col")
    order = rows * n_row

    def col_ring(i, carry):
        block, panel_ = carry
        panel_ = lax.dynamic_update_slice(panel_, block, (((r - i) % n_row) * rows, 0))
        return lax.ppermute(block, "row", [(k, (k + 1) % n_row) for k in range(n_row)]), panel_

    _, panel_ = lax.fori_loop(0, n_row, col_ring, (matrix, jnp.zeros((order, cols), BF16)))

    def row_ring(i, carry):
        block, acc = carry
        part = lax.dynamic_slice(panel_, (((c - i) % n_col) * cols, 0), (cols, cols))
        acc = acc + jnp.dot(block, part, preferred_element_type=F32)
        return lax.ppermute(block, "col", [(k, (k + 1) % n_col) for k in range(n_col)]), acc

    _, product = lax.fori_loop(0, n_col, row_ring, (matrix, jnp.zeros((rows, cols), F32)))
    means = lax.psum(jnp.sum(product, axis=0), "row") / order
    pruned = jnp.maximum(product - 0.125 * thr_index.astype(F32) * means, 0.0) * kept
    totals = lax.psum(jnp.sum(pruned, axis=0), "row") / order
    return (pruned / jnp.maximum(totals, 0.1)).astype(BF16)


def on_device(values, tile_mask, keep_mask, thr_index, n_row, n_col):
    return body(values, tile_mask, keep_mask, thr_index, n_row, n_col)


def body(values, tile_mask, keep_mask, thr_index, n_row, n_col):
    rows, cols = values.shape
    ti, tj = tiles_of(values.shape)
    first = ti * tj // 2
    extra = ti * tj * 3 // 16
    slots = ti * tj * 13 // 16
    half = slots // 2 * TB
    n_z = n_col // 2
    last = n_z - 1
    order = rows * n_row

    def send(x, dr=0, dz=0, dc=0):
        pairs = [
            (r * n_col + z * 2 + c, (r ^ dr) * n_col + (z ^ dz) * 2 + (c ^ dc))
            for r in range(n_row)
            for z in range(n_z)
            for c in range(2)
        ]
        return lax.ppermute(x, AXES, pairs)

    own, head = pack(values, tile_mask.T, slots, first)
    own_swapped = send(own, dc=1)
    spare, sums = pool(values, tile_mask.T, own, own_swapped, first, extra)

    line = {0: [head, spare]}
    swapped = {}
    for j in range(1, n_z):
        low = j & -j
        line[j] = [send(x, dz=low) for x in line[j ^ low]]
        swapped[j] = [send(x, dc=1) for x in line[j]]

    column = {0: [own]}
    for q in range(1, n_row):
        low = q & -q
        rest = q ^ low
        if rest and rest & -rest == rest:
            column[q] = [send(column[low][0][:half], dr=rest), send(column[rest][0][half:], dr=low)]
        else:
            column[q] = [send(own, dr=q)]

    dense = panel([column[q] for q in range(n_row)], slots, rows, cols)

    sums = functools.reduce(jnp.add, [send(sums, dr=q) for q in range(1, n_row)], sums)
    both = jnp.concatenate([sums, send(sums, dc=1)], axis=0)
    messages = [both] + [send(both, dz=j) for j in range(1, n_z)]
    cut, over = cuts_of(messages, thr_index.reshape(1, cols), dense, sums.shape[0], order)

    acc = None
    for j in range(n_z):
        if j == 0:
            acc = dots("whole", [own, own_swapped], j, dense, acc, rows)
        elif j < last:
            parts = [line[j][0], swapped[j][0], line[j][1], swapped[j][1]]
            acc = dots("all", parts, j, dense, acc, rows)
        else:
            acc = dots("heads", [line[j][0], swapped[j][0]], j, dense, acc, rows)

    def fast():
        parts = [line[last][0], swapped[last][0], line[last][1], swapped[last][1]]
        pruned, tot = finish("pools", keep_mask.T, parts, last, dense, acc, cut, rows)
        totals = [tot] + [send(tot, dr=q) for q in range(1, n_row)]
        return scale(pruned, totals, order)

    def full():
        return dense_path(values, tile_mask, keep_mask, thr_index, n_row, n_col)

    return lax.cond(over[0] > 0, full, fast)


def solution(mesh):
    n_row, n_col = mesh.shape["row"], mesh.shape["col"]
    return jax.shard_map(
        functools.partial(on_device, n_row=n_row, n_col=n_col),
        mesh=mesh,
        in_specs=(P("row", "col"), P("row", "col"), P("row", "col"), P("col")),
        out_specs=P("row", "col"),
        check_vma=False,
    )
```

time: 92.4 us -> 93.9 us (1.016)
  waiting for transfers between devices: 49.6 us -> 42.6 us
  starting transfers between devices: 25 us -> 29.8 us
  Pallas kernels: 16.7 us -> 20.2 us
    ppermute x18 -> x27, waiting for transfers between devices: 49.6 us -> 42.6 us  [send(): return lax.ppermute(x, AXES, pairs)]
    ppermute x18 -> x27, starting transfers between devices: 25 us -> 29.8 us  [send(): return lax.ppermute(x, AXES, pairs)]
    pallas_call x6 -> x7, Pallas kernels: 12.3 us -> 15.8 us  [the longest x4 10.3 us: dots(): pl.pallas_call(functools.partial(dot_kernel, kind, n, pair, rows, len(ext...]
  transfers between devices with their start and end apart: 18 -> 27, of which waited for: 8 -> 11; matrix products, arithmetic and copies ran while one was open for 0% -> 0% of each run, Pallas kernels for 13% -> 16%
where the time goes in v3:
time: 93.9 us; the launch traced here: 93.7 us
  waiting for transfers between devices  42.6 us (45%)
  starting transfers between devices  29.8 us (32%)
  Pallas kernels  20.2 us (22%)
    ppermute x27, waiting for transfers between devices, send(): return lax.ppermute(x, AXES, pairs)  42.6 us
    ppermute x27, starting transfers between devices, send(): return lax.ppermute(x, AXES, pairs)  29.8 us
    pallas_call x4, Pallas kernels, dots(): pl.pallas_call(functools.partial(dot_kernel, kind, n, pair, rows, len(ext...  10.3 us
    pallas_call x1, Pallas kernels, finish(): pl.pallas_call(functools.partial(last_kernel, kind, n, pair, rows), out_s...  2.31 us
    pallas_call x1, Pallas kernels, panel(): pl.pallas_call(functools.partial(panel_kernel, slots, sizes, rows), out_s...  2.19 us
  transfers between devices with their start and end apart: 27, of which 11 were waited for; matrix products, arithmetic and copies ran while one was open for 0% of the time, Pallas kernels for 16%

profile of v3, /device:TPU:0, one launch (start us, length us, event | category | flops | bytes accessed | tf_op | source)
XLA Modules:
  0.0 93.7 jit_solution(3178164091223171533)
XLA Ops:
  0.0 1.6 %pack.1 = (bf16[3344,128]{1,0:T(8,128)(2,1)S(1)}, bf16[2064,128]{1,0:T(8,128)(2,1)S(1)}) custom-call(s32[4,8]{1,0:T(4,128)} %bitcast.28, bf16[1024,512]{1,0:T(8,128)(2,1)} %block_ref.3), custom_call_target="tpu_custom_call" | custom-call | flops 1000000 | bytes 2097152 | tf_op jit(solution)/shard_map/pack/pallas_call | solution.py:68
  2.2 3.6 %collective-permute-start.17 = (bf16[2064,128]{1,0:T(8,128)(2,1)S(1)}, bf16[2064,128]{1,0:T(8,128)(2,1)S(1)}, u32[]{:S(2)}, u32[]{:S(2)}) collective-permute-start(bf16[2064,128]{1,0:T(8,128)(2,1)S(1)} %get-tuple-element.299), channel_id=1, source_target_pairs={{0,4},{1,5},{2,6},{3,7},{4,0},{5,1},{6,2},{7,3},{8,12},{9,13},{10,... | collective-permute-start | bytes 1585160 | tf_op jit(solution)/shard_map/ppermute | solution.py:459
  5.8 1.5 %collective-permute-start.14 = (bf16[3344,128]{1,0:T(8,128)(2,1)S(1)}, bf16[3344,128]{1,0:T(8,128)(2,1)S(1)}, u32[]{:S(2)}, u32[]{:S(2)}) collective-permute-start(bf16[3344,128]{1,0:T(8,128)(2,1)S(1)} %get-tuple-element.296.own_ref.refs_0_), channel_id=1, source_target_pairs={{0,16},{1,17},{2,18},{3,19},{4,20},{5,21},{6,22},{7,23},{8,24},{9,... | collective-permute-start | bytes 2568200 | tf_op jit(solution)/shard_map/ppermute | solution.py:459
  8.9 1.6 %collective-permute-start.25 = (bf16[2064,128]{1,0:T(8,128)(2,1)S(1)}, bf16[2064,128]{1,0:T(8,128)(2,1)S(1)}, u32[]{:S(2)}, u32[]{:S(2)}) collective-permute-start(bf16[2064,128]{1,0:T(8,128)(2,1)S(1)} %get-tuple-element.299), channel_id=1, source_target_pairs={{0,2},{1,3},{2,0},{3,1},{4,6},{5,7},{6,4},{7,5},{8,10},{9,11},{10,... | collective-permute-start | bytes 1585160 | tf_op jit(solution)/shard_map/ppermute | solution.py:459
  10.5 1.5 %pool.1 = (bf16[768,128]{1,0:T(8,128)(2,1)S(1)}, f32[8,128]{1,0:T(8,128)S(1)}) custom-call(s32[4,8]{1,0:T(4,128)} %bitcast.29, bf16[1024,512]{1,0:T(8,128)(2,1)} %block_ref.3, bf16[3344,128]{1,0:T(8,128)(2,1)S(1)} %get-tuple-element.296.own_ref.refs_0_, bf16[3344,128]{1,0:T(8,128)(2,1)S(1)} %collective-permute-done.5.other_ref.refs_1_), custom_call_target="tpu_custom_call" | custom-call | flops 1000000 | bytes 2097152 | tf_op jit(solution)/shard_map/pool/pallas_call | solution.py:116
  12.6 17.3 %collective-permute-done.17.refs_0_ = bf16[2064,128]{1,0:T(8,128)(2,1)S(1)} collective-permute-done((bf16[2064,128]{1,0:T(8,128)(2,1)S(1)}, bf16[2064,128]{1,0:T(8,128)(2,1)S(1)}, u32[]{:S(2)}, u32[]{:S(2)}) %collective-permute-start.17) | collective-permute-done | bytes 528416 | tf_op jit(solution)/shard_map/ppermute | solution.py:459
  29.9 1.6 %collective-permute-start.7 = (f32[8,128]{1,0:T(8,128)S(1)}, f32[8,128]{1,0:T(8,128)S(1)}, u32[]{:S(2)}, u32[]{:S(2)}) collective-permute-start(f32[8,128]{1,0:T(8,128)S(1)} %get-tuple-element.297), channel_id=1, source_target_pairs={{0,16},{1,17},{2,18},{3,19},{4,20},{5,21},{6,22},{7,23},{8,24},{9,... | collective-permute-start | bytes 12296 | tf_op jit(solution)/shard_map/ppermute | solution.py:459
  34.2 1.8 %collective-permute-done.8 = f32[8,128]{1,0:T(8,128)S(1)} collective-permute-done((f32[8,128]{1,0:T(8,128)S(1)}, f32[8,128]{1,0:T(8,128)S(1)}, u32[]{:S(2)}, u32[]{:S(2)}) %collective-permute-start.8) | collective-permute-done | bytes 4128 | tf_op jit(solution)/shard_map/ppermute | solution.py:459
  39.2 2.1 %collective-permute-start.11 = (f32[16,128]{1,0:T(8,128)S(1)}, f32[16,128]{1,0:T(8,128)S(1)}, u32[]{:S(2)}, u32[]{:S(2)}) collective-permute-start(f32[16,128]{1,0:T(8,128)S(1)} %pad_maximum_fusion.refs_0_), channel_id=1, source_target_pairs={{0,4},{1,5},{2,6},{3,7},{4,0},{5,1},{6,2},{7,3},{8,12},{9,13},{10,... | collective-permute-start | bytes 24584 | tf_op jit(solution)/shard_map/ppermute | solution.py:459
  42.7 8.2 %collective-permute-done.10.refs_1_ = f32[16,128]{1,0:T(8,128)S(1)} collective-permute-done((f32[16,128]{1,0:T(8,128)S(1)}, f32[16,128]{1,0:T(8,128)S(1)}, u32[]{:S(2)}, u32[]{:S(2)}) %collective-permute-start.10) | collective-permute-done | bytes 8224 | tf_op jit(solution)/shard_map/ppermute | solution.py:459
  52.8 2.0 %collective-permute-start.20 = (bf16[768,128]{1,0:T(8,128)(2,1)S(1)}, bf16[768,128]{1,0:T(8,128)(2,1)S(1)}, u32[]{:S(2)}, u32[]{:S(2)}) collective-permute-start(bf16[768,128]{1,0:T(8,128)(2,1)S(1)} %get-tuple-element.300), channel_id=1, source_target_pairs={{0,4},{1,5},{2,6},{3,7},{4,0},{5,1},{6,2},{7,3},{8,12},{9,13},{10,... | collective-permute-start | bytes 589832 | tf_op jit(solution)/shard_map/ppermute | solution.py:459
  54.8 1.5 %collective-permute-start.15 = (bf16[1664,128]{1,0:T(8,128)(2,1)S(1)}, bf16[1664,128]{1,0:T(8,128)(2,1)S(1)}, u32[]{:S(2)}, u32[]{:S(2)}) collective-permute-start(bf16[1664,128]{1,0:T(8,128)(2,1)S(1)} %slice.8), channel_id=1, source_target_pairs={{0,16},{1,17},{2,18},{3,19},{4,20},{5,21},{6,22},{7,23},{8,24},{9,... | collective-permute-start | bytes 1277960 | tf_op jit(solution)/shard_map/ppermute | solution.py:459
  56.4 7.9 %collective-permute-done.20.refs_2_ = bf16[768,128]{1,0:T(8,128)(2,1)S(1)} collective-permute-done((bf16[768,128]{1,0:T(8,128)(2,1)S(1)}, bf16[768,128]{1,0:T(8,128)(2,1)S(1)}, u32[]{:S(2)}, u32[]{:S(2)}) %collective-permute-start.20) | collective-permute-done | bytes 196640 | tf_op jit(solution)/shard_map/ppermute | solution.py:459
  64.8 1.8 %collective-permute-done.15.refs_3_ = bf16[1664,128]{1,0:T(8,128)(2,1)S(1)} collective-permute-done((bf16[1664,128]{1,0:T(8,128)(2,1)S(1)}, bf16[1664,128]{1,0:T(8,128)(2,1)S(1)}, u32[]{:S(2)}, u32[]{:S(2)}) %collective-permute-start.15) | collective-permute-done | bytes 426016 | tf_op jit(solution)/shard_map/ppermute | solution.py:459
  66.6 1.9 %collective-permute-start.21 = (bf16[768,128]{1,0:T(8,128)(2,1)S(1)}, bf16[768,128]{1,0:T(8,128)(2,1)S(1)}, u32[]{:S(2)}, u32[]{:S(2)}) collective-permute-start(bf16[768,128]{1,0:T(8,128)(2,1)S(1)} %collective-permute-done.20.refs_2_), channel_id=1, source_target_pairs={{0,2},{1,3},{2,0},{3,1},{4,6},{5,7},{6,4},{7,5},{8,10},{9,11},{10,... | collective-permute-start | bytes 589832 | tf_op jit(solution)/shard_map/ppermute | solution.py:459
  68.5 2.2 %panel.1.refs_5_.refs_2_.refs_4_ = bf16[4096,512]{1,0:T(8,128)(2,1)S(1)} custom-call(bf16[3344,128]{1,0:T(8,128)(2,1)S(1)} %get-tuple-element.296.own_ref.refs_0_, bf16[3344,128]{1,0:T(8,128)(2,1)S(1)} %collective-permute-done.13.refs_1_, bf16[3344,128]{1,0:T(8,128)(2,1)S(1)} %collective-permute-done.14.refs_2_, ...), custom_call_target="tpu_custom_call" | custom-call | flops 10000000 | bytes 8388608 | tf_op jit(solution)/shard_map/panel/pallas_call | solution.py:185
  73.1 2.1 %dots.4.refs_5_ = f32[1024,512]{1,0:T(8,128)S(1)} custom-call(bf16[3344,128]{1,0:T(8,128)(2,1)S(1)} %get-tuple-element.296.own_ref.refs_0_, bf16[3344,128]{1,0:T(8,128)(2,1)S(1)} %collective-permute-done.5.other_ref.refs_1_, bf16[4096,512]{1,0:T(8,128)(2,1)S(1)} %panel.1.refs_5_.refs_2_.refs_4_), custom_call_target="tpu_custom_call" | custom-call | flops 1073741824 | bytes 6291456 | tf_op jit(solution)/shard_map/dots/pallas_call | solution.py:291
  75.3 3.0 %dots.5.refs_5_ = f32[1024,512]{1,0:T(8,128)S(1)} custom-call(bf16[2064,128]{1,0:T(8,128)(2,1)S(1)} %collective-permute-done.25.refs_0_, bf16[2064,128]{1,0:T(8,128)(2,1)S(1)} %collective-permute-done.26.refs_1_, bf16[768,128]{1,0:T(8,128)(2,1)S(1)} %collective-permute-done.27.refs_2_, ...), custom_call_target="tpu_custom_call", output_to_operand_aliasing={{}: (5, {})} | custom-call | flops 1073741824 | bytes 6291456 | tf_op jit(solution)/shard_map/dots/pallas_call | solution.py:291
  78.3 3.0 %dots.6.refs_3_ = f32[1024,512]{1,0:T(8,128)S(1)} custom-call(bf16[2064,128]{1,0:T(8,128)(2,1)S(1)} %collective-permute-done.17.refs_0_, bf16[2064,128]{1,0:T(8,128)(2,1)S(1)} %collective-permute-done.23.refs_1_, bf16[768,128]{1,0:T(8,128)(2,1)S(1)} %collective-permute-done.20.refs_2_, ...), custom_call_target="tpu_custom_call", output_to_operand_aliasing={{}: (5, {})} | custom-call | flops 1073741824 | bytes 6291456 | tf_op jit(solution)/shard_map/dots/pallas_call | solution.py:291
  81.3 2.3 %dots.7 = f32[1024,512]{1,0:T(8,128)S(1)} custom-call(bf16[2064,128]{1,0:T(8,128)(2,1)S(1)} %collective-permute-done.18.refs_0_, bf16[2064,128]{1,0:T(8,128)(2,1)S(1)} %collective-permute-done.19.refs_1_, bf16[4096,512]{1,0:T(8,128)(2,1)S(1)} %panel.1.refs_5_.refs_2_.refs_4_, f32[1024,512]{1,0:T(8,128)S(1)} %dots.6.refs_3_), custom_call_target="tpu_custom_call", output_to_operand_aliasing={{}: (3, {})} | custom-call | flops 1073741824 | bytes 6291456 | tf_op jit(solution)/shard_map/dots/pallas_call | solution.py:291
  83.6 10.1 %conditional.1 = (bf16[1024,512]{1,0:T(8,128)(2,1)}) conditional(s32[]{:T(128)} %bitcast.3, (s32[8,4]{0,1:T(4,128)S(1)}, bf16[2064,128]{1,0:T(8,128)(2,1)S(1)}, bf16[2064,128]{1,0:T(8,128)(2,1)S(1)}, bf16[768,128]{1,0:T(8,128)(2,1)S(1)}, bf16[768,128]{1,0:T(8,128)(2,1)S(1)}, /*index=5*/bf16[4096,512]{1,0:T(8,128)(2,1)S(1)}, ...), branch_computations={%region_0.0_spmd, %region_1.10_spmd} | conditional | flops 1074790400 | bytes 55080728 | solution.py:507
  83.7 2.3 %finish.1 = (f32[1024,512]{1,0:T(8,128)S(1)}, f32[1,512]{1,0:T(1,128)S(1)}) custom-call(s32[4,8]{1,0:T(4,128)S(1)} %bitcast.31, bf16[2064,128]{1,0:T(8,128)(2,1)S(1)} %get-tuple-element.264.refs_0_, bf16[2064,128]{1,0:T(8,128)(2,1)S(1)} %get-tuple-element.265.refs_1_, bf16[768,128]{1,0:T(8,128)(2,1)S(1)} %get-tuple-element.266.refs_2_, ...), custom_call_target="tpu_custom_call" | custom-call | flops 1073741824 | bytes 6291456 | tf_op jit(solution)/shard_map/cond/branch_0_fun/finish/pallas_call | solution.py:372
  86.6 1.5 %collective-permute-start.1 = (f32[1,512]{1,0:T(1,128)S(1)}, f32[1,512]{1,0:T(1,128)S(1)}, u32[]{:S(2)}, u32[]{:S(2)}) collective-permute-start(f32[1,512]{1,0:T(1,128)S(1)} %get-tuple-element.272.refs_0_), channel_id=1, source_target_pairs={{0,16},{1,17},{2,18},{3,19},{4,20},{5,21},{6,22},{7,23},{8,24},{9,... | collective-permute-start | bytes 6152 | tf_op jit(solution)/shard_map/cond/branch_0_fun/ppermute | solution.py:459
  90.1 2.4 %collective-permute-done.2.refs_3_ = f32[1,512]{1,0:T(1,128)S(1)} collective-permute-done((f32[1,512]{1,0:T(1,128)S(1)}, f32[1,512]{1,0:T(1,128)S(1)}, u32[]{:S(2)}, u32[]{:S(2)}) %collective-permute-start.2) | collective-permute-done | bytes 2080 | tf_op jit(solution)/shard_map/cond/branch_0_fun/ppermute | solution.py:459
  (53 shorter events, 17.9 us)
Async XLA Ops:
  1.7 8.8 %collective-permute-start.5 = (bf16[3344,128]{1,0:T(8,128)(2,1)S(1)}, bf16[3344,128]{1,0:T(8,128)(2,1)S(1)}, u32[]{:S(2)}, u32[]{:S(2)}) collective-permute-start(bf16[3344,128]{1,0:T(8,128)(2,1)S(1)} %get-tuple-element.296.own_ref.refs_0_), channel_id=1, source_target_pairs={{0,1},{1,0},{2,3},{3,2},{4,5},{5,4},{6,7},{7,6},{8,9},{9,8},{10,11... | collective-permute-start | bytes 2568200 | tf_op jit(solution)/shard_map/ppermute | solution.py:459
  2.2 27.7 %collective-permute-start.17 = (bf16[2064,128]{1,0:T(8,128)(2,1)S(1)}, bf16[2064,128]{1,0:T(8,128)(2,1)S(1)}, u32[]{:S(2)}, u32[]{:S(2)}) collective-permute-start(bf16[2064,128]{1,0:T(8,128)(2,1)S(1)} %get-tuple-element.299), channel_id=1, source_target_pairs={{0,4},{1,5},{2,6},{3,7},{4,0},{5,1},{6,2},{7,3},{8,12},{9,13},{10,... | collective-permute-start | bytes 1585160 | tf_op jit(solution)/shard_map/ppermute | solution.py:459
  5.8 33.4 %collective-permute-start.14 = (bf16[3344,128]{1,0:T(8,128)(2,1)S(1)}, bf16[3344,128]{1,0:T(8,128)(2,1)S(1)}, u32[]{:S(2)}, u32[]{:S(2)}) collective-permute-start(bf16[3344,128]{1,0:T(8,128)(2,1)S(1)} %get-tuple-element.296.own_ref.refs_0_), channel_id=1, source_target_pairs={{0,16},{1,17},{2,18},{3,19},{4,20},{5,21},{6,22},{7,23},{8,24},{9,... | collective-permute-start | bytes 2568200 | tf_op jit(solution)/shard_map/ppermute | solution.py:459
  7.4 33.9 %collective-permute-start.13 = (bf16[3344,128]{1,0:T(8,128)(2,1)S(1)}, bf16[3344,128]{1,0:T(8,128)(2,1)S(1)}, u32[]{:S(2)}, u32[]{:S(2)}) collective-permute-start(bf16[3344,128]{1,0:T(8,128)(2,1)S(1)} %get-tuple-element.296.own_ref.refs_0_), channel_id=1, source_target_pairs={{0,8},{1,9},{2,10},{3,11},{4,12},{5,13},{6,14},{7,15},{8,0},{9,1},... | collective-permute-start | bytes 2568200 | tf_op jit(solution)/shard_map/ppermute | solution.py:459
  8.9 28.9 %collective-permute-start.25 = (bf16[2064,128]{1,0:T(8,128)(2,1)S(1)}, bf16[2064,128]{1,0:T(8,128)(2,1)S(1)}, u32[]{:S(2)}, u32[]{:S(2)}) collective-permute-start(bf16[2064,128]{1,0:T(8,128)(2,1)S(1)} %get-tuple-element.299), channel_id=1, source_target_pairs={{0,2},{1,3},{2,0},{3,1},{4,6},{5,7},{6,4},{7,5},{8,10},{9,11},{10,... | collective-permute-start | bytes 1585160 | tf_op jit(solution)/shard_map/ppermute | solution.py:459
  12.0 19.5 %collective-permute-start.6 = (f32[8,128]{1,0:T(8,128)S(1)}, f32[8,128]{1,0:T(8,128)S(1)}, u32[]{:S(2)}, u32[]{:S(2)}) collective-permute-start(f32[8,128]{1,0:T(8,128)S(1)} %get-tuple-element.297), channel_id=1, source_target_pairs={{0,8},{1,9},{2,10},{3,11},{4,12},{5,13},{6,14},{7,15},{8,0},{9,1},... | collective-permute-start | bytes 12296 | tf_op jit(solution)/shard_map/ppermute | solution.py:459
  31.5 4.5 %collective-permute-start.8 = (f32[8,128]{1,0:T(8,128)S(1)}, f32[8,128]{1,0:T(8,128)S(1)}, u32[]{:S(2)}, u32[]{:S(2)}) collective-permute-start(f32[8,128]{1,0:T(8,128)S(1)} %get-tuple-element.297), channel_id=1, source_target_pairs={{0,24},{1,25},{2,26},{3,27},{4,28},{5,29},{6,30},{7,31},{8,16},{9,... | collective-permute-start | bytes 12296 | tf_op jit(solution)/shard_map/ppermute | solution.py:459
  33.5 30.8 %collective-permute-start.18 = (bf16[2064,128]{1,0:T(8,128)(2,1)S(1)}, bf16[2064,128]{1,0:T(8,128)(2,1)S(1)}, u32[]{:S(2)}, u32[]{:S(2)}) collective-permute-start(bf16[2064,128]{1,0:T(8,128)(2,1)S(1)} %collective-permute-done.17.refs_0_), channel_id=1, source_target_pairs={{0,2},{1,3},{2,0},{3,1},{4,6},{5,7},{6,4},{7,5},{8,10},{9,11},{10,... | collective-permute-start | bytes 1585160 | tf_op jit(solution)/shard_map/ppermute | solution.py:459
  37.2 17.7 %collective-permute-start.27 = (bf16[768,128]{1,0:T(8,128)(2,1)S(1)}, bf16[768,128]{1,0:T(8,128)(2,1)S(1)}, u32[]{:S(2)}, u32[]{:S(2)}) collective-permute-start(bf16[768,128]{1,0:T(8,128)(2,1)S(1)} %get-tuple-element.300), channel_id=1, source_target_pairs={{0,2},{1,3},{2,0},{3,1},{4,6},{5,7},{6,4},{7,5},{8,10},{9,11},{10,... | collective-permute-start | bytes 589832 | tf_op jit(solution)/shard_map/ppermute | solution.py:459
  37.8 13.2 %collective-permute-start.10 = (f32[16,128]{1,0:T(8,128)S(1)}, f32[16,128]{1,0:T(8,128)S(1)}, u32[]{:S(2)}, u32[]{:S(2)}) collective-permute-start(f32[16,128]{1,0:T(8,128)S(1)} %pad_maximum_fusion.refs_0_), channel_id=1, source_target_pairs={{0,2},{1,3},{2,0},{3,1},{4,6},{5,7},{6,4},{7,5},{8,10},{9,11},{10,... | collective-permute-start | bytes 24584 | tf_op jit(solution)/shard_map/ppermute | solution.py:459
  39.2 11.8 %collective-permute-start.11 = (f32[16,128]{1,0:T(8,128)S(1)}, f32[16,128]{1,0:T(8,128)S(1)}, u32[]{:S(2)}, u32[]{:S(2)}) collective-permute-start(f32[16,128]{1,0:T(8,128)S(1)} %pad_maximum_fusion.refs_0_), channel_id=1, source_target_pairs={{0,4},{1,5},{2,6},{3,7},{4,0},{5,1},{6,2},{7,3},{8,12},{9,13},{10,... | collective-permute-start | bytes 24584 | tf_op jit(solution)/shard_map/ppermute | solution.py:459
  41.3 11.5 %collective-permute-start.12 = (f32[16,128]{1,0:T(8,128)S(1)}, f32[16,128]{1,0:T(8,128)S(1)}, u32[]{:S(2)}, u32[]{:S(2)}) collective-permute-start(f32[16,128]{1,0:T(8,128)S(1)} %pad_maximum_fusion.refs_0_), channel_id=1, source_target_pairs={{0,6},{1,7},{2,4},{3,5},{4,2},{5,3},{6,0},{7,1},{8,14},{9,15},{10,... | collective-permute-start | bytes 24584 | tf_op jit(solution)/shard_map/ppermute | solution.py:459
  51.0 21.5 %collective-permute-start.26 = (bf16[2064,128]{1,0:T(8,128)(2,1)S(1)}, bf16[2064,128]{1,0:T(8,128)(2,1)S(1)}, u32[]{:S(2)}, u32[]{:S(2)}) collective-permute-start(bf16[2064,128]{1,0:T(8,128)(2,1)S(1)} %collective-permute-done.25.refs_0_), channel_id=1, source_target_pairs={{0,1},{1,0},{2,3},{3,2},{4,5},{5,4},{6,7},{7,6},{8,9},{9,8},{10,11... | collective-permute-start | bytes 1585160 | tf_op jit(solution)/shard_map/ppermute | solution.py:459
  51.0 17.5 %collective-permute-start.16 = (bf16[1680,128]{1,0:T(8,128)(2,1)S(1)}, bf16[1680,128]{1,0:T(8,128)(2,1)S(1)}, u32[]{:S(2)}, u32[]{:S(2)}) collective-permute-start(bf16[1680,128]{1,0:T(8,128)(2,1)S(1)} %slice.9), channel_id=1, source_target_pairs={{0,8},{1,9},{2,10},{3,11},{4,12},{5,13},{6,14},{7,15},{8,0},{9,1},... | collective-permute-start | bytes 1290248 | tf_op jit(solution)/shard_map/ppermute | solution.py:459
  52.8 11.5 %collective-permute-start.20 = (bf16[768,128]{1,0:T(8,128)(2,1)S(1)}, bf16[768,128]{1,0:T(8,128)(2,1)S(1)}, u32[]{:S(2)}, u32[]{:S(2)}) collective-permute-start(bf16[768,128]{1,0:T(8,128)(2,1)S(1)} %get-tuple-element.300), channel_id=1, source_target_pairs={{0,4},{1,5},{2,6},{3,7},{4,0},{5,1},{6,2},{7,3},{8,12},{9,13},{10,... | collective-permute-start | bytes 589832 | tf_op jit(solution)/shard_map/ppermute | solution.py:459
  54.8 11.7 %collective-permute-start.15 = (bf16[1664,128]{1,0:T(8,128)(2,1)S(1)}, bf16[1664,128]{1,0:T(8,128)(2,1)S(1)}, u32[]{:S(2)}, u32[]{:S(2)}) collective-permute-start(bf16[1664,128]{1,0:T(8,128)(2,1)S(1)} %slice.8), channel_id=1, source_target_pairs={{0,16},{1,17},{2,18},{3,19},{4,20},{5,21},{6,22},{7,23},{8,24},{9,... | collective-permute-start | bytes 1277960 | tf_op jit(solution)/shard_map/ppermute | solution.py:459
  64.3 13.9 %collective-permute-start.23 = (bf16[2064,128]{1,0:T(8,128)(2,1)S(1)}, bf16[2064,128]{1,0:T(8,128)(2,1)S(1)}, u32[]{:S(2)}, u32[]{:S(2)}) collective-permute-start(bf16[2064,128]{1,0:T(8,128)(2,1)S(1)} %collective-permute-done.17.refs_0_), channel_id=1, source_target_pairs={{0,1},{1,0},{2,3},{3,2},{4,5},{5,4},{6,7},{7,6},{8,9},{9,8},{10,11... | collective-permute-start | bytes 1585160 | tf_op jit(solution)/shard_map/ppermute | solution.py:459
  64.3 17.0 %collective-permute-start.19 = (bf16[2064,128]{1,0:T(8,128)(2,1)S(1)}, bf16[2064,128]{1,0:T(8,128)(2,1)S(1)}, u32[]{:S(2)}, u32[]{:S(2)}) collective-permute-start(bf16[2064,128]{1,0:T(8,128)(2,1)S(1)} %collective-permute-done.18.refs_0_), channel_id=1, source_target_pairs={{0,1},{1,0},{2,3},{3,2},{4,5},{5,4},{6,7},{7,6},{8,9},{9,8},{10,11... | collective-permute-start | bytes 1585160 | tf_op jit(solution)/shard_map/ppermute | solution.py:459
  66.6 8.6 %collective-permute-start.21 = (bf16[768,128]{1,0:T(8,128)(2,1)S(1)}, bf16[768,128]{1,0:T(8,128)(2,1)S(1)}, u32[]{:S(2)}, u32[]{:S(2)}) collective-permute-start(bf16[768,128]{1,0:T(8,128)(2,1)S(1)} %collective-permute-done.20.refs_2_), channel_id=1, source_target_pairs={{0,2},{1,3},{2,0},{3,1},{4,6},{5,7},{6,4},{7,5},{8,10},{9,11},{10,... | collective-permute-start | bytes 589832 | tf_op jit(solution)/shard_map/ppermute | solution.py:459
  68.5 6.8 %collective-permute-start.28 = (bf16[768,128]{1,0:T(8,128)(2,1)S(1)}, bf16[768,128]{1,0:T(8,128)(2,1)S(1)}, u32[]{:S(2)}, u32[]{:S(2)}) collective-permute-start(bf16[768,128]{1,0:T(8,128)(2,1)S(1)} %collective-permute-done.27.refs_2_), channel_id=1, source_target_pairs={{0,1},{1,0},{2,3},{3,2},{4,5},{5,4},{6,7},{7,6},{8,9},{9,8},{10,11... | collective-permute-start | bytes 589832 | tf_op jit(solution)/shard_map/ppermute | solution.py:459
  72.5 5.8 %collective-permute-start.24 = (bf16[768,128]{1,0:T(8,128)(2,1)S(1)}, bf16[768,128]{1,0:T(8,128)(2,1)S(1)}, u32[]{:S(2)}, u32[]{:S(2)}) collective-permute-start(bf16[768,128]{1,0:T(8,128)(2,1)S(1)} %collective-permute-done.20.refs_2_), channel_id=1, source_target_pairs={{0,1},{1,0},{2,3},{3,2},{4,5},{5,4},{6,7},{7,6},{8,9},{9,8},{10,11... | collective-permute-start | bytes 589832 | tf_op jit(solution)/shard_map/ppermute | solution.py:459
  75.2 8.4 %collective-permute-start.22 = (bf16[768,128]{1,0:T(8,128)(2,1)S(1)}, bf16[768,128]{1,0:T(8,128)(2,1)S(1)}, u32[]{:S(2)}, u32[]{:S(2)}) collective-permute-start(bf16[768,128]{1,0:T(8,128)(2,1)S(1)} %collective-permute-done.21), channel_id=1, source_target_pairs={{0,1},{1,0},{2,3},{3,2},{4,5},{5,4},{6,7},{7,6},{8,9},{9,8},{10,11... | collective-permute-start | bytes 589832 | tf_op jit(solution)/shard_map/ppermute | solution.py:459
  86.0 3.7 %collective-permute-start = (f32[1,512]{1,0:T(1,128)S(1)}, f32[1,512]{1,0:T(1,128)S(1)}, u32[]{:S(2)}, u32[]{:S(2)}) collective-permute-start(f32[1,512]{1,0:T(1,128)S(1)} %get-tuple-element.272.refs_0_), channel_id=1, source_target_pairs={{0,8},{1,9},{2,10},{3,11},{4,12},{5,13},{6,14},{7,15},{8,0},{9,1},... | collective-permute-start | bytes 6152 | tf_op jit(solution)/shard_map/cond/branch_0_fun/ppermute | solution.py:459
  88.1 4.5 %collective-permute-start.2 = (f32[1,512]{1,0:T(1,128)S(1)}, f32[1,512]{1,0:T(1,128)S(1)}, u32[]{:S(2)}, u32[]{:S(2)}) collective-permute-start(f32[1,512]{1,0:T(1,128)S(1)} %get-tuple-element.272.refs_0_), channel_id=1, source_target_pairs={{0,24},{1,25},{2,26},{3,27},{4,28},{5,29},{6,30},{7,31},{8,16},{9,... | collective-permute-start | bytes 6152 | tf_op jit(solution)/shard_map/cond/branch_0_fun/ppermute | solution.py:459
  (7 other events, 17.7 us)

commit v4 on v3

--- a/solution.py
+++ b/solution.py
@@ -37,9 +37,13 @@
     return ref[end - PAD : end, :].astype(F32).astype(I32)[0:1, :]
 
 
-def pack_kernel(mask_ref, block_ref, out_ref, head_ref):
+def places(ref):
+    return (ref.shape[0] - PAD) // TB
+
+
+def pack_kernel(mask_ref, block_ref, head_ref, rest_ref):
     ti, tj = tiles_of(block_ref.shape)
-    slots, first = (out_ref.shape[0] - PAD) // TB, (head_ref.shape[0] - PAD) // TB
+    first, slots = places(head_ref), places(head_ref) + places(rest_ref)
     lane = lax.broadcasted_iota(I32, (PAD, TB), 1)
     table = jnp.full((PAD, TB), -1, I32)
     used = jnp.int32(0)
@@ -47,27 +51,29 @@
         for j in range(tj):
             stored = mask_ref[j, i]
 
-            @pl.when(jnp.logical_and(stored > 0, used < slots))
+            @pl.when(jnp.logical_and(stored > 0, used < first))
             def _(i=i, j=j, used=used):
                 tile = block_ref[i * TB : (i + 1) * TB, j * TB : (j + 1) * TB]
-                here = pl.ds(pl.multiple_of(used * TB, TB), TB)
-                out_ref[here, :] = tile
-
-                @pl.when(used < first)
-                def _():
-                    head_ref[here, :] = tile
+                head_ref[pl.ds(pl.multiple_of(used * TB, TB), TB), :] = tile
+
+            if i * tj + j >= first:
+
+                @pl.when(jnp.logical_and(stored > 0, jnp.logical_and(used >= first, used < slots)))
+                def _(i=i, j=j, used=used):
+                    tile = block_ref[i * TB : (i + 1) * TB, j * TB : (j + 1) * TB]
+                    rest_ref[pl.ds(pl.multiple_of((used - first) * TB, TB), TB), :] = tile
 
             table = jnp.where(lane == i * tj + j, jnp.where(stored > 0, used, -1), table)
             used = used + stored
     table = jnp.where(lane == ti * tj, used, table).astype(F32).astype(BF16)
-    out_ref[slots * TB :, :] = table
     head_ref[first * TB :, :] = table
+    rest_ref[(slots - first) * TB :, :] = table
 
 
 def pack(block, mask_t, slots, first):
     return pl.pallas_call(
         pack_kernel,
-        out_shape=tuple(jax.ShapeDtypeStruct((n * TB + PAD, TB), BF16) for n in (slots, first)),
+        out_shape=tuple(jax.ShapeDtypeStruct((n * TB + PAD, TB), BF16) for n in (first, slots - first)),
         in_specs=[SMEM, VMEM],
         out_specs=(VMEM, VMEM),
         compiler_params=params(8),
@@ -80,9 +86,9 @@
     return ref[pl.ds(pl.multiple_of(jnp.clip(at, 0, count - 1) * TB, TB), TB), :]
 
 
-def pool_kernel(first, mask_ref, block_ref, own_ref, other_ref, out_ref, msg_ref):
+def pool_kernel(first, mask_ref, block_ref, rest_ref, other_ref, out_ref, msg_ref):
     ti, tj = tiles_of(block_ref.shape)
-    slots, n = (own_ref.shape[0] - PAD) // TB, out_ref.shape[0] // TB
+    spare, n = places(rest_ref), out_ref.shape[0] // TB
     core = place()[2]
     count = jnp.int32(0)
     sums = [jnp.zeros((8, TB), F32) for _ in range(tj)]
@@ -100,18 +106,18 @@
     for i in range(n):
         p = core * n + i
         in_0 = p < left_0
-        at = first + jnp.where(in_0, p, p - left_0)
+        at = jnp.where(in_0, p, p - left_0)
         mine = jnp.where(in_0, 0, 1) == core
-        tile = jnp.where(mine, load(own_ref, at, slots), load(other_ref, at, slots))
+        tile = jnp.where(mine, load(rest_ref, at, spare), load(other_ref, at, spare))
         out_ref[i * TB : (i + 1) * TB, :] = tile
-    over = jnp.logical_or(count > slots, left + left_other > 2 * n)
+    over = jnp.logical_or(left > spare, left + left_other > 2 * n)
     msg_ref[...] = jnp.zeros_like(msg_ref)
     for j in range(tj):
         msg_ref[j : j + 1, :] = jnp.sum(sums[j], axis=0, keepdims=True)
     msg_ref[tj : tj + 1, :] = jnp.full((1, TB), 1.0, F32) * jnp.where(over, 1.0, 0.0)
 
 
-def pool(block, mask_t, own, other, first, n):
+def pool(block, mask_t, rest, other, first, n):
     s_rows = -(-(block.shape[1] // TB + 1) // 8) * 8
     return pl.pallas_call(
         functools.partial(pool_kernel, first),
@@ -124,7 +130,7 @@
         compiler_params=params(8),
         cost_estimate=cost(1e6, 2 * block.size * 2),
         name="pool",
-    )(mask_t, block, own, other)
+    )(mask_t, block, rest, other)
 
 
 def read_tables(refs, itab, stab, sem):
@@ -139,11 +145,11 @@
     return jnp.zeros((TB, TB), BF16)
 
 
-def whole_tile(parts, slots, at):
-    first = parts[0].shape[0] // TB if len(parts) == 2 else slots
+def whole_tile(parts, at, low):
+    first = places(parts[0])
     tile = load(parts[0], at, first)
-    if len(parts) == 2:
-        tile = jnp.where(at >= first, load(parts[1], at - first, slots - first), tile)
+    if not low:
+        tile = jnp.where(at >= first, load(parts[1], at - first, places(parts[1])), tile)
     return jnp.where(at >= 0, tile, zero_tile())
 
 
@@ -160,94 +166,61 @@
     return out
 
 
-def panel_kernel(slots, sizes, rows, *refs):
-    blocks = regroup(refs, sizes)
-    panel_ref, itab, stab, sem = refs[sum(sizes) :]
-    cols = panel_ref.shape[1]
-    ti, tj = rows // TB, cols // TB
-    me = place()[0]
-    read_tables([b[-1] for b in blocks], itab, stab, sem)
-    for q in range(len(sizes)):
-        base = (me ^ q) * rows
-
-        def strip(i, done, q=q, base=base):
-            for j in range(tj):
-                tile = whole_tile(blocks[q], slots, stab[q, i * tj + j])
-                panel_ref[pl.ds(pl.multiple_of(base + i * TB, TB), TB), j * TB : (j + 1) * TB] = tile
-            return done
-
-        lax.fori_loop(0, ti, strip, 0, unroll=2)
-
-
-def panel(payloads, slots, rows, cols):
-    n = len(payloads)
-    sizes = [len(p) for p in payloads]
-    return pl.pallas_call(
-        functools.partial(panel_kernel, slots, sizes, rows),
-        out_shape=jax.ShapeDtypeStruct((n * rows, cols), BF16),
-        in_specs=[VMEM] * sum(sizes),
-        out_specs=VMEM,
-        scratch_shapes=table_scratch(n),
-        compiler_params=params(20),
-        cost_estimate=cost(1e7, 2 * n * rows * cols * 2),
-        name="panel",
-    )(*[x for p in payloads for x in p])
-
-
 def strip_rows(rows):
     return min(rows, 256)
 
 
-def tile_getters(kind, refs, stab, tiles, core):
+def tile_getters(kind, refs, stab, at_table, tiles, core):
+    first = places(refs[0])
     if kind == "whole":
-        slots = (refs[0].shape[0] - PAD) // TB
-        return [lambda at, r=r: whole_tile([r], slots, at) for r in refs]
-    first = (refs[0].shape[0] - PAD) // TB
+        return [lambda at, low, b=b: whole_tile((refs[b], refs[2 + b]), at, low) for b in range(2)]
+
+    def head(side, at):
+        return jnp.where(
+            jnp.logical_and(at >= 0, at < first), load(refs[side], at, first), zero_tile()
+        )
+
     if kind == "heads":
-        return [
-            lambda at, r=r: jnp.where(
-                jnp.logical_and(at >= 0, at < first), load(r, at, first), zero_tile()
-            )
-            for r in refs
-        ]
+        return [lambda at, low, b=b: head(b, at) for b in range(2)]
     n = refs[2].shape[0] // TB
-    left = [jnp.maximum(stab[b, tiles] - first, 0) for b in range(2)]
+    left = [jnp.maximum(stab[at_table[b], tiles] - first, 0) for b in range(2)]
     left_0 = jnp.where(core == 0, left[0], left[1])
 
     def getter(side):
         base = jnp.where((core ^ side) == 1, left_0, 0) - first
 
-        def get(at):
+        def get(at, low):
+            if low:
+                return head(side, at)
             p = at + base
             part = jnp.where(p >= n, 1, 0)
             local = p - part * n
             rest = jnp.where(part == core, load(refs[2], local, n), load(refs[3], local, n))
             if kind == "pools":
                 return jnp.where(at >= first, rest, zero_tile())
-            tile = jnp.where(at >= first, rest, load(refs[side], at, first))
-            return jnp.where(at >= 0, tile, zero_tile())
+            return jnp.where(at >= first, rest, head(side, at))
 
         return get
 
     return [getter(0), getter(1)]
 
 
-def products(kind, refs, pair, panel_ref, itab, stab, sem, lhs, rows, use):
+def products(kind, refs, pair, panel_ref, stab, at_table, lhs, rows, use):
     cols = panel_ref.shape[1]
     step = strip_rows(rows)
     tj = cols // TB
     _, z, core = place()
-    read_tables(refs[:2], itab, stab, sem)
-    getters = tile_getters(kind, refs, stab, rows // TB * tj, core)
+    getters = tile_getters(kind, refs, stab, at_table, rows // TB * tj, core)
     n = rows // step
-    start = (refs[0].shape[0] - PAD) // TB // tj * TB // step if kind == "pools" else 0
+    safe = places(refs[0]) // tj
+    start = safe * TB // step if kind == "pools" else 0
 
     def unpack(m):
         for b, get in enumerate(getters):
             for a in range(step // TB):
-                for j in range(tj):
-                    tile = get(stab[b, (m * (step // TB) + a) * tj + j])
-                    lhs[m % 2, a * TB : (a + 1) * TB, b * cols + j * TB : b * cols + (j + 1) * TB] = tile
+                i = m * (step // TB) + a
+                tiles = [get(stab[at_table[b], i * tj + j], i < safe) for j in range(tj)]
+                lhs[m % 2, a * TB : (a + 1) * TB, b * cols : (b + 1) * cols] = jnp.concatenate(tiles, axis=1)
 
     unpack(start)
     for m in range(start):
@@ -267,38 +240,84 @@
         use(m, total)
 
 
-def dot_kernel(kind, n, pair, rows, has_prior, *refs):
-    panel_ref = refs[n]
-    prior_ref = refs[n + 1] if has_prior else None
-    acc_ref, itab, stab, sem, lhs = refs[n + 1 + has_prior :]
+def adder(acc_ref, prior_ref, rows):
     step = strip_rows(rows)
 
     def use(m, got):
         here = slice(m * step, (m + 1) * step)
-        acc_ref[here, :] = prior_ref[here, :] + got if has_prior else got
-
-    products(kind, refs[:n], pair, panel_ref, itab, stab, sem, lhs, rows, use)
-
-
-def dot_scratch(rows, cols):
-    return table_scratch(2) + [pltpu.VMEM((2, strip_rows(rows), 2 * cols), BF16)]
-
-
-def dots(kind, payloads, pair, dense, prior, rows):
+        acc_ref[here, :] = got if prior_ref is None else prior_ref[here, :] + got
+
+    return use
+
+
+def dot_scratch(n, rows, cols):
+    return table_scratch(n) + [pltpu.VMEM((2, strip_rows(rows), 2 * cols), BF16)]
+
+
+def panel_kernel(n, rows, *refs):
+    blocks, other = regroup(refs, [2] * n), refs[2 * n : 2 * n + 2]
+    panel_ref, acc_ref, itab, stab, sem, lhs = refs[2 * n + 2 :]
+    cols = panel_ref.shape[1]
+    ti, tj = rows // TB, cols // TB
+    me = place()[0]
+    read_tables([b[1] for b in blocks] + [other[1]], itab, stab, sem)
+    safe = places(blocks[0][0]) // tj
+    for q in range(n):
+        base = (me ^ q) * rows
+
+        def strip(i, done, q=q, base=base, low=False):
+            tiles = [whole_tile(blocks[q], stab[q, i * tj + j], low) for j in range(tj)]
+            panel_ref[pl.ds(pl.multiple_of(base + i * TB, TB), TB), :] = jnp.concatenate(tiles, axis=1)
+            return done
+
+        lax.fori_loop(0, safe, functools.partial(strip, low=True), 0, unroll=2)
+        lax.fori_loop(safe, ti, strip, 0, unroll=2)
+    mine = blocks[0]
+    heads_rests = (mine[0], other[0], mine[1], other[1])
+    products("whole", heads_rests, 0, panel_ref, stab, (0, n), lhs, rows, adder(acc_ref, None, rows))
+
+
+def panel(payloads, other, rows, cols):
+    n = len(payloads)
+    return pl.pallas_call(
+        functools.partial(panel_kernel, n, rows),
+        out_shape=(
+            jax.ShapeDtypeStruct((n * rows, cols), BF16),
+            jax.ShapeDtypeStruct((rows, cols), F32),
+        ),
+        in_specs=[VMEM] * (2 * n + 2),
+        out_specs=(VMEM, VMEM),
+        scratch_shapes=dot_scratch(n + 1, rows, cols),
+        compiler_params=params(24),
+        cost_estimate=cost(4 * rows * cols * cols, 2 * n * rows * cols * 2),
+        name="panel",
+    )(*[x for p in payloads for x in p], *other)
+
+
+def dot_kernel(kind, pairs, rows, *refs):
+    per = 4 if kind == "all" else 2
+    blocks = regroup(refs, [per] * len(pairs))
+    panel_ref, prior_ref, acc_ref, itab, stab, sem, lhs = refs[per * len(pairs) :]
+    read_tables([r for b in blocks for r in b[:2]], itab, stab, sem)
+    for k, (pair, b) in enumerate(zip(pairs, blocks)):
+        use = adder(acc_ref, acc_ref if k else prior_ref, rows)
+        products(kind, b, pair, panel_ref, stab, (2 * k, 2 * k + 1), lhs, rows, use)
+
+
+def dots(kind, blocks, pairs, dense, prior, rows):
     cols = dense.shape[1]
-    n = len(payloads)
-    extra = [] if prior is None else [prior]
-    return pl.pallas_call(
-        functools.partial(dot_kernel, kind, n, pair, rows, len(extra)),
+    flat = [x for b in blocks for x in b]
+    return pl.pallas_call(
+        functools.partial(dot_kernel, kind, pairs, rows),
         out_shape=jax.ShapeDtypeStruct((rows, cols), F32),
-        in_specs=[VMEM] * (n + 1 + len(extra)),
+        in_specs=[VMEM] * (len(flat) + 2),
         out_specs=VMEM,
-        scratch_shapes=dot_scratch(rows, cols),
-        input_output_aliases={n + 1: 0} if extra else {},
-        compiler_params=params(20),
-        cost_estimate=cost(4 * rows * cols * cols, 12 * rows * cols),
+        scratch_shapes=dot_scratch(2 * len(pairs), rows, cols),
+        input_output_aliases={len(flat) + 1: 0},
+        compiler_params=params(24),
+        cost_estimate=cost(4 * rows * cols * cols * len(pairs), 12 * rows * cols),
         name="dots",
-    )(*payloads, dense, *extra)
+    )(*flat, dense, prior)
 
 
 def means_kernel(n_pairs, s_rows, order, *refs):
@@ -343,42 +362,40 @@
     )(*messages, thr, dense)
 
 
-def last_kernel(kind, n, pair, rows, keep_ref, *refs):
-    panel_ref, prior_ref, cut_ref, acc_ref, tot_ref, itab, stab, sem, lhs = refs[n:]
+def last_kernel(pair, rows, *refs):
+    blocks, (panel_ref, prior_ref, cut_ref, keep_ref, acc_ref, tot_ref) = refs[:4], refs[4:10]
+    itab, stab, sem, lhs = refs[10:]
     step = strip_rows(rows)
     cols = panel_ref.shape[1]
     per = step // TB
-    totals = [jnp.zeros((8, TB), F32) for _ in range(cols // TB)]
+    totals = [jnp.zeros((8, cols), F32)]
+    read_tables(blocks[:2], itab, stab, sem)
 
     def use(m, got):
         prior = prior_ref[m * step : (m + 1) * step, :]
         got = jnp.maximum((prior if got is None else prior + got) - cut_ref[0:1, :], 0.0)
         for a in range(per):
-            at = (m * per + a) * TB
-            for j in range(cols // TB):
-                kept = keep_ref[j, m * per + a].astype(F32)
-                cell = got[a * TB : (a + 1) * TB, j * TB : (j + 1) * TB] * kept
-                acc_ref[at : at + TB, j * TB : (j + 1) * TB] = cell
-                totals[j] += jnp.sum(cell.reshape(TB // 8, 8, TB), axis=0)
-
-    products(kind, refs[:n], pair, panel_ref, itab, stab, sem, lhs, rows, use)
-    for j, t in enumerate(totals):
-        tot_ref[:, j * TB : (j + 1) * TB] = jnp.sum(t, axis=0, keepdims=True)
-
-
-def finish(kind, keep_t, payloads, pair, dense, prior, cut, rows):
+            i = m * per + a
+            cell = got[a * TB : (a + 1) * TB, :] * keep_ref[i : i + 1, :]
+            acc_ref[i * TB : (i + 1) * TB, :] = cell
+            totals[0] += jnp.sum(cell.reshape(TB // 8, 8, cols), axis=0)
+
+    products("pools", blocks, pair, panel_ref, stab, (0, 1), lhs, rows, use)
+    tot_ref[...] = jnp.sum(totals[0], axis=0, keepdims=True)
+
+
+def finish(keep, blocks, pair, dense, prior, cut, rows):
     cols = dense.shape[1]
-    n = len(payloads)
-    return pl.pallas_call(
-        functools.partial(last_kernel, kind, n, pair, rows),
+    return pl.pallas_call(
+        functools.partial(last_kernel, pair, rows),
         out_shape=(jax.ShapeDtypeStruct((rows, cols), F32), jax.ShapeDtypeStruct((1, cols), F32)),
-        in_specs=[SMEM] + [VMEM] * (n + 3),
+        in_specs=[VMEM] * 8,
         out_specs=(VMEM, VMEM),
-        scratch_shapes=dot_scratch(rows, cols),
+        scratch_shapes=dot_scratch(2, rows, cols),
         compiler_params=params(20),
         cost_estimate=cost(4 * rows * cols * cols, 12 * rows * cols),
         name="finish",
-    )(keep_t, *payloads, dense, prior, cut)
+    )(*blocks, dense, prior, cut, keep)
 
 
 def scale_kernel(n, order, x_ref, *refs):
@@ -444,7 +461,6 @@
     first = ti * tj // 2
     extra = ti * tj * 3 // 16
     slots = ti * tj * 13 // 16
-    half = slots // 2 * TB
     n_z = n_col // 2
     last = n_z - 1
     order = rows * n_row
@@ -458,47 +474,48 @@
         ]
         return lax.ppermute(x, AXES, pairs)
 
-    own, head = pack(values, tile_mask.T, slots, first)
-    own_swapped = send(own, dc=1)
-    spare, sums = pool(values, tile_mask.T, own, own_swapped, first, extra)
-
-    line = {0: [head, spare]}
+    own = pack(values, tile_mask.T, slots, first)
+    own_swapped = [send(x, dc=1) for x in own]
+    spare, sums = pool(values, tile_mask.T, own[1], own_swapped[1], first, extra)
+
+    line = {0: [own[0], spare]}
     swapped = {}
     for j in range(1, n_z):
         low = j & -j
         line[j] = [send(x, dz=low) for x in line[j ^ low]]
         swapped[j] = [send(x, dc=1) for x in line[j]]
 
-    column = {0: [own]}
+    column = {0: own}
     for q in range(1, n_row):
         low = q & -q
         rest = q ^ low
         if rest and rest & -rest == rest:
-            column[q] = [send(column[low][0][:half], dr=rest), send(column[rest][0][half:], dr=low)]
+            column[q] = [send(column[low][0], dr=rest), send(column[rest][1], dr=low)]
         else:
-            column[q] = [send(own, dr=q)]
-
-    dense = panel([column[q] for q in range(n_row)], slots, rows, cols)
+            column[q] = [send(x, dr=q) for x in own]
+
+    dense, acc = panel([column[q] for q in range(n_row)], own_swapped, rows, cols)
 
     sums = functools.reduce(jnp.add, [send(sums, dr=q) for q in range(1, n_row)], sums)
     both = jnp.concatenate([sums, send(sums, dc=1)], axis=0)
     messages = [both] + [send(both, dz=j) for j in range(1, n_z)]
     cut, over = cuts_of(messages, thr_index.reshape(1, cols), dense, sums.shape[0], order)
 
-    acc = None
-    for j in range(n_z):
-        if j == 0:
-            acc = dots("whole", [own, own_swapped], j, dense, acc, rows)
-        elif j < last:
-            parts = [line[j][0], swapped[j][0], line[j][1], swapped[j][1]]
-            acc = dots("all", parts, j, dense, acc, rows)
-        else:
-            acc = dots("heads", [line[j][0], swapped[j][0]], j, dense, acc, rows)
+    early = tuple(range(1, last))
+    if early:
+        blocks = [(line[j][0], swapped[j][0], line[j][1], swapped[j][1]) for j in early]
+        acc = dots("all", blocks, early, dense, acc, rows)
+    acc = dots("heads", [(line[last][0], swapped[last][0])], (last,), dense, acc, rows)
+    keep = jnp.repeat(keep_mask.astype(F32), TB, axis=1)
 
     def fast():
-        parts = [line[last][0], swapped[last][0], line[last][1], swapped[last][1]]
-        pruned, tot = finish("pools", keep_mask.T, parts, last, dense, acc, cut, rows)
-        totals = [tot] + [send(tot, dr=q) for q in range(1, n_row)]
+        blocks = (line[last][0], swapped[last][0], line[last][1], swapped[last][1])
+        pruned, tot = finish(keep, blocks, last, dense, acc, cut, rows)
+        totals = {0: tot}
+        for q in range(1, n_row):
+            low = q & -q
+            totals[q] = send(totals[q ^ low], dr=low)
+        totals = list(totals.values())
         return scale(pruned, totals, order)
 
     def full():

time: 93.9 us -> 98.5 us (1.049)
  starting transfers between devices: 29.8 us -> 35.3 us
  Pallas kernels: 20.2 us -> 15.8 us
  waiting for transfers between devices: 42.6 us -> 46.2 us
    ppermute x27 -> x30, starting transfers between devices: 29.8 us -> 35.3 us  [send(): return lax.ppermute(x, AXES, pairs)]
    pallas_call x6 -> x4, Pallas kernels: 14.8 us -> 10.4 us  [the longest x2 5.34 us: dots(): pl.pallas_call(functools.partial(dot_kernel, kind, pairs, rows), out_shap...]
    ppermute x27 -> x30, waiting for transfers between devices: 42.6 us -> 46.2 us  [send(): return lax.ppermute(x, AXES, pairs)]
  transfers between devices with their start and end apart: 27 -> 30, of which waited for: 11 -> 12; matrix products, arithmetic and copies ran while one was open for 0% -> 0% of each run, Pallas kernels for 16% -> 12%
where the time goes in v4:
time: 98.5 us; the launch traced here: 98.3 us
  waiting for transfers between devices  46.2 us (47%)
  starting transfers between devices  35.3 us (36%)
  Pallas kernels  15.8 us (16%)
    ppermute x30, waiting for transfers between devices, send(): return lax.ppermute(x, AXES, pairs)  46.2 us
    ppermute x30, starting transfers between devices, send(): return lax.ppermute(x, AXES, pairs)  35.3 us
    pallas_call x2, Pallas kernels, dots(): pl.pallas_call(functools.partial(dot_kernel, kind, pairs, rows), out_shap...  5.34 us
    pallas_call x1, Pallas kernels, panel(): pl.pallas_call(functools.partial(panel_kernel, n, rows), out_shape=(jax.S...  3.38 us
  transfers between devices with their start and end apart: 30, of which 12 were waited for; matrix products, arithmetic and copies ran while one was open for 0% of the time, Pallas kernels for 12%

profile of v4, /device:TPU:0, one launch (start us, length us, event | category | flops | bytes accessed | tf_op | source)
XLA Modules:
  0.0 98.3 jit_solution(4346162529216861366)
XLA Ops:
  0.0 1.7 %pack.1 = (bf16[2064,128]{1,0:T(8,128)(2,1)S(1)}, bf16[1296,128]{1,0:T(8,128)(2,1)S(1)}) custom-call(s32[4,8]{1,0:T(4,128)} %bitcast.29, bf16[1024,512]{1,0:T(8,128)(2,1)} %block_ref.3), custom_call_target="tpu_custom_call" | custom-call | flops 1000000 | bytes 2097152 | tf_op jit(solution)/shard_map/pack/pallas_call | solution.py:74
  2.3 2.6 %collective-permute-start.16 = (bf16[1296,128]{1,0:T(8,128)(2,1)S(1)}, bf16[1296,128]{1,0:T(8,128)(2,1)S(1)}, u32[]{:S(2)}, u32[]{:S(2)}) collective-permute-start(bf16[1296,128]{1,0:T(8,128)(2,1)S(1)} %get-tuple-element.300.rest_ref.refs_1_), channel_id=1, source_target_pairs={{0,16},{1,17},{2,18},{3,19},{4,20},{5,21},{6,22},{7,23},{8,24},{9,... | collective-permute-start | bytes 995336 | tf_op jit(solution)/shard_map/ppermute | solution.py:475
  6.9 2.6 %collective-permute-start.20 = (bf16[2064,128]{1,0:T(8,128)(2,1)S(1)}, bf16[2064,128]{1,0:T(8,128)(2,1)S(1)}, u32[]{:S(2)}, u32[]{:S(2)}) collective-permute-start(bf16[2064,128]{1,0:T(8,128)(2,1)S(1)} %get-tuple-element.302.refs_0_), channel_id=1, source_target_pairs={{0,4},{1,5},{2,6},{3,7},{4,0},{5,1},{6,2},{7,3},{8,12},{9,13},{10,... | collective-permute-start | bytes 1585160 | tf_op jit(solution)/shard_map/ppermute | solution.py:475
  9.5 1.5 %pool.1 = (bf16[768,128]{1,0:T(8,128)(2,1)S(1)}, f32[8,128]{1,0:T(8,128)S(1)}) custom-call(s32[4,8]{1,0:T(4,128)} %bitcast.30, bf16[1024,512]{1,0:T(8,128)(2,1)} %block_ref.3, bf16[1296,128]{1,0:T(8,128)(2,1)S(1)} %get-tuple-element.300.rest_ref.refs_1_, bf16[1296,128]{1,0:T(8,128)(2,1)S(1)} %collective-permute-done.5.other_ref.refs_9_), custom_call_target="tpu_custom_call" | custom-call | flops 1000000 | bytes 2097152 | tf_op jit(solution)/shard_map/pool/pallas_call | solution.py:122
  11.0 1.6 %collective-permute-start.6 = (f32[8,128]{1,0:T(8,128)S(1)}, f32[8,128]{1,0:T(8,128)S(1)}, u32[]{:S(2)}, u32[]{:S(2)}) collective-permute-start(f32[8,128]{1,0:T(8,128)S(1)} %get-tuple-element.301), channel_id=1, source_target_pairs={{0,8},{1,9},{2,10},{3,11},{4,12},{5,13},{6,14},{7,15},{8,0},{9,1},... | collective-permute-start | bytes 12296 | tf_op jit(solution)/shard_map/ppermute | solution.py:475
  13.3 1.7 %collective-permute-start.7 = (f32[8,128]{1,0:T(8,128)S(1)}, f32[8,128]{1,0:T(8,128)S(1)}, u32[]{:S(2)}, u32[]{:S(2)}) collective-permute-start(f32[8,128]{1,0:T(8,128)S(1)} %get-tuple-element.301), channel_id=1, source_target_pairs={{0,16},{1,17},{2,18},{3,19},{4,20},{5,21},{6,22},{7,23},{8,24},{9,... | collective-permute-start | bytes 12296 | tf_op jit(solution)/shard_map/ppermute | solution.py:475
  15.0 11.1 %collective-permute-done.6 = f32[8,128]{1,0:T(8,128)S(1)} collective-permute-done((f32[8,128]{1,0:T(8,128)S(1)}, f32[8,128]{1,0:T(8,128)S(1)}, u32[]{:S(2)}, u32[]{:S(2)}) %collective-permute-start.6) | collective-permute-done | bytes 4128 | tf_op jit(solution)/shard_map/ppermute | solution.py:475
  29.1 1.7 %collective-permute-done.8 = f32[8,128]{1,0:T(8,128)S(1)} collective-permute-done((f32[8,128]{1,0:T(8,128)S(1)}, f32[8,128]{1,0:T(8,128)S(1)}, u32[]{:S(2)}, u32[]{:S(2)}) %collective-permute-start.8) | collective-permute-done | bytes 4128 | tf_op jit(solution)/shard_map/ppermute | solution.py:475
  32.7 1.6 %collective-permute-start.26 = (bf16[2064,128]{1,0:T(8,128)(2,1)S(1)}, bf16[2064,128]{1,0:T(8,128)(2,1)S(1)}, u32[]{:S(2)}, u32[]{:S(2)}) collective-permute-start(bf16[2064,128]{1,0:T(8,128)(2,1)S(1)} %get-tuple-element.302.refs_0_), channel_id=1, source_target_pairs={{0,2},{1,3},{2,0},{3,1},{4,6},{5,7},{6,4},{7,5},{8,10},{9,11},{10,... | collective-permute-start | bytes 1585160 | tf_op jit(solution)/shard_map/ppermute | solution.py:475
  34.2 2.6 %collective-permute-start.23 = (bf16[768,128]{1,0:T(8,128)(2,1)S(1)}, bf16[768,128]{1,0:T(8,128)(2,1)S(1)}, u32[]{:S(2)}, u32[]{:S(2)}) collective-permute-start(bf16[768,128]{1,0:T(8,128)(2,1)S(1)} %get-tuple-element.305), channel_id=1, source_target_pairs={{0,4},{1,5},{2,6},{3,7},{4,0},{5,1},{6,2},{7,3},{8,12},{9,13},{10,... | collective-permute-start | bytes 589832 | tf_op jit(solution)/shard_map/ppermute | solution.py:475
  37.3 3.3 %collective-permute-done.15.refs_4_ = bf16[2064,128]{1,0:T(8,128)(2,1)S(1)} collective-permute-done((bf16[2064,128]{1,0:T(8,128)(2,1)S(1)}, bf16[2064,128]{1,0:T(8,128)(2,1)S(1)}, u32[]{:S(2)}, u32[]{:S(2)}) %collective-permute-start.15) | collective-permute-done | bytes 528416 | tf_op jit(solution)/shard_map/ppermute | solution.py:475
  42.6 8.2 %collective-permute-done.23.refs_6_ = bf16[768,128]{1,0:T(8,128)(2,1)S(1)} collective-permute-done((bf16[768,128]{1,0:T(8,128)(2,1)S(1)}, bf16[768,128]{1,0:T(8,128)(2,1)S(1)}, u32[]{:S(2)}, u32[]{:S(2)}) %collective-permute-start.23) | collective-permute-done | bytes 196640 | tf_op jit(solution)/shard_map/ppermute | solution.py:475
  50.8 3.5 %collective-permute-start.28 = (bf16[768,128]{1,0:T(8,128)(2,1)S(1)}, bf16[768,128]{1,0:T(8,128)(2,1)S(1)}, u32[]{:S(2)}, u32[]{:S(2)}) collective-permute-start(bf16[768,128]{1,0:T(8,128)(2,1)S(1)} %get-tuple-element.305), channel_id=1, source_target_pairs={{0,2},{1,3},{2,0},{3,1},{4,6},{5,7},{6,4},{7,5},{8,10},{9,11},{10,... | collective-permute-start | bytes 589832 | tf_op jit(solution)/shard_map/ppermute | solution.py:475
  54.3 12.1 %collective-permute-done.28.refs_2_ = bf16[768,128]{1,0:T(8,128)(2,1)S(1)} collective-permute-done((bf16[768,128]{1,0:T(8,128)(2,1)S(1)}, bf16[768,128]{1,0:T(8,128)(2,1)S(1)}, u32[]{:S(2)}, u32[]{:S(2)}) %collective-permute-start.28) | collective-permute-done | bytes 196640 | tf_op jit(solution)/shard_map/ppermute | solution.py:475
  67.5 1.9 %collective-permute-done.31.refs_7_ = bf16[768,128]{1,0:T(8,128)(2,1)S(1)} collective-permute-done((bf16[768,128]{1,0:T(8,128)(2,1)S(1)}, bf16[768,128]{1,0:T(8,128)(2,1)S(1)}, u32[]{:S(2)}, u32[]{:S(2)}) %collective-permute-start.31) | collective-permute-done | bytes 196640 | tf_op jit(solution)/shard_map/ppermute | solution.py:475
  69.4 1.6 %collective-permute-start.24 = (bf16[768,128]{1,0:T(8,128)(2,1)S(1)}, bf16[768,128]{1,0:T(8,128)(2,1)S(1)}, u32[]{:S(2)}, u32[]{:S(2)}) collective-permute-start(bf16[768,128]{1,0:T(8,128)(2,1)S(1)} %collective-permute-done.23.refs_6_), channel_id=1, source_target_pairs={{0,2},{1,3},{2,0},{3,1},{4,6},{5,7},{6,4},{7,5},{8,10},{9,11},{10,... | collective-permute-start | bytes 589832 | tf_op jit(solution)/shard_map/ppermute | solution.py:475
  71.0 3.4 %panel.1 = (bf16[4096,512]{1,0:T(8,128)(2,1)S(1)}, f32[1024,512]{1,0:T(8,128)S(1)}) custom-call(bf16[2064,128]{1,0:T(8,128)(2,1)S(1)} %get-tuple-element.302.refs_0_, bf16[1296,128]{1,0:T(8,128)(2,1)S(1)} %get-tuple-element.300.rest_ref.refs_1_, bf16[2064,128]{1,0:T(8,128)(2,1)S(1)} %collective-permute-done.13.refs_2_, ...), custom_call_target="tpu_custom_call" | custom-call | flops 1073741824 | bytes 8388608 | tf_op jit(solution)/shard_map/panel/pallas_call | solution.py:282
  76.4 2.6 %collective-permute-start.11 = (f32[16,128]{1,0:T(8,128)S(1)}, f32[16,128]{1,0:T(8,128)S(1)}, u32[]{:S(2)}, u32[]{:S(2)}) collective-permute-start(f32[16,128]{1,0:T(8,128)S(1)} %pad_maximum_fusion.refs_0_), channel_id=1, source_target_pairs={{0,4},{1,5},{2,6},{3,7},{4,0},{5,1},{6,2},{7,3},{8,12},{9,13},{10,... | collective-permute-start | bytes 24584 | tf_op jit(solution)/shard_map/ppermute | solution.py:475
  80.3 3.3 %dots.2.refs_3_ = f32[1024,512]{1,0:T(8,128)S(1)} custom-call(bf16[2064,128]{1,0:T(8,128)(2,1)S(1)} %collective-permute-done.26.refs_0_, bf16[2064,128]{1,0:T(8,128)(2,1)S(1)} %collective-permute-done.27.refs_1_, bf16[768,128]{1,0:T(8,128)(2,1)S(1)} %collective-permute-done.28.refs_2_, ...), custom_call_target="tpu_custom_call", output_to_operand_aliasing={{}: (9, {})} | custom-call | flops 2147483648 | bytes 6291456 | tf_op jit(solution)/shard_map/dots/pallas_call | solution.py:310
  86.2 2.0 %dots.3 = f32[1024,512]{1,0:T(8,128)S(1)} custom-call(bf16[2064,128]{1,0:T(8,128)(2,1)S(1)} %collective-permute-done.21.refs_0_, bf16[2064,128]{1,0:T(8,128)(2,1)S(1)} %collective-permute-done.22.refs_1_, bf16[4096,512]{1,0:T(8,128)(2,1)S(1)} %get-tuple-element.303.refs_5_.refs_8_.refs_2_, f32[1024,512]{1,0:T(8,128)S(1)} %dots.2.refs_3_), custom_call_target="tpu_custom_call", output_to_operand_aliasing={{}: (3, {})} | custom-call | flops 1073741824 | bytes 6291456 | tf_op jit(solution)/shard_map/dots/pallas_call | solution.py:310
  88.3 10.1 %conditional.1 = (bf16[1024,512]{1,0:T(8,128)(2,1)}) conditional(s32[]{:T(128)} %bitcast.3, (f32[8,4]{0,1:T(4,128)S(1)}, bf16[2064,128]{1,0:T(8,128)(2,1)S(1)}, bf16[2064,128]{1,0:T(8,128)(2,1)S(1)}, bf16[768,128]{1,0:T(8,128)(2,1)S(1)}, bf16[768,128]{1,0:T(8,128)(2,1)S(1)}, /*index=5*/bf16[4096,512]{1,0:T(8,128)(2,1)S(1)}, ...), branch_computations={%region_0.0_spmd, %region_1.10_spmd} | conditional | flops 1074790400 | bytes 55080728 | solution.py:524
  88.3 1.6 %finish.1 = (f32[1024,512]{1,0:T(8,128)S(1)}, f32[1,512]{1,0:T(1,128)S(1)}) custom-call(bf16[2064,128]{1,0:T(8,128)(2,1)S(1)} %get-tuple-element.265.refs_0_, bf16[2064,128]{1,0:T(8,128)(2,1)S(1)} %get-tuple-element.266.refs_1_, bf16[768,128]{1,0:T(8,128)(2,1)S(1)} %get-tuple-element.267.refs_2_, bf16[768,128]{1,0:T(8,128)(2,1)S(1)} %get-tuple-element.268.refs_3_, ...), custom_call_target="tpu_custom_call" | custom-call | flops 1073741824 | bytes 6291456 | tf_op jit(solution)/shard_map/cond/branch_0_fun/finish/pallas_call | solution.py:389
  92.1 1.6 %collective-permute-done.1.refs_2_ = f32[1,512]{1,0:T(1,128)S(1)} collective-permute-done((f32[1,512]{1,0:T(1,128)S(1)}, f32[1,512]{1,0:T(1,128)S(1)}, u32[]{:S(2)}, u32[]{:S(2)}) %collective-permute-start.1) | collective-permute-done | bytes 2080 | tf_op jit(solution)/shard_map/cond/branch_0_fun/ppermute | solution.py:475
  95.1 2.1 %collective-permute-done.2.refs_3_ = f32[1,512]{1,0:T(1,128)S(1)} collective-permute-done((f32[1,512]{1,0:T(1,128)S(1)}, f32[1,512]{1,0:T(1,128)S(1)}, u32[]{:S(2)}, u32[]{:S(2)}) %collective-permute-start.2) | collective-permute-done | bytes 2080 | tf_op jit(solution)/shard_map/cond/branch_0_fun/ppermute | solution.py:475
  (57 shorter events, 21.6 us)
Async XLA Ops:
  1.7 7.8 %collective-permute-start.5 = (bf16[1296,128]{1,0:T(8,128)(2,1)S(1)}, bf16[1296,128]{1,0:T(8,128)(2,1)S(1)}, u32[]{:S(2)}, u32[]{:S(2)}) collective-permute-start(bf16[1296,128]{1,0:T(8,128)(2,1)S(1)} %get-tuple-element.300.rest_ref.refs_1_), channel_id=1, source_target_pairs={{0,1},{1,0},{2,3},{3,2},{4,5},{5,4},{6,7},{7,6},{8,9},{9,8},{10,11... | collective-permute-start | bytes 995336 | tf_op jit(solution)/shard_map/ppermute | solution.py:475
  2.3 11.0 %collective-permute-start.16 = (bf16[1296,128]{1,0:T(8,128)(2,1)S(1)}, bf16[1296,128]{1,0:T(8,128)(2,1)S(1)}, u32[]{:S(2)}, u32[]{:S(2)}) collective-permute-start(bf16[1296,128]{1,0:T(8,128)(2,1)S(1)} %get-tuple-element.300.rest_ref.refs_1_), channel_id=1, source_target_pairs={{0,16},{1,17},{2,18},{3,19},{4,20},{5,21},{6,22},{7,23},{8,24},{9,... | collective-permute-start | bytes 995336 | tf_op jit(solution)/shard_map/ppermute | solution.py:475
  4.9 29.4 %collective-permute-start.13 = (bf16[2064,128]{1,0:T(8,128)(2,1)S(1)}, bf16[2064,128]{1,0:T(8,128)(2,1)S(1)}, u32[]{:S(2)}, u32[]{:S(2)}) collective-permute-start(bf16[2064,128]{1,0:T(8,128)(2,1)S(1)} %get-tuple-element.302.refs_0_), channel_id=1, source_target_pairs={{0,8},{1,9},{2,10},{3,11},{4,12},{5,13},{6,14},{7,15},{8,0},{9,1},... | collective-permute-start | bytes 1585160 | tf_op jit(solution)/shard_map/ppermute | solution.py:475
  6.3 24.4 %collective-permute-start.14 = (bf16[1296,128]{1,0:T(8,128)(2,1)S(1)}, bf16[1296,128]{1,0:T(8,128)(2,1)S(1)}, u32[]{:S(2)}, u32[]{:S(2)}) collective-permute-start(bf16[1296,128]{1,0:T(8,128)(2,1)S(1)} %get-tuple-element.300.rest_ref.refs_1_), channel_id=1, source_target_pairs={{0,8},{1,9},{2,10},{3,11},{4,12},{5,13},{6,14},{7,15},{8,0},{9,1},... | collective-permute-start | bytes 995336 | tf_op jit(solution)/shard_map/ppermute | solution.py:475
  6.9 29.9 %collective-permute-start.20 = (bf16[2064,128]{1,0:T(8,128)(2,1)S(1)}, bf16[2064,128]{1,0:T(8,128)(2,1)S(1)}, u32[]{:S(2)}, u32[]{:S(2)}) collective-permute-start(bf16[2064,128]{1,0:T(8,128)(2,1)S(1)} %get-tuple-element.302.refs_0_), channel_id=1, source_target_pairs={{0,4},{1,5},{2,6},{3,7},{4,0},{5,1},{6,2},{7,3},{8,12},{9,13},{10,... | collective-permute-start | bytes 1585160 | tf_op jit(solution)/shard_map/ppermute | solution.py:475
  11.0 15.1 %collective-permute-start.6 = (f32[8,128]{1,0:T(8,128)S(1)}, f32[8,128]{1,0:T(8,128)S(1)}, u32[]{:S(2)}, u32[]{:S(2)}) collective-permute-start(f32[8,128]{1,0:T(8,128)S(1)} %get-tuple-element.301), channel_id=1, source_target_pairs={{0,8},{1,9},{2,10},{3,11},{4,12},{5,13},{6,14},{7,15},{8,0},{9,1},... | collective-permute-start | bytes 12296 | tf_op jit(solution)/shard_map/ppermute | solution.py:475
  13.3 14.3 %collective-permute-start.7 = (f32[8,128]{1,0:T(8,128)S(1)}, f32[8,128]{1,0:T(8,128)S(1)}, u32[]{:S(2)}, u32[]{:S(2)}) collective-permute-start(f32[8,128]{1,0:T(8,128)S(1)} %get-tuple-element.301), channel_id=1, source_target_pairs={{0,16},{1,17},{2,18},{3,19},{4,20},{5,21},{6,22},{7,23},{8,24},{9,... | collective-permute-start | bytes 12296 | tf_op jit(solution)/shard_map/ppermute | solution.py:475
  26.1 4.6 %collective-permute-start.8 = (f32[8,128]{1,0:T(8,128)S(1)}, f32[8,128]{1,0:T(8,128)S(1)}, u32[]{:S(2)}, u32[]{:S(2)}) collective-permute-start(f32[8,128]{1,0:T(8,128)S(1)} %get-tuple-element.301), channel_id=1, source_target_pairs={{0,24},{1,25},{2,26},{3,27},{4,28},{5,29},{6,30},{7,31},{8,16},{9,... | collective-permute-start | bytes 12296 | tf_op jit(solution)/shard_map/ppermute | solution.py:475
  27.6 13.0 %collective-permute-start.15 = (bf16[2064,128]{1,0:T(8,128)(2,1)S(1)}, bf16[2064,128]{1,0:T(8,128)(2,1)S(1)}, u32[]{:S(2)}, u32[]{:S(2)}) collective-permute-start(bf16[2064,128]{1,0:T(8,128)(2,1)S(1)} %get-tuple-element.302.refs_0_), channel_id=1, source_target_pairs={{0,16},{1,17},{2,18},{3,19},{4,20},{5,21},{6,22},{7,23},{8,24},{9,... | collective-permute-start | bytes 1585160 | tf_op jit(solution)/shard_map/ppermute | solution.py:475
  30.7 10.4 %collective-permute-start.19 = (bf16[2064,128]{1,0:T(8,128)(2,1)S(1)}, bf16[2064,128]{1,0:T(8,128)(2,1)S(1)}, u32[]{:S(2)}, u32[]{:S(2)}) collective-permute-start(bf16[2064,128]{1,0:T(8,128)(2,1)S(1)} %get-tuple-element.302.refs_0_), channel_id=1, source_target_pairs={{0,1},{1,0},{2,3},{3,2},{4,5},{5,4},{6,7},{7,6},{8,9},{9,8},{10,11... | collective-permute-start | bytes 1585160 | tf_op jit(solution)/shard_map/ppermute | solution.py:475
  32.7 33.8 %collective-permute-start.26 = (bf16[2064,128]{1,0:T(8,128)(2,1)S(1)}, bf16[2064,128]{1,0:T(8,128)(2,1)S(1)}, u32[]{:S(2)}, u32[]{:S(2)}) collective-permute-start(bf16[2064,128]{1,0:T(8,128)(2,1)S(1)} %get-tuple-element.302.refs_0_), channel_id=1, source_target_pairs={{0,2},{1,3},{2,0},{3,1},{4,6},{5,7},{6,4},{7,5},{8,10},{9,11},{10,... | collective-permute-start | bytes 1585160 | tf_op jit(solution)/shard_map/ppermute | solution.py:475
  34.2 16.6 %collective-permute-start.23 = (bf16[768,128]{1,0:T(8,128)(2,1)S(1)}, bf16[768,128]{1,0:T(8,128)(2,1)S(1)}, u32[]{:S(2)}, u32[]{:S(2)}) collective-permute-start(bf16[768,128]{1,0:T(8,128)(2,1)S(1)} %get-tuple-element.305), channel_id=1, source_target_pairs={{0,4},{1,5},{2,6},{3,7},{4,0},{5,1},{6,2},{7,3},{8,12},{9,13},{10,... | collective-permute-start | bytes 589832 | tf_op jit(solution)/shard_map/ppermute | solution.py:475
  36.8 30.2 %collective-permute-start.21 = (bf16[2064,128]{1,0:T(8,128)(2,1)S(1)}, bf16[2064,128]{1,0:T(8,128)(2,1)S(1)}, u32[]{:S(2)}, u32[]{:S(2)}) collective-permute-start(bf16[2064,128]{1,0:T(8,128)(2,1)S(1)} %collective-permute-done.20.refs_4_), channel_id=1, source_target_pairs={{0,2},{1,3},{2,0},{3,1},{4,6},{5,7},{6,4},{7,5},{8,10},{9,11},{10,... | collective-permute-start | bytes 1585160 | tf_op jit(solution)/shard_map/ppermute | solution.py:475
  40.5 26.4 %collective-permute-start.18 = (bf16[1296,128]{1,0:T(8,128)(2,1)S(1)}, bf16[1296,128]{1,0:T(8,128)(2,1)S(1)}, u32[]{:S(2)}, u32[]{:S(2)}) collective-permute-start(bf16[1296,128]{1,0:T(8,128)(2,1)S(1)} %collective-permute-done.16.refs_5_), channel_id=1, source_target_pairs={{0,8},{1,9},{2,10},{3,11},{4,12},{5,13},{6,14},{7,15},{8,0},{9,1},... | collective-permute-start | bytes 995336 | tf_op jit(solution)/shard_map/ppermute | solution.py:475
  41.1 29.9 %collective-permute-start.17 = (bf16[2064,128]{1,0:T(8,128)(2,1)S(1)}, bf16[2064,128]{1,0:T(8,128)(2,1)S(1)}, u32[]{:S(2)}, u32[]{:S(2)}) collective-permute-start(bf16[2064,128]{1,0:T(8,128)(2,1)S(1)} %collective-permute-done.13.refs_2_), channel_id=1, source_target_pairs={{0,16},{1,17},{2,18},{3,19},{4,20},{5,21},{6,22},{7,23},{8,24},{9,... | collective-permute-start | bytes 1585160 | tf_op jit(solution)/shard_map/ppermute | solution.py:475
  50.8 15.6 %collective-permute-start.28 = (bf16[768,128]{1,0:T(8,128)(2,1)S(1)}, bf16[768,128]{1,0:T(8,128)(2,1)S(1)}, u32[]{:S(2)}, u32[]{:S(2)}) collective-permute-start(bf16[768,128]{1,0:T(8,128)(2,1)S(1)} %get-tuple-element.305), channel_id=1, source_target_pairs={{0,2},{1,3},{2,0},{3,1},{4,6},{5,7},{6,4},{7,5},{8,10},{9,11},{10,... | collective-permute-start | bytes 589832 | tf_op jit(solution)/shard_map/ppermute | solution.py:475
  66.5 12.5 %collective-permute-start.30 = (bf16[2064,128]{1,0:T(8,128)(2,1)S(1)}, bf16[2064,128]{1,0:T(8,128)(2,1)S(1)}, u32[]{:S(2)}, u32[]{:S(2)}) collective-permute-start(bf16[2064,128]{1,0:T(8,128)(2,1)S(1)} %collective-permute-done.20.refs_4_), channel_id=1, source_target_pairs={{0,1},{1,0},{2,3},{3,2},{4,5},{5,4},{6,7},{7,6},{8,9},{9,8},{10,11... | collective-permute-start | bytes 1585160 | tf_op jit(solution)/shard_map/ppermute | solution.py:475
  66.5 13.8 %collective-permute-start.27 = (bf16[2064,128]{1,0:T(8,128)(2,1)S(1)}, bf16[2064,128]{1,0:T(8,128)(2,1)S(1)}, u32[]{:S(2)}, u32[]{:S(2)}) collective-permute-start(bf16[2064,128]{1,0:T(8,128)(2,1)S(1)} %collective-permute-done.26.refs_0_), channel_id=1, source_target_pairs={{0,1},{1,0},{2,3},{3,2},{4,5},{5,4},{6,7},{7,6},{8,9},{9,8},{10,11... | collective-permute-start | bytes 1585160 | tf_op jit(solution)/shard_map/ppermute | solution.py:475
  67.1 19.1 %collective-permute-start.22 = (bf16[2064,128]{1,0:T(8,128)(2,1)S(1)}, bf16[2064,128]{1,0:T(8,128)(2,1)S(1)}, u32[]{:S(2)}, u32[]{:S(2)}) collective-permute-start(bf16[2064,128]{1,0:T(8,128)(2,1)S(1)} %collective-permute-done.21.refs_0_), channel_id=1, source_target_pairs={{0,1},{1,0},{2,3},{3,2},{4,5},{5,4},{6,7},{7,6},{8,9},{9,8},{10,11... | collective-permute-start | bytes 1585160 | tf_op jit(solution)/shard_map/ppermute | solution.py:475
  69.4 6.9 %collective-permute-start.24 = (bf16[768,128]{1,0:T(8,128)(2,1)S(1)}, bf16[768,128]{1,0:T(8,128)(2,1)S(1)}, u32[]{:S(2)}, u32[]{:S(2)}) collective-permute-start(bf16[768,128]{1,0:T(8,128)(2,1)S(1)} %collective-permute-done.23.refs_6_), channel_id=1, source_target_pairs={{0,2},{1,3},{2,0},{3,1},{4,6},{5,7},{6,4},{7,5},{8,10},{9,11},{10,... | collective-permute-start | bytes 589832 | tf_op jit(solution)/shard_map/ppermute | solution.py:475
  74.4 9.2 %collective-permute-start.10 = (f32[16,128]{1,0:T(8,128)S(1)}, f32[16,128]{1,0:T(8,128)S(1)}, u32[]{:S(2)}, u32[]{:S(2)}) collective-permute-start(f32[16,128]{1,0:T(8,128)S(1)} %pad_maximum_fusion.refs_0_), channel_id=1, source_target_pairs={{0,2},{1,3},{2,0},{3,1},{4,6},{5,7},{6,4},{7,5},{8,10},{9,11},{10,... | collective-permute-start | bytes 24584 | tf_op jit(solution)/shard_map/ppermute | solution.py:475
  76.4 7.3 %collective-permute-start.11 = (f32[16,128]{1,0:T(8,128)S(1)}, f32[16,128]{1,0:T(8,128)S(1)}, u32[]{:S(2)}, u32[]{:S(2)}) collective-permute-start(f32[16,128]{1,0:T(8,128)S(1)} %pad_maximum_fusion.refs_0_), channel_id=1, source_target_pairs={{0,4},{1,5},{2,6},{3,7},{4,0},{5,1},{6,2},{7,3},{8,12},{9,13},{10,... | collective-permute-start | bytes 24584 | tf_op jit(solution)/shard_map/ppermute | solution.py:475
  78.9 5.4 %collective-permute-start.12 = (f32[16,128]{1,0:T(8,128)S(1)}, f32[16,128]{1,0:T(8,128)S(1)}, u32[]{:S(2)}, u32[]{:S(2)}) collective-permute-start(f32[16,128]{1,0:T(8,128)S(1)} %pad_maximum_fusion.refs_0_), channel_id=1, source_target_pairs={{0,6},{1,7},{2,4},{3,5},{4,2},{5,3},{6,0},{7,1},{8,14},{9,15},{10,... | collective-permute-start | bytes 24584 | tf_op jit(solution)/shard_map/ppermute | solution.py:475
  80.3 7.9 %collective-permute-start.25 = (bf16[768,128]{1,0:T(8,128)(2,1)S(1)}, bf16[768,128]{1,0:T(8,128)(2,1)S(1)}, u32[]{:S(2)}, u32[]{:S(2)}) collective-permute-start(bf16[768,128]{1,0:T(8,128)(2,1)S(1)} %collective-permute-done.24), channel_id=1, source_target_pairs={{0,1},{1,0},{2,3},{3,2},{4,5},{5,4},{6,7},{7,6},{8,9},{9,8},{10,11... | collective-permute-start | bytes 589832 | tf_op jit(solution)/shard_map/ppermute | solution.py:475
  (10 other events, 95.3 us)
